TPU v7x, 16 devices: a whole 2x2x2 slice. The times are simulated.
16 devices in a mesh: frag: 2 (over z), dev: 8 (over y, x, core).
Axes of the slice: x: 2, y: 2, z: 2, core: 2. Of those that a mesh axis runs over, the one named last changes fastest.
Arguments:
- ao_ints: bfloat16 [192, 96, 96, 96], P(('frag', 'dev')), parts along dimension 0
- coeffs: bfloat16 [192, 96], P('frag'), parts along dimension 0
Outputs:
- output: float32 [192, 96, 9216], P('frag', None, 'dev'), parts along dimension 0
There are 2 independent parts. A program takes and returns all parts, laid end to end along the dimension named above; each array names one.
All inputs are finite; a program needn't handle non-finite values.
Results may differ from a plain program's by a relative error of at most 0.001.
Values are sent between devices in bfloat16 or wider.
A program may use at most 1 GiB of HBM per device.

v0:
```python
import functools

import jax
import jax.numpy as jnp
from jax import lax
from jax.experimental import pallas as pl
from jax.experimental.pallas import tpu as pltpu
from jax.sharding import PartitionSpec as P


TILES = ((0, 48, 0, 1152), (48, 24, 0, 1152), (72, 8, 0, 1152), (80, 8, 0, 1152), (88, 8, 0, 768), (88, 8, 768, 384))
DIAGONAL = (6, 7)
DIRECT = (2, 4, 3, 5, 1)
F32, BF16 = jnp.float32, jnp.bfloat16


def one_hot(shape, fn):
    rows = lax.broadcasted_iota(jnp.int32, shape, 0)
    cols = lax.broadcasted_iota(jnp.int32, shape, 1)
    return fn(rows, cols)


def dot(a, b):
    return jnp.dot(a, b, preferred_element_type=F32)


def pick(shape, fn):
    return one_hot(shape, fn).astype(BF16)


def transposed(c, n):
    eye = pick((n, n), lambda i, j: i == j)
    return lax.dot_general(c, eye, (((0,), (0,)), ((), ())), preferred_element_type=F32).astype(BF16)


def build_first(n, c_ref, l1_ref, r2_ref, ct_ref):
    c = c_ref[...]
    ct = transposed(c, n)
    ct_ref[...] = ct
    tall = dot(pick((8 * n, n), lambda i, j: i // 8 == j), ct).astype(BF16)
    wide = dot(tall, pick((n, 8 * n), lambda i, j: j % n == i))
    keep = one_hot((8 * n, 8 * n), lambda i, j: i % 8 == j // n)
    l1_ref[...] = jnp.where(keep, wide, 0.0).astype(BF16)
    tall = dot(pick((512, n), lambda i, j: i % 128 == j), c).astype(BF16)
    wide = dot(tall, pick((n, 4 * n), lambda i, j: j % n == i))
    keep = one_hot((512, 4 * n), lambda i, j: i // 128 == j // n)
    r2_ref[...] = jnp.where(keep, wide, 0.0).astype(BF16)


def last_kernel(n, rows, me_ref, c_ref, after_ref, l4_ref):
    me = me_ref[0]

    def source(r, col):
        m = col // 8
        return r == (me ^ (m // rows)) * rows + m % rows

    ct = transposed(c_ref[...], n)
    tall = dot(pick((8 * n, n), lambda i, j: i // 8 == j), ct).astype(BF16)
    wide = dot(tall, pick((n, 8 * n), source))
    keep = one_hot((8 * n, 8 * n), lambda i, j: i % 8 == j % 8)
    l4_ref[...] = jnp.where(keep, wide, 0.0).astype(BF16)


def flipped(me, k):
    out = 0
    for bit in (1, 2, 4):
        b = (me // bit) % 2
        out = out + bit * (1 - b if k & bit else b)
    return out


def exchange_kernel(n, n_dev, rows, a_hbm, c_ref, *refs):
    n_got, n_tile = n_dev - len(DIAGONAL), len(TILES)
    got, tiles = refs[:n_got], refs[n_got:n_got + len(DIAGONAL) * n_tile]
    (a_buf, t1_ref, g_ref, l1_ref, r2_ref, ct_ref, a_sem, chunk_sem, own_sem, tile_sem, send_sem,
     recv_sem) = refs[n_got + len(tiles):]
    nj = n // n_dev
    me = lax.axis_index('dev')
    barrier = pltpu.get_barrier_semaphore()
    for k in DIRECT:
        pl.semaphore_signal(barrier, inc=1, device_id={'dev': flipped(me, k)}, device_id_type=pl.DeviceIdType.MESH)

    def chunk(g):
        q = pl.ds(g * 16, 16)
        return pltpu.make_async_copy(a_hbm.at[0, q], a_buf.at[0, q], chunk_sem.at[g])

    def fetch(i):
        slot = lax.rem(i, 2)
        return pltpu.make_async_copy(a_hbm.at[i], a_buf.at[slot], a_sem.at[slot])

    for g in range(n // 16):
        chunk(g).start()
    fetch(1).start()
    build_first(n, c_ref, l1_ref, r2_ref, ct_ref)
    zero = jnp.zeros((8 * n, 128 - n), BF16)

    def remote(k, src, dst):
        return pltpu.make_async_remote_copy(
            src_ref=src, dst_ref=dst, send_sem=send_sem.at[k], recv_sem=recv_sem.at[k],
            device_id={'dev': flipped(me, k)}, device_id_type=pl.DeviceIdType.MESH)

    def tile_copies(k, rows_):
        x = DIAGONAL.index(k)
        for t, (a0, size, lane, lanes) in enumerate(TILES):
            j = x * n_tile + t
            src = g_ref.at[k, rows_, pl.ds(a0, size), pl.ds(lane, lanes)]
            yield pltpu.make_async_copy(src, tiles[j].at[rows_], tile_sem.at[j])

    def send(k, i):
        if k == 0:
            pltpu.make_async_copy(g_ref.at[0, i], got[0].at[i], own_sem).start()
        elif k in DIAGONAL:
            for copy in tile_copies(k, i):
                copy.start()
        else:
            remote(k, g_ref.at[k, i], got[k].at[i]).start()

    def step_one(slot, g, lhs):
        q0 = pl.multiple_of(g * 16, 16)
        lo = a_buf[slot, pl.ds(q0, 8)].reshape(8 * n, n)
        hi = a_buf[slot, pl.ds(q0 + 8, 8)].reshape(8 * n, n)
        t = dot(lhs, jnp.concatenate([lo, zero, hi, zero], axis=1))
        nj = t.shape[0] // 8
        t = jnp.concatenate([t[:, :128].reshape(nj, 8, 128), t[:, 128:].reshape(nj, 8, 128)], axis=1)
        return pl.ds(q0, 16), t.astype(BF16)

    def step_two_three(k, i):
        d = flipped(me, k)
        t = t1_ref[pl.ds(d * nj, nj)].reshape(nj // 4, 4, n, 128)
        lhs = jnp.concatenate([t[:, jj].reshape(nj // 4 * n, 128) for jj in range(4)], axis=1)
        h = dot(lhs, r2_ref[...]).astype(BF16)
        h = jnp.concatenate([h[g * n:(g + 1) * n] for g in range(nj // 4)], axis=1)
        g_ref[k, i] = dot(ct_ref[...], h).astype(BF16)

    def some(ks, i, slot, wait):
        def first(g, carry):
            if wait:
                chunk(g).wait()
            lhs = jnp.concatenate(
                [l1_ref[pl.ds(pl.multiple_of(flipped(me, k) * 8 * nj, 8 * nj), 8 * nj)] for k in ks], axis=0)
            q, t = step_one(slot, g, lhs)
            for x, k in enumerate(ks):
                t1_ref[pl.ds(flipped(me, k) * nj, nj), q, :] = t[x * nj:(x + 1) * nj]
            return carry

        lax.fori_loop(0, n // 16, first, 0)
        for k in ks:
            step_two_three(k, i)

    some(DIRECT[:2], 0, 0, True)
    pl.semaphore_wait(barrier, len(DIRECT))
    for k in DIRECT[:2]:
        send(k, 0)
    some((*DIRECT[2:], 0, *DIAGONAL), 0, 0, False)
    for k in (*DIRECT[2:], 0, *DIAGONAL):
        send(k, 0)

    def row(i, carry):
        slot = lax.rem(i, 2)
        fetch(i).wait()

        @pl.when(i + 1 < rows)
        def _():
            fetch(i + 1).start()

        def first(g, carry):
            q, t = step_one(slot, g, l1_ref[...])
            t1_ref[:, q, :] = t
            return carry

        lax.fori_loop(0, n // 16, first, 0)
        before = None
        for k in (*DIRECT, 0, *DIAGONAL):
            step_two_three(k, i)
            if before is not None:
                send(before, i)
            before = k
        send(before, i)
        return carry

    lax.fori_loop(1, rows, row, 0)
    pltpu.make_async_copy(g_ref.at[0], got[0], own_sem).wait()
    for k in DIAGONAL:
        for copy in tile_copies(k, pl.ds(0, rows)):
            copy.wait()
    for k in DIRECT:
        remote(k, g_ref.at[k], got[k]).wait()


def out_kernel(n, n_in, wide, *refs):
    l4_ref, out_ref = refs[n_in], refs[-1]
    rhs = jnp.concatenate([r[...].reshape(-1, wide) for r in refs[:n_in]], axis=0)
    out_ref[...] = dot(l4_ref[...], rhs).reshape(n, 8, wide)


def solution(mesh):
    n_dev = mesh.shape['dev']

    def transform(ao_rows, coeffs):
        rows = ao_rows.shape[0]
        n = coeffs.shape[0]
        wide = n * n // n_dev
        me_arr = jnp.full((1,), lax.axis_index('dev'), jnp.int32)
        smem = pl.BlockSpec(memory_space=pltpu.SMEM)
        vmem = pl.BlockSpec(memory_space=pltpu.VMEM)
        hbm = pl.BlockSpec(memory_space=pl.ANY)

        def const(shape):
            return pl.BlockSpec(shape, lambda *_: (0,) * len(shape))

        square, second = (8 * n, 8 * n), (512, 4 * n)
        n_got = n_dev - len(DIAGONAL)
        shapes = [(rows, n, wide)] * n_got
        shapes += [(rows, size, lanes) for _ in DIAGONAL for _, size, _, lanes in TILES]
        outs = pl.pallas_call(
            functools.partial(exchange_kernel, n, n_dev, rows),
            in_specs=[hbm, vmem],
            out_specs=[hbm] * len(shapes),
            out_shape=[jax.ShapeDtypeStruct(s, BF16) for s in shapes],
            scratch_shapes=[
                pltpu.VMEM((2, n, n, n), BF16), pltpu.VMEM((n, n, 128), BF16),
                pltpu.VMEM((n_dev, rows, n, wide), BF16), pltpu.VMEM(square, BF16),
                pltpu.VMEM(second, BF16), pltpu.VMEM((n, n), BF16),
                pltpu.SemaphoreType.DMA((2,)), pltpu.SemaphoreType.DMA((n // 16,)), pltpu.SemaphoreType.DMA,
                pltpu.SemaphoreType.DMA((len(shapes) - n_got,)),
                pltpu.SemaphoreType.DMA((n_dev,)), pltpu.SemaphoreType.DMA((n_dev,))],
            compiler_params=pltpu.CompilerParams(collective_id=0, has_side_effects=True),
            name='exchange',
        )(ao_rows, coeffs)
        got, tiles = outs[:n_got], outs[n_got:]
        moved = {}
        for t in range(len(TILES)):
            for x, k in enumerate(DIAGONAL):
                moved[k, t] = lax.ppermute(
                    tiles[x * len(TILES) + t], 'dev', [(i, i ^ k) for i in range(n_dev)])
        l4 = pl.pallas_call(
            functools.partial(last_kernel, n, rows),
            in_specs=[smem, vmem, hbm],
            out_specs=vmem,
            out_shape=jax.ShapeDtypeStruct(square, BF16),
            name='last',
        )(me_arr, coeffs, got[0])

        out = None
        for t_i, (a0, size, lane, lanes) in enumerate(TILES):
            ins, specs = [], []
            for k in range(n_dev):
                block, at = (moved[k, t_i], (0, 0)) if (k, t_i) in moved else (got[k], (a0 // 8, lane // lanes))
                ins.append(block)
                specs.append(pl.BlockSpec((rows, 8, lanes), lambda i, at=at: (0, at[0] + i, at[1])))
            n_in = len(ins)
            ins.append(l4)
            specs.append(const(square))
            if out is not None:
                ins.append(out)
                specs.append(hbm)
            out = pl.pallas_call(
                functools.partial(out_kernel, n, n_in, lanes),
                grid=(size // 8,),
                in_specs=specs,
                out_specs=pl.BlockSpec((n, 8, lanes), lambda i, at=(a0 // 8, lane // lanes): (0, at[0] + i, at[1])),
                out_shape=jax.ShapeDtypeStruct((n, n, wide), F32),
                input_output_aliases={} if t_i == 0 else {len(ins) - 1: 0},
                compiler_params=pltpu.CompilerParams(vmem_limit_bytes=67043328),
                name='out',
            )(*ins)
        return out

    return jax.shard_map(transform, mesh=mesh, in_specs=(P(('frag', 'dev')), P('frag')), out_specs=P('frag', None, 'dev'), check_vma=False)
```

profile of v0, /device:TPU:0, one launch (start us, length us, event | category | flops | bytes accessed | tf_op | source)
XLA Modules:
  0.0 284.4 jit_solution(11508629871916328748)
XLA Ops:
  0.0 121.5 %exchange.1 = (bf16[12,96,1152]{2,1,0:T(8,128)(2,1)}, bf16[12,96,1152]{2,1,0:T(8,128)(2,1)}, bf16[12,96,1152]{2,1,0:T(8,128)(2,1)}, bf16[12,96,1152]{2,1,0:T(8,1...) custom-call(bf16[12,96,96,96]{3,2,1,0:T(8,128)(2,1)} %a_hbm.1, ...), custom_call_target="tpu_custom_call" | custom-call | tf_op jit(solution)/shard_map/exchange/pallas_call | solution.py:215
  121.5 1.5 collective-permute-start.10
  123.0 1.3 collective-permute-start.11
  124.3 1.5 collective-permute-start.4
  125.7 1.5 collective-permute-start.8
  127.2 0.8 collective-permute-start.9
  128.0 59.9 %collective-permute-done.4.refs_6_ = bf16[12,8,1152]{2,1,0:T(8,128)(2,1)} collective-permute-done((bf16[12,8,1152]{2,1,0:T(8,128)(2,1)}, bf16[12,8,1152]{2,1,0:T(8,128)(2,1)}, u32[]{:S(2)}, u32[]{:S(2)}) %collective-permute-start.4) | collective-permute-done | bytes 221216 | tf_op jit(solution)/shard_map/ppermute | solution.py:234
  187.9 1.5 collective-permute-start.6
  189.4 31.2 %collective-permute-done.6.refs_6_ = bf16[12,8,1152]{2,1,0:T(8,128)(2,1)} collective-permute-done((bf16[12,8,1152]{2,1,0:T(8,128)(2,1)}, bf16[12,8,1152]{2,1,0:T(8,128)(2,1)}, u32[]{:S(2)}, u32[]{:S(2)}) %collective-permute-start.6) | collective-permute-done | bytes 221216 | tf_op jit(solution)/shard_map/ppermute | solution.py:234
  220.6 0.7 collective-permute-start.7
  221.3 8.1 %collective-permute-done.7.refs_7_ = bf16[12,8,1152]{2,1,0:T(8,128)(2,1)} collective-permute-done((bf16[12,8,1152]{2,1,0:T(8,128)(2,1)}, bf16[12,8,1152]{2,1,0:T(8,128)(2,1)}, u32[]{:S(2)}, u32[]{:S(2)}) %collective-permute-start.7) | collective-permute-done | bytes 221216 | tf_op jit(solution)/shard_map/ppermute | solution.py:234
  229.4 1.0 collective-permute-start.5
  230.4 1.5 collective-permute-start.2
  231.8 0.0 collective-permute-done.9.refs_7_
  231.8 1.4 collective-permute-start.3
  233.2 1.5 collective-permute-start
  234.7 1.0 collective-permute-start.1
  235.7 2.5 last.1.refs_8_
  238.2 17.1 %out.6.refs_9_ = f32[96,96,1152]{2,1,0:T(8,128)} custom-call(bf16[12,96,1152]{2,1,0:T(8,128)(2,1)} %get-tuple-element.23.after_ref.refs_0_, bf16[12,96,1152]{2,1,0:T(8,128)(2,1)} %get-tuple-element.24.refs_1_, bf16[12,96,1152]{2,1,0:T(8,128)(2,1)} %get-tuple-element.25.refs_2_, bf16[12,96,1152]{2,1,0:T(8,128)(2,1)} %get-tuple-element.26.refs_3_, ...), custom_call_target="tpu_custom_call" | custom-call | tf_op jit(solution)/shard_map/out/pallas_call | solution.py:257
  255.4 10.5 %out.7.refs_9_ = f32[96,96,1152]{2,1,0:T(8,128)} custom-call(bf16[12,96,1152]{2,1,0:T(8,128)(2,1)} %get-tuple-element.23.after_ref.refs_0_, bf16[12,96,1152]{2,1,0:T(8,128)(2,1)} %get-tuple-element.24.refs_1_, bf16[12,96,1152]{2,1,0:T(8,128)(2,1)} %get-tuple-element.25.refs_2_, ...), custom_call_target="tpu_custom_call", output_to_operand_aliasing={{}: (9, {})} | custom-call | tf_op jit(solution)/shard_map/out/pallas_call | solution.py:257
  265.9 5.4 %out.8.refs_9_ = f32[96,96,1152]{2,1,0:T(8,128)} custom-call(bf16[12,96,1152]{2,1,0:T(8,128)(2,1)} %get-tuple-element.23.after_ref.refs_0_, bf16[12,96,1152]{2,1,0:T(8,128)(2,1)} %get-tuple-element.24.refs_1_, bf16[12,96,1152]{2,1,0:T(8,128)(2,1)} %get-tuple-element.25.refs_2_, ...), custom_call_target="tpu_custom_call", output_to_operand_aliasing={{}: (9, {})} | custom-call | tf_op jit(solution)/shard_map/out/pallas_call | solution.py:257
  271.3 5.4 %out.9.refs_9_ = f32[96,96,1152]{2,1,0:T(8,128)} custom-call(bf16[12,96,1152]{2,1,0:T(8,128)(2,1)} %get-tuple-element.23.after_ref.refs_0_, bf16[12,96,1152]{2,1,0:T(8,128)(2,1)} %get-tuple-element.24.refs_1_, bf16[12,96,1152]{2,1,0:T(8,128)(2,1)} %get-tuple-element.25.refs_2_, ...), custom_call_target="tpu_custom_call", output_to_operand_aliasing={{}: (9, {})} | custom-call | tf_op jit(solution)/shard_map/out/pallas_call | solution.py:257
  276.8 4.3 %out.10.refs_9_ = f32[96,96,1152]{2,1,0:T(8,128)} custom-call(bf16[12,96,1152]{2,1,0:T(8,128)(2,1)} %get-tuple-element.23.after_ref.refs_0_, bf16[12,96,1152]{2,1,0:T(8,128)(2,1)} %get-tuple-element.24.refs_1_, bf16[12,96,1152]{2,1,0:T(8,128)(2,1)} %get-tuple-element.25.refs_2_, ...), custom_call_target="tpu_custom_call", output_to_operand_aliasing={{}: (9, {})} | custom-call | tf_op jit(solution)/shard_map/out/pallas_call | solution.py:257
  281.0 3.4 %out.11 = f32[96,96,1152]{2,1,0:T(8,128)} custom-call(bf16[12,96,1152]{2,1,0:T(8,128)(2,1)} %get-tuple-element.23.after_ref.refs_0_, bf16[12,96,1152]{2,1,0:T(8,128)(2,1)} %get-tuple-element.24.refs_1_, bf16[12,96,1152]{2,1,0:T(8,128)(2,1)} %get-tuple-element.25.refs_2_, ...), custom_call_target="tpu_custom_call", output_to_operand_aliasing={{}: (9, {})} | custom-call | tf_op jit(solution)/shard_map/out/pallas_call | solution.py:257
  (8 shorter events, 0.0 us)
Async XLA Ops:
  121.5 111.7 %collective-permute-start.10 = (bf16[12,48,1152]{2,1,0:T(8,128)(2,1)}, bf16[12,48,1152]{2,1,0:T(8,128)(2,1)}, u32[]{:S(2)}, u32[]{:S(2)}) collective-permute-start(bf16[12,48,1152]{2,1,0:T(8,128)(2,1)} %get-tuple-element.39), channel_id=1, source_target_pairs={{0,6},{1,7},{2,4},{3,5},{4,2},{5,3},{6,0},{7,1},{8,14},{9,15},{10,... | collective-permute-start | bytes 3981320 | tf_op jit(solution)/shard_map/ppermute | solution.py:234
  123.0 111.7 %collective-permute-start.11 = (bf16[12,48,1152]{2,1,0:T(8,128)(2,1)}, bf16[12,48,1152]{2,1,0:T(8,128)(2,1)}, u32[]{:S(2)}, u32[]{:S(2)}) collective-permute-start(bf16[12,48,1152]{2,1,0:T(8,128)(2,1)} %get-tuple-element.40), channel_id=1, source_target_pairs={{0,7},{1,6},{2,5},{3,4},{4,3},{5,2},{6,1},{7,0},{8,15},{9,14},{10,... | collective-permute-start | bytes 3981320 | tf_op jit(solution)/shard_map/ppermute | solution.py:234
  124.3 63.7 %collective-permute-start.4 = (bf16[12,8,1152]{2,1,0:T(8,128)(2,1)}, bf16[12,8,1152]{2,1,0:T(8,128)(2,1)}, u32[]{:S(2)}, u32[]{:S(2)}) collective-permute-start(bf16[12,8,1152]{2,1,0:T(8,128)(2,1)} %get-tuple-element.33), channel_id=1, source_target_pairs={{0,6},{1,7},{2,4},{3,5},{4,2},{5,3},{6,0},{7,1},{8,14},{9,15},{10,... | collective-permute-start | bytes 663560 | tf_op jit(solution)/shard_map/ppermute | solution.py:234
  125.7 104.6 %collective-permute-start.8 = (bf16[12,24,1152]{2,1,0:T(8,128)(2,1)}, bf16[12,24,1152]{2,1,0:T(8,128)(2,1)}, u32[]{:S(2)}, u32[]{:S(2)}) collective-permute-start(bf16[12,24,1152]{2,1,0:T(8,128)(2,1)} %get-tuple-element.37), channel_id=1, source_target_pairs={{0,6},{1,7},{2,4},{3,5},{4,2},{5,3},{6,0},{7,1},{8,14},{9,15},{10,... | collective-permute-start | bytes 1990664 | tf_op jit(solution)/shard_map/ppermute | solution.py:234
  127.2 104.6 %collective-permute-start.9 = (bf16[12,24,1152]{2,1,0:T(8,128)(2,1)}, bf16[12,24,1152]{2,1,0:T(8,128)(2,1)}, u32[]{:S(2)}, u32[]{:S(2)}) collective-permute-start(bf16[12,24,1152]{2,1,0:T(8,128)(2,1)} %get-tuple-element.38), channel_id=1, source_target_pairs={{0,7},{1,6},{2,5},{3,4},{4,3},{5,2},{6,1},{7,0},{8,15},{9,14},{10,... | collective-permute-start | bytes 1990664 | tf_op jit(solution)/shard_map/ppermute | solution.py:234
  187.9 32.7 %collective-permute-start.6 = (bf16[12,8,1152]{2,1,0:T(8,128)(2,1)}, bf16[12,8,1152]{2,1,0:T(8,128)(2,1)}, u32[]{:S(2)}, u32[]{:S(2)}) collective-permute-start(bf16[12,8,1152]{2,1,0:T(8,128)(2,1)} %get-tuple-element.35), channel_id=1, source_target_pairs={{0,6},{1,7},{2,4},{3,5},{4,2},{5,3},{6,0},{7,1},{8,14},{9,15},{10,... | collective-permute-start | bytes 663560 | tf_op jit(solution)/shard_map/ppermute | solution.py:234
  220.6 8.7 %collective-permute-start.7 = (bf16[12,8,1152]{2,1,0:T(8,128)(2,1)}, bf16[12,8,1152]{2,1,0:T(8,128)(2,1)}, u32[]{:S(2)}, u32[]{:S(2)}) collective-permute-start(bf16[12,8,1152]{2,1,0:T(8,128)(2,1)} %get-tuple-element.36), channel_id=1, source_target_pairs={{0,7},{1,6},{2,5},{3,4},{4,3},{5,2},{6,1},{7,0},{8,15},{9,14},{10,... | collective-permute-start | bytes 663560 | tf_op jit(solution)/shard_map/ppermute | solution.py:234
  229.4 41.9 %collective-permute-start.5 = (bf16[12,8,1152]{2,1,0:T(8,128)(2,1)}, bf16[12,8,1152]{2,1,0:T(8,128)(2,1)}, u32[]{:S(2)}, u32[]{:S(2)}) collective-permute-start(bf16[12,8,1152]{2,1,0:T(8,128)(2,1)} %get-tuple-element.34), channel_id=1, source_target_pairs={{0,7},{1,6},{2,5},{3,4},{4,3},{5,2},{6,1},{7,0},{8,15},{9,14},{10,... | collective-permute-start | bytes 663560 | tf_op jit(solution)/shard_map/ppermute | solution.py:234
  230.4 46.4 %collective-permute-start.2 = (bf16[12,8,768]{2,1,0:T(8,128)(2,1)}, bf16[12,8,768]{2,1,0:T(8,128)(2,1)}, u32[]{:S(2)}, u32[]{:S(2)}) collective-permute-start(bf16[12,8,768]{2,1,0:T(8,128)(2,1)} %get-tuple-element.31), channel_id=1, source_target_pairs={{0,6},{1,7},{2,4},{3,5},{4,2},{5,3},{6,0},{7,1},{8,14},{9,15},{10,... | collective-permute-start | bytes 442376 | tf_op jit(solution)/shard_map/ppermute | solution.py:234
  231.8 44.9 %collective-permute-start.3 = (bf16[12,8,768]{2,1,0:T(8,128)(2,1)}, bf16[12,8,768]{2,1,0:T(8,128)(2,1)}, u32[]{:S(2)}, u32[]{:S(2)}) collective-permute-start(bf16[12,8,768]{2,1,0:T(8,128)(2,1)} %get-tuple-element.32), channel_id=1, source_target_pairs={{0,7},{1,6},{2,5},{3,4},{4,3},{5,2},{6,1},{7,0},{8,15},{9,14},{10,... | collective-permute-start | bytes 442376 | tf_op jit(solution)/shard_map/ppermute | solution.py:234
  233.2 47.8 %collective-permute-start = (bf16[12,8,384]{2,1,0:T(8,128)(2,1)}, bf16[12,8,384]{2,1,0:T(8,128)(2,1)}, u32[]{:S(2)}, u32[]{:S(2)}) collective-permute-start(bf16[12,8,384]{2,1,0:T(8,128)(2,1)} %get-tuple-element.29), channel_id=1, source_target_pairs={{0,6},{1,7},{2,4},{3,5},{4,2},{5,3},{6,0},{7,1},{8,14},{9,15},{10,... | collective-permute-start | bytes 221192 | tf_op jit(solution)/shard_map/ppermute | solution.py:234
  234.7 46.3 %collective-permute-start.1 = (bf16[12,8,384]{2,1,0:T(8,128)(2,1)}, bf16[12,8,384]{2,1,0:T(8,128)(2,1)}, u32[]{:S(2)}, u32[]{:S(2)}) collective-permute-start(bf16[12,8,384]{2,1,0:T(8,128)(2,1)} %get-tuple-element.30), channel_id=1, source_target_pairs={{0,7},{1,6},{2,5},{3,4},{4,3},{5,2},{6,1},{7,0},{8,15},{9,14},{10,... | collective-permute-start | bytes 221192 | tf_op jit(solution)/shard_map/ppermute | solution.py:234
where the time goes:
time: 285 us; the launch traced here: 284 us
  Pallas kernels  170 us (60%)
  waiting for transfers between devices  99.2 us (35%)
  starting transfers between devices  14.9 us (5%)
    pallas_call x1, Pallas kernels, transform(): pl.pallas_call(functools.partial(exchange_kernel, n, n_dev, rows), in_spe...  121 us
    ppermute x12, waiting for transfers between devices, transform(): lax.ppermute(tiles[x * len(TILES) + t], 'dev', [(i, i ^ k) for i in range...  99.2 us
    pallas_call x6, Pallas kernels, transform(): pl.pallas_call(functools.partial(out_kernel, n, n_in, lanes), grid=(size...  46.2 us
    ppermute x12, starting transfers between devices, transform(): lax.ppermute(tiles[x * len(TILES) + t], 'dev', [(i, i ^ k) for i in range...  14.9 us
  transfers between devices with their start and end apart: 12, of which 3 were waited for; matrix products, arithmetic and copies ran while one was open for 0% of the time, Pallas kernels for 16%

commit v1 on v0

--- a/solution.py
+++ b/solution.py
@@ -9,6 +9,7 @@
 
 
 TILES = ((0, 48, 0, 1152), (48, 24, 0, 1152), (72, 8, 0, 1152), (80, 8, 0, 1152), (88, 8, 0, 768), (88, 8, 768, 384))
+PARTS = (1, 1, 1, 1, 3, 3)
 DIAGONAL = (6, 7)
 DIRECT = (2, 4, 3, 5, 1)
 F32, BF16 = jnp.float32, jnp.bfloat16
@@ -144,16 +145,18 @@
             return carry
 
         lax.fori_loop(0, n // 16, first, 0)
+        before = None
         for k in ks:
             step_two_three(k, i)
+            if before is not None:
+                send(before, i)
+            elif wait:
+                pl.semaphore_wait(barrier, len(DIRECT))
+            before = k
+        send(before, i)
 
     some(DIRECT[:2], 0, 0, True)
-    pl.semaphore_wait(barrier, len(DIRECT))
-    for k in DIRECT[:2]:
-        send(k, 0)
     some((*DIRECT[2:], 0, *DIAGONAL), 0, 0, False)
-    for k in (*DIRECT[2:], 0, *DIAGONAL):
-        send(k, 0)
 
     def row(i, carry):
         slot = lax.rem(i, 2)
@@ -187,10 +190,10 @@
         remote(k, g_ref.at[k], got[k]).wait()
 
 
-def out_kernel(n, n_in, wide, *refs):
+def out_kernel(n_in, wide, *refs):
     l4_ref, out_ref = refs[n_in], refs[-1]
     rhs = jnp.concatenate([r[...].reshape(-1, wide) for r in refs[:n_in]], axis=0)
-    out_ref[...] = dot(l4_ref[...], rhs).reshape(n, 8, wide)
+    out_ref[...] = dot(l4_ref[...], rhs).reshape(out_ref.shape)
 
 
 def solution(mesh):
@@ -204,9 +207,6 @@
         smem = pl.BlockSpec(memory_space=pltpu.SMEM)
         vmem = pl.BlockSpec(memory_space=pltpu.VMEM)
         hbm = pl.BlockSpec(memory_space=pl.ANY)
-
-        def const(shape):
-            return pl.BlockSpec(shape, lambda *_: (0,) * len(shape))
 
         square, second = (8 * n, 8 * n), (512, 4 * n)
         n_got = n_dev - len(DIAGONAL)
@@ -247,18 +247,19 @@
             for k in range(n_dev):
                 block, at = (moved[k, t_i], (0, 0)) if (k, t_i) in moved else (got[k], (a0 // 8, lane // lanes))
                 ins.append(block)
-                specs.append(pl.BlockSpec((rows, 8, lanes), lambda i, at=at: (0, at[0] + i, at[1])))
+                specs.append(pl.BlockSpec((rows, 8, lanes), lambda i, j, at=at: (0, at[0] + i, at[1])))
             n_in = len(ins)
             ins.append(l4)
-            specs.append(const(square))
+            parts = PARTS[t_i]
+            specs.append(pl.BlockSpec((8 * n // parts, 8 * n), lambda i, j: (j, 0)))
             if out is not None:
                 ins.append(out)
                 specs.append(hbm)
             out = pl.pallas_call(
-                functools.partial(out_kernel, n, n_in, lanes),
-                grid=(size // 8,),
+                functools.partial(out_kernel, n_in, lanes),
+                grid=(size // 8, parts),
                 in_specs=specs,
-                out_specs=pl.BlockSpec((n, 8, lanes), lambda i, at=(a0 // 8, lane // lanes): (0, at[0] + i, at[1])),
+                out_specs=pl.BlockSpec((n // parts, 8, lanes), lambda i, j, at=(a0 // 8, lane // lanes): (j, at[0] + i, at[1])),
                 out_shape=jax.ShapeDtypeStruct((n, n, wide), F32),
                 input_output_aliases={} if t_i == 0 else {len(ins) - 1: 0},
                 compiler_params=pltpu.CompilerParams(vmem_limit_bytes=67043328),

time: 285 us -> 286 us (level)
  no operation moved by 1% of the time
where the time goes in v1:
time: 286 us; the launch traced here: 285 us
  Pallas kernels  171 us (60%)
  waiting for transfers between devices  99.1 us (35%)
  starting transfers between devices  14.6 us (5%)
    pallas_call x1, Pallas kernels, transform(): pl.pallas_call(functools.partial(exchange_kernel, n, n_dev, rows), in_spe...  122 us
    ppermute x12, waiting for transfers between devices, transform(): lax.ppermute(tiles[x * len(TILES) + t], 'dev', [(i, i ^ k) for i in range...  99.1 us
    pallas_call x6, Pallas kernels, transform(): pl.pallas_call(functools.partial(out_kernel, n_in, lanes), grid=(size //...  47.1 us
    ppermute x12, starting transfers between devices, transform(): lax.ppermute(tiles[x * len(TILES) + t], 'dev', [(i, i ^ k) for i in range...  14.6 us
  transfers between devices with their start and end apart: 12, of which 3 were waited for; matrix products, arithmetic and copies ran while one was open for 0% of the time, Pallas kernels for 16%

profile of v1, /device:TPU:0, one launch (start us, length us, event | category | flops | bytes accessed | tf_op | source)
XLA Modules:
  0.0 285.2 jit_solution(779220193027735486)
XLA Ops:
  0.0 121.8 %exchange.1 = (bf16[12,96,1152]{2,1,0:T(8,128)(2,1)}, bf16[12,96,1152]{2,1,0:T(8,128)(2,1)}, bf16[12,96,1152]{2,1,0:T(8,128)(2,1)}, bf16[12,96,1152]{2,1,0:T(8,1...) custom-call(bf16[12,96,96,96]{3,2,1,0:T(8,128)(2,1)} %a_hbm.1, ...), custom_call_target="tpu_custom_call" | custom-call | tf_op jit(solution)/shard_map/exchange/pallas_call | solution.py:215
  121.8 1.5 collective-permute-start.10
  123.3 1.1 collective-permute-start.11
  124.4 1.5 collective-permute-start.4
  125.9 1.5 collective-permute-start.8
  127.3 1.0 collective-permute-start.9
  128.3 59.9 %collective-permute-done.4.refs_6_ = bf16[12,8,1152]{2,1,0:T(8,128)(2,1)} collective-permute-done((bf16[12,8,1152]{2,1,0:T(8,128)(2,1)}, bf16[12,8,1152]{2,1,0:T(8,128)(2,1)}, u32[]{:S(2)}, u32[]{:S(2)}) %collective-permute-start.4) | collective-permute-done | bytes 221216 | tf_op jit(solution)/shard_map/ppermute | solution.py:234
  188.2 1.4 collective-permute-start.6
  189.7 31.1 %collective-permute-done.6.refs_6_ = bf16[12,8,1152]{2,1,0:T(8,128)(2,1)} collective-permute-done((bf16[12,8,1152]{2,1,0:T(8,128)(2,1)}, bf16[12,8,1152]{2,1,0:T(8,128)(2,1)}, u32[]{:S(2)}, u32[]{:S(2)}) %collective-permute-start.6) | collective-permute-done | bytes 221216 | tf_op jit(solution)/shard_map/ppermute | solution.py:234
  220.8 0.6 collective-permute-start.7
  221.3 8.0 %collective-permute-done.7.refs_7_ = bf16[12,8,1152]{2,1,0:T(8,128)(2,1)} collective-permute-done((bf16[12,8,1152]{2,1,0:T(8,128)(2,1)}, bf16[12,8,1152]{2,1,0:T(8,128)(2,1)}, u32[]{:S(2)}, u32[]{:S(2)}) %collective-permute-start.7) | collective-permute-done | bytes 221216 | tf_op jit(solution)/shard_map/ppermute | solution.py:234
  229.3 0.9 collective-permute-start.5
  230.2 0.0 collective-permute-done.8.refs_6_
  230.2 1.4 collective-permute-start.2
  231.6 1.6 collective-permute-start.3
  233.2 1.4 collective-permute-start
  234.7 0.9 collective-permute-start.1
  235.5 2.5 last.1.refs_8_
  238.1 17.2 %out.6.refs_9_ = f32[96,96,1152]{2,1,0:T(8,128)} custom-call(bf16[12,96,1152]{2,1,0:T(8,128)(2,1)} %get-tuple-element.23.after_ref.refs_0_, bf16[12,96,1152]{2,1,0:T(8,128)(2,1)} %get-tuple-element.24.refs_1_, bf16[12,96,1152]{2,1,0:T(8,128)(2,1)} %get-tuple-element.25.refs_2_, bf16[12,96,1152]{2,1,0:T(8,128)(2,1)} %get-tuple-element.26.refs_3_, ...), custom_call_target="tpu_custom_call" | custom-call | tf_op jit(solution)/shard_map/out/pallas_call | solution.py:258
  255.3 10.6 %out.7.refs_9_ = f32[96,96,1152]{2,1,0:T(8,128)} custom-call(bf16[12,96,1152]{2,1,0:T(8,128)(2,1)} %get-tuple-element.23.after_ref.refs_0_, bf16[12,96,1152]{2,1,0:T(8,128)(2,1)} %get-tuple-element.24.refs_1_, bf16[12,96,1152]{2,1,0:T(8,128)(2,1)} %get-tuple-element.25.refs_2_, ...), custom_call_target="tpu_custom_call", output_to_operand_aliasing={{}: (9, {})} | custom-call | tf_op jit(solution)/shard_map/out/pallas_call | solution.py:258
  265.9 5.4 %out.8.refs_9_ = f32[96,96,1152]{2,1,0:T(8,128)} custom-call(bf16[12,96,1152]{2,1,0:T(8,128)(2,1)} %get-tuple-element.23.after_ref.refs_0_, bf16[12,96,1152]{2,1,0:T(8,128)(2,1)} %get-tuple-element.24.refs_1_, bf16[12,96,1152]{2,1,0:T(8,128)(2,1)} %get-tuple-element.25.refs_2_, ...), custom_call_target="tpu_custom_call", output_to_operand_aliasing={{}: (9, {})} | custom-call | tf_op jit(solution)/shard_map/out/pallas_call | solution.py:258
  271.3 5.4 %out.9.refs_9_ = f32[96,96,1152]{2,1,0:T(8,128)} custom-call(bf16[12,96,1152]{2,1,0:T(8,128)(2,1)} %get-tuple-element.23.after_ref.refs_0_, bf16[12,96,1152]{2,1,0:T(8,128)(2,1)} %get-tuple-element.24.refs_1_, bf16[12,96,1152]{2,1,0:T(8,128)(2,1)} %get-tuple-element.25.refs_2_, ...), custom_call_target="tpu_custom_call", output_to_operand_aliasing={{}: (9, {})} | custom-call | tf_op jit(solution)/shard_map/out/pallas_call | solution.py:258
  276.8 4.5 %out.10.refs_9_ = f32[96,96,1152]{2,1,0:T(8,128)} custom-call(bf16[12,96,1152]{2,1,0:T(8,128)(2,1)} %get-tuple-element.23.after_ref.refs_0_, bf16[12,96,1152]{2,1,0:T(8,128)(2,1)} %get-tuple-element.24.refs_1_, bf16[12,96,1152]{2,1,0:T(8,128)(2,1)} %get-tuple-element.25.refs_2_, ...), custom_call_target="tpu_custom_call", output_to_operand_aliasing={{}: (9, {})} | custom-call | tf_op jit(solution)/shard_map/out/pallas_call | solution.py:258
  281.3 3.9 %out.11 = f32[96,96,1152]{2,1,0:T(8,128)} custom-call(bf16[12,96,1152]{2,1,0:T(8,128)(2,1)} %get-tuple-element.23.after_ref.refs_0_, bf16[12,96,1152]{2,1,0:T(8,128)(2,1)} %get-tuple-element.24.refs_1_, bf16[12,96,1152]{2,1,0:T(8,128)(2,1)} %get-tuple-element.25.refs_2_, ...), custom_call_target="tpu_custom_call", output_to_operand_aliasing={{}: (9, {})} | custom-call | tf_op jit(solution)/shard_map/out/pallas_call | solution.py:258
  (8 shorter events, 0.0 us)
Async XLA Ops:
  121.8 111.4 %collective-permute-start.10 = (bf16[12,48,1152]{2,1,0:T(8,128)(2,1)}, bf16[12,48,1152]{2,1,0:T(8,128)(2,1)}, u32[]{:S(2)}, u32[]{:S(2)}) collective-permute-start(bf16[12,48,1152]{2,1,0:T(8,128)(2,1)} %get-tuple-element.39), channel_id=1, source_target_pairs={{0,6},{1,7},{2,4},{3,5},{4,2},{5,3},{6,0},{7,1},{8,14},{9,15},{10,... | collective-permute-start | bytes 3981320 | tf_op jit(solution)/shard_map/ppermute | solution.py:234
  123.3 111.4 %collective-permute-start.11 = (bf16[12,48,1152]{2,1,0:T(8,128)(2,1)}, bf16[12,48,1152]{2,1,0:T(8,128)(2,1)}, u32[]{:S(2)}, u32[]{:S(2)}) collective-permute-start(bf16[12,48,1152]{2,1,0:T(8,128)(2,1)} %get-tuple-element.40), channel_id=1, source_target_pairs={{0,7},{1,6},{2,5},{3,4},{4,3},{5,2},{6,1},{7,0},{8,15},{9,14},{10,... | collective-permute-start | bytes 3981320 | tf_op jit(solution)/shard_map/ppermute | solution.py:234
  124.4 63.8 %collective-permute-start.4 = (bf16[12,8,1152]{2,1,0:T(8,128)(2,1)}, bf16[12,8,1152]{2,1,0:T(8,128)(2,1)}, u32[]{:S(2)}, u32[]{:S(2)}) collective-permute-start(bf16[12,8,1152]{2,1,0:T(8,128)(2,1)} %get-tuple-element.33), channel_id=1, source_target_pairs={{0,6},{1,7},{2,4},{3,5},{4,2},{5,3},{6,0},{7,1},{8,14},{9,15},{10,... | collective-permute-start | bytes 663560 | tf_op jit(solution)/shard_map/ppermute | solution.py:234
  125.9 104.4 %collective-permute-start.8 = (bf16[12,24,1152]{2,1,0:T(8,128)(2,1)}, bf16[12,24,1152]{2,1,0:T(8,128)(2,1)}, u32[]{:S(2)}, u32[]{:S(2)}) collective-permute-start(bf16[12,24,1152]{2,1,0:T(8,128)(2,1)} %get-tuple-element.37), channel_id=1, source_target_pairs={{0,6},{1,7},{2,4},{3,5},{4,2},{5,3},{6,0},{7,1},{8,14},{9,15},{10,... | collective-permute-start | bytes 1990664 | tf_op jit(solution)/shard_map/ppermute | solution.py:234
  127.3 104.3 %collective-permute-start.9 = (bf16[12,24,1152]{2,1,0:T(8,128)(2,1)}, bf16[12,24,1152]{2,1,0:T(8,128)(2,1)}, u32[]{:S(2)}, u32[]{:S(2)}) collective-permute-start(bf16[12,24,1152]{2,1,0:T(8,128)(2,1)} %get-tuple-element.38), channel_id=1, source_target_pairs={{0,7},{1,6},{2,5},{3,4},{4,3},{5,2},{6,1},{7,0},{8,15},{9,14},{10,... | collective-permute-start | bytes 1990664 | tf_op jit(solution)/shard_map/ppermute | solution.py:234
  188.2 32.5 %collective-permute-start.6 = (bf16[12,8,1152]{2,1,0:T(8,128)(2,1)}, bf16[12,8,1152]{2,1,0:T(8,128)(2,1)}, u32[]{:S(2)}, u32[]{:S(2)}) collective-permute-start(bf16[12,8,1152]{2,1,0:T(8,128)(2,1)} %get-tuple-element.35), channel_id=1, source_target_pairs={{0,6},{1,7},{2,4},{3,5},{4,2},{5,3},{6,0},{7,1},{8,14},{9,15},{10,... | collective-permute-start | bytes 663560 | tf_op jit(solution)/shard_map/ppermute | solution.py:234
  220.8 8.6 %collective-permute-start.7 = (bf16[12,8,1152]{2,1,0:T(8,128)(2,1)}, bf16[12,8,1152]{2,1,0:T(8,128)(2,1)}, u32[]{:S(2)}, u32[]{:S(2)}) collective-permute-start(bf16[12,8,1152]{2,1,0:T(8,128)(2,1)} %get-tuple-element.36), channel_id=1, source_target_pairs={{0,7},{1,6},{2,5},{3,4},{4,3},{5,2},{6,1},{7,0},{8,15},{9,14},{10,... | collective-permute-start | bytes 663560 | tf_op jit(solution)/shard_map/ppermute | solution.py:234
  229.3 42.0 %collective-permute-start.5 = (bf16[12,8,1152]{2,1,0:T(8,128)(2,1)}, bf16[12,8,1152]{2,1,0:T(8,128)(2,1)}, u32[]{:S(2)}, u32[]{:S(2)}) collective-permute-start(bf16[12,8,1152]{2,1,0:T(8,128)(2,1)} %get-tuple-element.34), channel_id=1, source_target_pairs={{0,7},{1,6},{2,5},{3,4},{4,3},{5,2},{6,1},{7,0},{8,15},{9,14},{10,... | collective-permute-start | bytes 663560 | tf_op jit(solution)/shard_map/ppermute | solution.py:234
  230.2 46.5 %collective-permute-start.2 = (bf16[12,8,768]{2,1,0:T(8,128)(2,1)}, bf16[12,8,768]{2,1,0:T(8,128)(2,1)}, u32[]{:S(2)}, u32[]{:S(2)}) collective-permute-start(bf16[12,8,768]{2,1,0:T(8,128)(2,1)} %get-tuple-element.31), channel_id=1, source_target_pairs={{0,6},{1,7},{2,4},{3,5},{4,2},{5,3},{6,0},{7,1},{8,14},{9,15},{10,... | collective-permute-start | bytes 442376 | tf_op jit(solution)/shard_map/ppermute | solution.py:234
  231.6 45.1 %collective-permute-start.3 = (bf16[12,8,768]{2,1,0:T(8,128)(2,1)}, bf16[12,8,768]{2,1,0:T(8,128)(2,1)}, u32[]{:S(2)}, u32[]{:S(2)}) collective-permute-start(bf16[12,8,768]{2,1,0:T(8,128)(2,1)} %get-tuple-element.32), channel_id=1, source_target_pairs={{0,7},{1,6},{2,5},{3,4},{4,3},{5,2},{6,1},{7,0},{8,15},{9,14},{10,... | collective-permute-start | bytes 442376 | tf_op jit(solution)/shard_map/ppermute | solution.py:234
  233.2 48.1 %collective-permute-start = (bf16[12,8,384]{2,1,0:T(8,128)(2,1)}, bf16[12,8,384]{2,1,0:T(8,128)(2,1)}, u32[]{:S(2)}, u32[]{:S(2)}) collective-permute-start(bf16[12,8,384]{2,1,0:T(8,128)(2,1)} %get-tuple-element.29), channel_id=1, source_target_pairs={{0,6},{1,7},{2,4},{3,5},{4,2},{5,3},{6,0},{7,1},{8,14},{9,15},{10,... | collective-permute-start | bytes 221192 | tf_op jit(solution)/shard_map/ppermute | solution.py:234
  234.7 46.7 %collective-permute-start.1 = (bf16[12,8,384]{2,1,0:T(8,128)(2,1)}, bf16[12,8,384]{2,1,0:T(8,128)(2,1)}, u32[]{:S(2)}, u32[]{:S(2)}) collective-permute-start(bf16[12,8,384]{2,1,0:T(8,128)(2,1)} %get-tuple-element.30), channel_id=1, source_target_pairs={{0,7},{1,6},{2,5},{3,4},{4,3},{5,2},{6,1},{7,0},{8,15},{9,14},{10,... | collective-permute-start | bytes 221192 | tf_op jit(solution)/shard_map/ppermute | solution.py:234

commit v2 on v1

--- a/solution.py
+++ b/solution.py
@@ -8,8 +8,7 @@
 from jax.sharding import PartitionSpec as P
 
 
-TILES = ((0, 48, 0, 1152), (48, 24, 0, 1152), (72, 8, 0, 1152), (80, 8, 0, 1152), (88, 8, 0, 768), (88, 8, 768, 384))
-PARTS = (1, 1, 1, 1, 3, 3)
+TILES = ((0, 48, 0, 1152), (48, 24, 0, 1152), (72, 8, 0, 1152), (80, 8, 0, 1152), (88, 8, 0, 640), (88, 8, 640, 512))
 DIAGONAL = (6, 7)
 DIRECT = (2, 4, 3, 5, 1)
 F32, BF16 = jnp.float32, jnp.bfloat16
@@ -196,6 +195,21 @@
     out_ref[...] = dot(l4_ref[...], rhs).reshape(out_ref.shape)
 
 
+def tail_kernel(n, n_in, a0, lane, lanes, parts, *refs):
+    l4_ref, out_hbm, (v_ref, sem) = refs[n_in], refs[-3], refs[-2:]
+    rhs = jnp.concatenate([r[...].reshape(-1, lanes) for r in refs[:n_in]], axis=0)
+    size = n // parts
+    copies = []
+    for x in range(parts):
+        i = pl.ds(x * size, size)
+        v_ref[i] = dot(l4_ref[pl.ds(8 * size * x, 8 * size)], rhs).reshape(size, 8, lanes)
+        copies.append(pltpu.make_async_copy(
+            v_ref.at[i], out_hbm.at[i, pl.ds(a0, 8), pl.ds(lane, lanes)], sem.at[x]))
+        copies[-1].start()
+    for copy in copies:
+        copy.wait()
+
+
 def solution(mesh):
     n_dev = mesh.shape['dev']
 
@@ -207,6 +221,9 @@
         smem = pl.BlockSpec(memory_space=pltpu.SMEM)
         vmem = pl.BlockSpec(memory_space=pltpu.VMEM)
         hbm = pl.BlockSpec(memory_space=pl.ANY)
+
+        def const(shape):
+            return pl.BlockSpec(shape, lambda *_: (0,) * len(shape))
 
         square, second = (8 * n, 8 * n), (512, 4 * n)
         n_got = n_dev - len(DIAGONAL)
@@ -245,23 +262,27 @@
         for t_i, (a0, size, lane, lanes) in enumerate(TILES):
             ins, specs = [], []
             for k in range(n_dev):
-                block, at = (moved[k, t_i], (0, 0)) if (k, t_i) in moved else (got[k], (a0 // 8, lane // lanes))
+                block, at = (moved[k, t_i], (0, 0)) if (k, t_i) in moved else (got[k], (a0, lane))
                 ins.append(block)
-                specs.append(pl.BlockSpec((rows, 8, lanes), lambda i, j, at=at: (0, at[0] + i, at[1])))
+                specs.append(pl.BlockSpec((pl.Element(rows), pl.Element(8), pl.Element(lanes)), lambda i, at=at: (0, pl.multiple_of(at[0] + 8 * i, 8), at[1])))
             n_in = len(ins)
             ins.append(l4)
-            parts = PARTS[t_i]
-            specs.append(pl.BlockSpec((8 * n // parts, 8 * n), lambda i, j: (j, 0)))
+            specs.append(const(square))
             if out is not None:
                 ins.append(out)
                 specs.append(hbm)
+            alone = size == 8
             out = pl.pallas_call(
-                functools.partial(out_kernel, n_in, lanes),
-                grid=(size // 8, parts),
+                functools.partial(tail_kernel, n, n_in, a0, lane, lanes, 3) if alone
+                else functools.partial(out_kernel, n_in, lanes),
+                grid=(size // 8,),
                 in_specs=specs,
-                out_specs=pl.BlockSpec((n // parts, 8, lanes), lambda i, j, at=(a0 // 8, lane // lanes): (j, at[0] + i, at[1])),
+                out_specs=hbm if alone else pl.BlockSpec(
+                    (pl.Element(n), pl.Element(8), pl.Element(lanes)),
+                    lambda i, at=(a0, lane): (0, pl.multiple_of(at[0] + 8 * i, 8), at[1])),
                 out_shape=jax.ShapeDtypeStruct((n, n, wide), F32),
                 input_output_aliases={} if t_i == 0 else {len(ins) - 1: 0},
+                scratch_shapes=[pltpu.VMEM((n, 8, lanes), F32), pltpu.SemaphoreType.DMA((3,))] * alone,
                 compiler_params=pltpu.CompilerParams(vmem_limit_bytes=67043328),
                 name='out',
             )(*ins)

time: 286 us -> 283 us (0.990)
  Pallas kernels: 171 us -> 168 us
    pallas_call x6, Pallas kernels: 47.1 us -> 44 us  [transform(): pl.pallas_call(functools.partial(tail_kernel, n, n_in, a0, lane, lanes, 3...]
  transfers between devices with their start and end apart: 12 -> 12, of which waited for: 3 -> 3; matrix products, arithmetic and copies ran while one was open for 0% -> 0% of each run, Pallas kernels for 16% -> 15%
where the time goes in v2:
time: 283 us; the launch traced here: 282 us
  Pallas kernels  168 us (59%)
  waiting for transfers between devices  99.1 us (35%)
  starting transfers between devices  14.6 us (5%)
    pallas_call x1, Pallas kernels, transform(): pl.pallas_call(functools.partial(exchange_kernel, n, n_dev, rows), in_spe...  122 us
    ppermute x12, waiting for transfers between devices, transform(): lax.ppermute(tiles[x * len(TILES) + t], 'dev', [(i, i ^ k) for i in range...  99.1 us
    pallas_call x6, Pallas kernels, transform(): pl.pallas_call(functools.partial(tail_kernel, n, n_in, a0, lane, lanes, 3...  44 us
    ppermute x12, starting transfers between devices, transform(): lax.ppermute(tiles[x * len(TILES) + t], 'dev', [(i, i ^ k) for i in range...  14.6 us
  transfers between devices with their start and end apart: 12, of which 3 were waited for; matrix products, arithmetic and copies ran while one was open for 0% of the time, Pallas kernels for 15%

profile of v2, /device:TPU:0, one launch (start us, length us, event | category | flops | bytes accessed | tf_op | source)
XLA Modules:
  0.0 282.4 jit_solution(11800372663565260058)
XLA Ops:
  0.0 121.8 %exchange.1 = (bf16[12,96,1152]{2,1,0:T(8,128)(2,1)}, bf16[12,96,1152]{2,1,0:T(8,128)(2,1)}, bf16[12,96,1152]{2,1,0:T(8,128)(2,1)}, bf16[12,96,1152]{2,1,0:T(8,1...) custom-call(bf16[12,96,96,96]{3,2,1,0:T(8,128)(2,1)} %a_hbm.1, ...), custom_call_target="tpu_custom_call" | custom-call | tf_op jit(solution)/shard_map/exchange/pallas_call | solution.py:232
  121.8 1.5 collective-permute-start.10
  123.3 1.1 collective-permute-start.11
  124.4 1.5 collective-permute-start.4
  125.9 1.5 collective-permute-start.8
  127.3 1.0 collective-permute-start.9
  128.3 59.9 %collective-permute-done.4.refs_6_ = bf16[12,8,1152]{2,1,0:T(8,128)(2,1)} collective-permute-done((bf16[12,8,1152]{2,1,0:T(8,128)(2,1)}, bf16[12,8,1152]{2,1,0:T(8,128)(2,1)}, u32[]{:S(2)}, u32[]{:S(2)}) %collective-permute-start.4) | collective-permute-done | bytes 221216 | tf_op jit(solution)/shard_map/ppermute | solution.py:251
  188.2 1.4 collective-permute-start.6
  189.7 31.1 %collective-permute-done.6.refs_6_ = bf16[12,8,1152]{2,1,0:T(8,128)(2,1)} collective-permute-done((bf16[12,8,1152]{2,1,0:T(8,128)(2,1)}, bf16[12,8,1152]{2,1,0:T(8,128)(2,1)}, u32[]{:S(2)}, u32[]{:S(2)}) %collective-permute-start.6) | collective-permute-done | bytes 221216 | tf_op jit(solution)/shard_map/ppermute | solution.py:251
  220.8 0.6 collective-permute-start.7
  221.3 8.0 %collective-permute-done.7.refs_7_ = bf16[12,8,1152]{2,1,0:T(8,128)(2,1)} collective-permute-done((bf16[12,8,1152]{2,1,0:T(8,128)(2,1)}, bf16[12,8,1152]{2,1,0:T(8,128)(2,1)}, u32[]{:S(2)}, u32[]{:S(2)}) %collective-permute-start.7) | collective-permute-done | bytes 221216 | tf_op jit(solution)/shard_map/ppermute | solution.py:251
  229.3 0.9 collective-permute-start.5
  230.2 0.0 collective-permute-done.8.refs_6_
  230.2 1.4 collective-permute-start.2
  231.6 1.6 collective-permute-start.3
  233.2 1.4 collective-permute-start
  234.7 0.9 collective-permute-start.1
  235.5 2.5 last.1.refs_8_
  238.1 17.2 %out.6.refs_9_ = f32[96,96,1152]{2,1,0:T(8,128)} custom-call(bf16[12,96,1152]{2,1,0:T(8,128)(2,1)} %get-tuple-element.23.after_ref.refs_0_, bf16[12,96,1152]{2,1,0:T(8,128)(2,1)} %get-tuple-element.24.refs_1_, bf16[12,96,1152]{2,1,0:T(8,128)(2,1)} %get-tuple-element.25.refs_2_, bf16[12,96,1152]{2,1,0:T(8,128)(2,1)} %get-tuple-element.26.refs_3_, ...), custom_call_target="tpu_custom_call" | custom-call | tf_op jit(solution)/shard_map/out/pallas_call | solution.py:275
  255.3 10.5 %out.7.refs_9_ = f32[96,96,1152]{2,1,0:T(8,128)} custom-call(bf16[12,96,1152]{2,1,0:T(8,128)(2,1)} %get-tuple-element.23.after_ref.refs_0_, bf16[12,96,1152]{2,1,0:T(8,128)(2,1)} %get-tuple-element.24.refs_1_, bf16[12,96,1152]{2,1,0:T(8,128)(2,1)} %get-tuple-element.25.refs_2_, ...), custom_call_target="tpu_custom_call", output_to_operand_aliasing={{}: (9, {})} | custom-call | tf_op jit(solution)/shard_map/out/pallas_call | solution.py:275
  265.8 4.7 %out.8.refs_9_ = f32[96,96,1152]{2,1,0:T(8,128)} custom-call(bf16[12,96,1152]{2,1,0:T(8,128)(2,1)} %get-tuple-element.23.after_ref.refs_0_, bf16[12,96,1152]{2,1,0:T(8,128)(2,1)} %get-tuple-element.24.refs_1_, bf16[12,96,1152]{2,1,0:T(8,128)(2,1)} %get-tuple-element.25.refs_2_, ...), custom_call_target="tpu_custom_call", output_to_operand_aliasing={{}: (9, {})} | custom-call | tf_op jit(solution)/shard_map/out/pallas_call | solution.py:275
  270.5 4.7 %out.9.refs_9_ = f32[96,96,1152]{2,1,0:T(8,128)} custom-call(bf16[12,96,1152]{2,1,0:T(8,128)(2,1)} %get-tuple-element.23.after_ref.refs_0_, bf16[12,96,1152]{2,1,0:T(8,128)(2,1)} %get-tuple-element.24.refs_1_, bf16[12,96,1152]{2,1,0:T(8,128)(2,1)} %get-tuple-element.25.refs_2_, ...), custom_call_target="tpu_custom_call", output_to_operand_aliasing={{}: (9, {})} | custom-call | tf_op jit(solution)/shard_map/out/pallas_call | solution.py:275
  275.3 3.7 %out.10.refs_9_ = f32[96,96,1152]{2,1,0:T(8,128)} custom-call(bf16[12,96,1152]{2,1,0:T(8,128)(2,1)} %get-tuple-element.23.after_ref.refs_0_, bf16[12,96,1152]{2,1,0:T(8,128)(2,1)} %get-tuple-element.24.refs_1_, bf16[12,96,1152]{2,1,0:T(8,128)(2,1)} %get-tuple-element.25.refs_2_, ...), custom_call_target="tpu_custom_call", output_to_operand_aliasing={{}: (9, {})} | custom-call | tf_op jit(solution)/shard_map/out/pallas_call | solution.py:275
  279.0 3.2 %out.11 = f32[96,96,1152]{2,1,0:T(8,128)} custom-call(bf16[12,96,1152]{2,1,0:T(8,128)(2,1)} %get-tuple-element.23.after_ref.refs_0_, bf16[12,96,1152]{2,1,0:T(8,128)(2,1)} %get-tuple-element.24.refs_1_, bf16[12,96,1152]{2,1,0:T(8,128)(2,1)} %get-tuple-element.25.refs_2_, ...), custom_call_target="tpu_custom_call", output_to_operand_aliasing={{}: (9, {})} | custom-call | tf_op jit(solution)/shard_map/out/pallas_call | solution.py:275
  (8 shorter events, 0.0 us)
Async XLA Ops:
  121.8 111.4 %collective-permute-start.10 = (bf16[12,48,1152]{2,1,0:T(8,128)(2,1)}, bf16[12,48,1152]{2,1,0:T(8,128)(2,1)}, u32[]{:S(2)}, u32[]{:S(2)}) collective-permute-start(bf16[12,48,1152]{2,1,0:T(8,128)(2,1)} %get-tuple-element.39), channel_id=1, source_target_pairs={{0,6},{1,7},{2,4},{3,5},{4,2},{5,3},{6,0},{7,1},{8,14},{9,15},{10,... | collective-permute-start | bytes 3981320 | tf_op jit(solution)/shard_map/ppermute | solution.py:251
  123.3 111.4 %collective-permute-start.11 = (bf16[12,48,1152]{2,1,0:T(8,128)(2,1)}, bf16[12,48,1152]{2,1,0:T(8,128)(2,1)}, u32[]{:S(2)}, u32[]{:S(2)}) collective-permute-start(bf16[12,48,1152]{2,1,0:T(8,128)(2,1)} %get-tuple-element.40), channel_id=1, source_target_pairs={{0,7},{1,6},{2,5},{3,4},{4,3},{5,2},{6,1},{7,0},{8,15},{9,14},{10,... | collective-permute-start | bytes 3981320 | tf_op jit(solution)/shard_map/ppermute | solution.py:251
  124.4 63.8 %collective-permute-start.4 = (bf16[12,8,1152]{2,1,0:T(8,128)(2,1)}, bf16[12,8,1152]{2,1,0:T(8,128)(2,1)}, u32[]{:S(2)}, u32[]{:S(2)}) collective-permute-start(bf16[12,8,1152]{2,1,0:T(8,128)(2,1)} %get-tuple-element.33), channel_id=1, source_target_pairs={{0,6},{1,7},{2,4},{3,5},{4,2},{5,3},{6,0},{7,1},{8,14},{9,15},{10,... | collective-permute-start | bytes 663560 | tf_op jit(solution)/shard_map/ppermute | solution.py:251
  125.9 104.4 %collective-permute-start.8 = (bf16[12,24,1152]{2,1,0:T(8,128)(2,1)}, bf16[12,24,1152]{2,1,0:T(8,128)(2,1)}, u32[]{:S(2)}, u32[]{:S(2)}) collective-permute-start(bf16[12,24,1152]{2,1,0:T(8,128)(2,1)} %get-tuple-element.37), channel_id=1, source_target_pairs={{0,6},{1,7},{2,4},{3,5},{4,2},{5,3},{6,0},{7,1},{8,14},{9,15},{10,... | collective-permute-start | bytes 1990664 | tf_op jit(solution)/shard_map/ppermute | solution.py:251
  127.3 104.3 %collective-permute-start.9 = (bf16[12,24,1152]{2,1,0:T(8,128)(2,1)}, bf16[12,24,1152]{2,1,0:T(8,128)(2,1)}, u32[]{:S(2)}, u32[]{:S(2)}) collective-permute-start(bf16[12,24,1152]{2,1,0:T(8,128)(2,1)} %get-tuple-element.38), channel_id=1, source_target_pairs={{0,7},{1,6},{2,5},{3,4},{4,3},{5,2},{6,1},{7,0},{8,15},{9,14},{10,... | collective-permute-start | bytes 1990664 | tf_op jit(solution)/shard_map/ppermute | solution.py:251
  188.2 32.5 %collective-permute-start.6 = (bf16[12,8,1152]{2,1,0:T(8,128)(2,1)}, bf16[12,8,1152]{2,1,0:T(8,128)(2,1)}, u32[]{:S(2)}, u32[]{:S(2)}) collective-permute-start(bf16[12,8,1152]{2,1,0:T(8,128)(2,1)} %get-tuple-element.35), channel_id=1, source_target_pairs={{0,6},{1,7},{2,4},{3,5},{4,2},{5,3},{6,0},{7,1},{8,14},{9,15},{10,... | collective-permute-start | bytes 663560 | tf_op jit(solution)/shard_map/ppermute | solution.py:251
  220.8 8.6 %collective-permute-start.7 = (bf16[12,8,1152]{2,1,0:T(8,128)(2,1)}, bf16[12,8,1152]{2,1,0:T(8,128)(2,1)}, u32[]{:S(2)}, u32[]{:S(2)}) collective-permute-start(bf16[12,8,1152]{2,1,0:T(8,128)(2,1)} %get-tuple-element.36), channel_id=1, source_target_pairs={{0,7},{1,6},{2,5},{3,4},{4,3},{5,2},{6,1},{7,0},{8,15},{9,14},{10,... | collective-permute-start | bytes 663560 | tf_op jit(solution)/shard_map/ppermute | solution.py:251
  229.3 41.2 %collective-permute-start.5 = (bf16[12,8,1152]{2,1,0:T(8,128)(2,1)}, bf16[12,8,1152]{2,1,0:T(8,128)(2,1)}, u32[]{:S(2)}, u32[]{:S(2)}) collective-permute-start(bf16[12,8,1152]{2,1,0:T(8,128)(2,1)} %get-tuple-element.34), channel_id=1, source_target_pairs={{0,7},{1,6},{2,5},{3,4},{4,3},{5,2},{6,1},{7,0},{8,15},{9,14},{10,... | collective-permute-start | bytes 663560 | tf_op jit(solution)/shard_map/ppermute | solution.py:251
  230.2 45.0 %collective-permute-start.2 = (bf16[12,8,640]{2,1,0:T(8,128)(2,1)}, bf16[12,8,640]{2,1,0:T(8,128)(2,1)}, u32[]{:S(2)}, u32[]{:S(2)}) collective-permute-start(bf16[12,8,640]{2,1,0:T(8,128)(2,1)} %get-tuple-element.31), channel_id=1, source_target_pairs={{0,6},{1,7},{2,4},{3,5},{4,2},{5,3},{6,0},{7,1},{8,14},{9,15},{10,... | collective-permute-start | bytes 368648 | tf_op jit(solution)/shard_map/ppermute | solution.py:251
  231.6 43.6 %collective-permute-start.3 = (bf16[12,8,640]{2,1,0:T(8,128)(2,1)}, bf16[12,8,640]{2,1,0:T(8,128)(2,1)}, u32[]{:S(2)}, u32[]{:S(2)}) collective-permute-start(bf16[12,8,640]{2,1,0:T(8,128)(2,1)} %get-tuple-element.32), channel_id=1, source_target_pairs={{0,7},{1,6},{2,5},{3,4},{4,3},{5,2},{6,1},{7,0},{8,15},{9,14},{10,... | collective-permute-start | bytes 368648 | tf_op jit(solution)/shard_map/ppermute | solution.py:251
  233.2 45.7 %collective-permute-start = (bf16[12,8,512]{2,1,0:T(8,128)(2,1)}, bf16[12,8,512]{2,1,0:T(8,128)(2,1)}, u32[]{:S(2)}, u32[]{:S(2)}) collective-permute-start(bf16[12,8,512]{2,1,0:T(8,128)(2,1)} %get-tuple-element.29), channel_id=1, source_target_pairs={{0,6},{1,7},{2,4},{3,5},{4,2},{5,3},{6,0},{7,1},{8,14},{9,15},{10,... | collective-permute-start | bytes 294920 | tf_op jit(solution)/shard_map/ppermute | solution.py:251
  234.7 44.3 %collective-permute-start.1 = (bf16[12,8,512]{2,1,0:T(8,128)(2,1)}, bf16[12,8,512]{2,1,0:T(8,128)(2,1)}, u32[]{:S(2)}, u32[]{:S(2)}) collective-permute-start(bf16[12,8,512]{2,1,0:T(8,128)(2,1)} %get-tuple-element.30), channel_id=1, source_target_pairs={{0,7},{1,6},{2,5},{3,4},{4,3},{5,2},{6,1},{7,0},{8,15},{9,14},{10,... | collective-permute-start | bytes 294920 | tf_op jit(solution)/shard_map/ppermute | solution.py:251

commit v3 on v2

--- a/solution.py
+++ b/solution.py
@@ -8,7 +8,8 @@
 from jax.sharding import PartitionSpec as P
 
 
-TILES = ((0, 48, 0, 1152), (48, 24, 0, 1152), (72, 8, 0, 1152), (80, 8, 0, 1152), (88, 8, 0, 640), (88, 8, 640, 512))
+TILES = ((0, 48, 0, 1152), (48, 24, 0, 1152), (72, 8, 0, 1152), (80, 8, 0, 1152), (88, 8, 0, 768), (88, 8, 768, 384))
+TAIL = 88
 DIAGONAL = (6, 7)
 DIRECT = (2, 4, 3, 5, 1)
 F32, BF16 = jnp.float32, jnp.bfloat16
@@ -33,32 +34,35 @@
     return lax.dot_general(c, eye, (((0,), (0,)), ((), ())), preferred_element_type=F32).astype(BF16)
 
 
-def build_first(n, c_ref, l1_ref, r2_ref, ct_ref):
+def build_small(n, c_ref, r2_ref, ct_ref):
     c = c_ref[...]
-    ct = transposed(c, n)
-    ct_ref[...] = ct
-    tall = dot(pick((8 * n, n), lambda i, j: i // 8 == j), ct).astype(BF16)
-    wide = dot(tall, pick((n, 8 * n), lambda i, j: j % n == i))
-    keep = one_hot((8 * n, 8 * n), lambda i, j: i % 8 == j // n)
-    l1_ref[...] = jnp.where(keep, wide, 0.0).astype(BF16)
+    ct_ref[...] = transposed(c, n)
     tall = dot(pick((512, n), lambda i, j: i % 128 == j), c).astype(BF16)
     wide = dot(tall, pick((n, 4 * n), lambda i, j: j % n == i))
     keep = one_hot((512, 4 * n), lambda i, j: i // 128 == j // n)
     r2_ref[...] = jnp.where(keep, wide, 0.0).astype(BF16)
 
 
-def last_kernel(n, rows, me_ref, c_ref, after_ref, l4_ref):
+def build_l1(n, first, size, ct_ref, l1_ref):
+    tall = dot(pick((8 * size, n), lambda i, j: i // 8 + first == j), ct_ref[...]).astype(BF16)
+    wide = dot(tall, pick((n, 8 * n), lambda i, j: j % n == i))
+    keep = one_hot((8 * size, 8 * n), lambda i, j: i % 8 == j // n)
+    l1_ref[pl.ds(pl.multiple_of(first * 8, 8 * size), 8 * size)] = jnp.where(keep, wide, 0.0).astype(BF16)
+
+
+def last_kernel(n, rows, spans, me_ref, c_ref, after_ref, *l4_refs):
     me = me_ref[0]
-
-    def source(r, col):
-        m = col // 8
-        return r == (me ^ (m // rows)) * rows + m % rows
-
     ct = transposed(c_ref[...], n)
     tall = dot(pick((8 * n, n), lambda i, j: i // 8 == j), ct).astype(BF16)
-    wide = dot(tall, pick((n, 8 * n), source))
-    keep = one_hot((8 * n, 8 * n), lambda i, j: i % 8 == j % 8)
-    l4_ref[...] = jnp.where(keep, wide, 0.0).astype(BF16)
+    for (k0, k1), l4_ref in zip(spans, l4_refs):
+        def source(r, col, k0=k0):
+            m = col // 8 + k0 * rows
+            return r == (me ^ (m // rows)) * rows + m % rows
+
+        width = 8 * rows * (k1 - k0)
+        wide = dot(tall, pick((n, width), source))
+        keep = one_hot((8 * n, width), lambda i, j: i % 8 == j % 8)
+        l4_ref[...] = jnp.where(keep, wide, 0.0).astype(BF16)
 
 
 def flipped(me, k):
@@ -91,7 +95,9 @@
     for g in range(n // 16):
         chunk(g).start()
     fetch(1).start()
-    build_first(n, c_ref, l1_ref, r2_ref, ct_ref)
+    build_small(n, c_ref, r2_ref, ct_ref)
+    for k in DIRECT[:2]:
+        build_l1(n, flipped(me, k) * nj, nj, ct_ref, l1_ref)
     zero = jnp.zeros((8 * n, 128 - n), BF16)
 
     def remote(k, src, dst):
@@ -155,6 +161,7 @@
         send(before, i)
 
     some(DIRECT[:2], 0, 0, True)
+    build_l1(n, 0, n, ct_ref, l1_ref)
     some((*DIRECT[2:], 0, *DIAGONAL), 0, 0, False)
 
     def row(i, carry):
@@ -196,15 +203,23 @@
 
 
 def tail_kernel(n, n_in, a0, lane, lanes, parts, *refs):
-    l4_ref, out_hbm, (v_ref, sem) = refs[n_in], refs[-3], refs[-2:]
+    l4_ref, v_hbm, out_hbm, v_ref, in_sem, out_sem = refs[n_in:]
+    size = n // parts
+
+    def part(x):
+        return pl.ds(x * size, size), pl.ds(a0, 8), pl.ds(lane, lanes)
+
+    loads = [pltpu.make_async_copy(v_hbm.at[part(x)], v_ref.at[part(x)[0]], in_sem.at[x]) for x in range(parts)]
+    for copy in loads:
+        copy.start()
     rhs = jnp.concatenate([r[...].reshape(-1, lanes) for r in refs[:n_in]], axis=0)
-    size = n // parts
     copies = []
     for x in range(parts):
-        i = pl.ds(x * size, size)
-        v_ref[i] = dot(l4_ref[pl.ds(8 * size * x, 8 * size)], rhs).reshape(size, 8, lanes)
-        copies.append(pltpu.make_async_copy(
-            v_ref.at[i], out_hbm.at[i, pl.ds(a0, 8), pl.ds(lane, lanes)], sem.at[x]))
+        i = part(x)[0]
+        v = dot(l4_ref[pl.ds(8 * size * x, 8 * size)], rhs).reshape(size, 8, lanes)
+        loads[x].wait()
+        v_ref[i] = v_ref[i] + v
+        copies.append(pltpu.make_async_copy(v_ref.at[i], out_hbm.at[part(x)], out_sem.at[x]))
         copies[-1].start()
     for copy in copies:
         copy.wait()
@@ -250,39 +265,48 @@
             for x, k in enumerate(DIAGONAL):
                 moved[k, t] = lax.ppermute(
                     tiles[x * len(TILES) + t], 'dev', [(i, i ^ k) for i in range(n_dev)])
-        l4 = pl.pallas_call(
-            functools.partial(last_kernel, n, rows),
+        spans = ((0, n_dev), (0, n_got), (n_got, n_dev))
+        widths = [8 * rows * (k1 - k0) for k0, k1 in spans]
+        l4, l4_direct, l4_diagonal = pl.pallas_call(
+            functools.partial(last_kernel, n, rows, spans),
             in_specs=[smem, vmem, hbm],
-            out_specs=vmem,
-            out_shape=jax.ShapeDtypeStruct(square, BF16),
+            out_specs=[vmem] * 3,
+            out_shape=[jax.ShapeDtypeStruct((8 * n, w), BF16) for w in widths],
             name='last',
         )(me_arr, coeffs, got[0])
 
+        def spec(size, a0, lane, lanes):
+            return pl.BlockSpec(tuple(map(pl.Element, (size, 8, lanes))),
+                                lambda i: (0, pl.multiple_of(a0 + 8 * i, 8), lane))
+
+        parts = 3
         out = None
-        for t_i, (a0, size, lane, lanes) in enumerate(TILES):
+        for t_i, (a0, size, lane, lanes) in ((None, (TAIL, n - TAIL, 0, wide)), *enumerate(TILES)):
             ins, specs = [], []
             for k in range(n_dev):
-                block, at = (moved[k, t_i], (0, 0)) if (k, t_i) in moved else (got[k], (a0, lane))
-                ins.append(block)
-                specs.append(pl.BlockSpec((pl.Element(rows), pl.Element(8), pl.Element(lanes)), lambda i, at=at: (0, pl.multiple_of(at[0] + 8 * i, 8), at[1])))
+                if (k, t_i) in moved:
+                    ins.append(moved[k, t_i])
+                    specs.append(spec(rows, 0, 0, lanes))
+                elif k < n_got and (t_i is None or a0 < TAIL):
+                    ins.append(got[k])
+                    specs.append(spec(rows, a0, lane, lanes))
             n_in = len(ins)
-            ins.append(l4)
-            specs.append(const(square))
+            tail = t_i is not None and a0 >= TAIL
+            ins.append(l4_direct if t_i is None else l4_diagonal if tail else l4)
+            specs.append(const(ins[-1].shape))
             if out is not None:
                 ins.append(out)
                 specs.append(hbm)
-            alone = size == 8
             out = pl.pallas_call(
-                functools.partial(tail_kernel, n, n_in, a0, lane, lanes, 3) if alone
+                functools.partial(tail_kernel, n, n_in, a0, lane, lanes, parts) if tail
                 else functools.partial(out_kernel, n_in, lanes),
                 grid=(size // 8,),
                 in_specs=specs,
-                out_specs=hbm if alone else pl.BlockSpec(
-                    (pl.Element(n), pl.Element(8), pl.Element(lanes)),
-                    lambda i, at=(a0, lane): (0, pl.multiple_of(at[0] + 8 * i, 8), at[1])),
+                out_specs=hbm if tail else spec(n, a0, lane, lanes),
                 out_shape=jax.ShapeDtypeStruct((n, n, wide), F32),
-                input_output_aliases={} if t_i == 0 else {len(ins) - 1: 0},
-                scratch_shapes=[pltpu.VMEM((n, 8, lanes), F32), pltpu.SemaphoreType.DMA((3,))] * alone,
+                input_output_aliases={} if t_i is None else {len(ins) - 1: 0},
+                scratch_shapes=[pltpu.VMEM((n, 8, lanes), F32), pltpu.SemaphoreType.DMA((parts,)),
+                                pltpu.SemaphoreType.DMA((parts,))] * tail,
                 compiler_params=pltpu.CompilerParams(vmem_limit_bytes=67043328),
                 name='out',
             )(*ins)

time: 283 us -> 292 us (1.032)
  Pallas kernels: 168 us -> 176 us
    pallas_call x7 -> x8, Pallas kernels: 46.6 us -> 54.2 us  [the longest x7 51.3 us: transform(): pl.pallas_call(functools.partial(tail_kernel, n, n_in, a0, lane, lanes, p...]
  transfers between devices with their start and end apart: 12 -> 12, of which waited for: 3 -> 3; matrix products, arithmetic and copies ran while one was open for 0% -> 0% of each run, Pallas kernels for 15% -> 17%
where the time goes in v3:
time: 292 us; the launch traced here: 291 us
  Pallas kernels  176 us (60%)
  waiting for transfers between devices  99.5 us (34%)
  starting transfers between devices  15.2 us (5%)
    pallas_call x1, Pallas kernels, transform(): pl.pallas_call(functools.partial(exchange_kernel, n, n_dev, rows), in_spe...  122 us
    ppermute x12, waiting for transfers between devices, transform(): lax.ppermute(tiles[x * len(TILES) + t], 'dev', [(i, i ^ k) for i in range...  99.5 us
    pallas_call x7, Pallas kernels, transform(): pl.pallas_call(functools.partial(tail_kernel, n, n_in, a0, lane, lanes, p...  51.3 us
    ppermute x12, starting transfers between devices, transform(): lax.ppermute(tiles[x * len(TILES) + t], 'dev', [(i, i ^ k) for i in range...  15.2 us
  transfers between devices with their start and end apart: 12, of which 3 were waited for; matrix products, arithmetic and copies ran while one was open for 0% of the time, Pallas kernels for 17%

profile of v3, /device:TPU:0, one launch (start us, length us, event | category | flops | bytes accessed | tf_op | source)
XLA Modules:
  0.0 290.9 jit_solution(13736316815286016446)
XLA Ops:
  0.0 121.8 %exchange.1 = (bf16[12,96,1152]{2,1,0:T(8,128)(2,1)}, bf16[12,96,1152]{2,1,0:T(8,128)(2,1)}, bf16[12,96,1152]{2,1,0:T(8,128)(2,1)}, bf16[12,96,1152]{2,1,0:T(8,1...) custom-call(bf16[12,96,96,96]{3,2,1,0:T(8,128)(2,1)} %a_hbm.1, ...), custom_call_target="tpu_custom_call" | custom-call | tf_op jit(solution)/shard_map/exchange/pallas_call | solution.py:247
  121.8 1.5 collective-permute-start.10
  123.3 1.5 collective-permute-start.11
  124.8 1.4 collective-permute-start.4
  126.2 1.5 collective-permute-start.8
  127.7 0.6 collective-permute-start.9
  128.3 59.9 %collective-permute-done.4.refs_6_ = bf16[12,8,1152]{2,1,0:T(8,128)(2,1)} collective-permute-done((bf16[12,8,1152]{2,1,0:T(8,128)(2,1)}, bf16[12,8,1152]{2,1,0:T(8,128)(2,1)}, u32[]{:S(2)}, u32[]{:S(2)}) %collective-permute-start.4) | collective-permute-done | bytes 221216 | tf_op jit(solution)/shard_map/ppermute | solution.py:266
  188.2 1.4 collective-permute-start.6
  189.7 31.5 %collective-permute-done.6.refs_6_ = bf16[12,8,1152]{2,1,0:T(8,128)(2,1)} collective-permute-done((bf16[12,8,1152]{2,1,0:T(8,128)(2,1)}, bf16[12,8,1152]{2,1,0:T(8,128)(2,1)}, u32[]{:S(2)}, u32[]{:S(2)}) %collective-permute-start.6) | collective-permute-done | bytes 221216 | tf_op jit(solution)/shard_map/ppermute | solution.py:266
  221.1 0.9 collective-permute-start.7
  222.0 8.1 %collective-permute-done.7.refs_7_ = bf16[12,8,1152]{2,1,0:T(8,128)(2,1)} collective-permute-done((bf16[12,8,1152]{2,1,0:T(8,128)(2,1)}, bf16[12,8,1152]{2,1,0:T(8,128)(2,1)}, u32[]{:S(2)}, u32[]{:S(2)}) %collective-permute-start.7) | collective-permute-done | bytes 221216 | tf_op jit(solution)/shard_map/ppermute | solution.py:266
  230.1 1.2 collective-permute-start.5
  231.2 1.5 collective-permute-start.2
  232.7 1.2 collective-permute-start.3
  233.9 1.5 collective-permute-start
  235.4 1.2 collective-permute-start.1
  236.5 2.9 %last.1 = (bf16[768,768]{1,0:T(8,128)(2,1)}, bf16[768,576]{1,0:T(8,128)(2,1)}, bf16[768,192]{1,0:T(8,128)(2,1)}) custom-call(s32[1]{0:T(128)} %bitcast.me_ref, bf16[96,96]{1,0:T(8,128)(2,1)} %c_ref.3, bf16[12,96,1152]{2,1,0:T(8,128)(2,1)} %get-tuple-element.28.after_ref.refs_0_), custom_call_target="tpu_custom_call" | custom-call | tf_op jit(solution)/shard_map/last/pallas_call | solution.py:270
  239.5 5.2 %out.7.refs_9_ = f32[96,96,1152]{2,1,0:T(8,128)} custom-call(bf16[12,96,1152]{2,1,0:T(8,128)(2,1)} %get-tuple-element.28.after_ref.refs_0_, bf16[12,96,1152]{2,1,0:T(8,128)(2,1)} %get-tuple-element.32.refs_1_, bf16[12,96,1152]{2,1,0:T(8,128)(2,1)} %get-tuple-element.33.refs_2_, bf16[12,96,1152]{2,1,0:T(8,128)(2,1)} %get-tuple-element.34.refs_3_, ...), custom_call_target="tpu_custom_call" | custom-call | tf_op jit(solution)/shard_map/out/pallas_call | solution.py:300
  244.6 17.2 %out.8.refs_9_ = f32[96,96,1152]{2,1,0:T(8,128)} custom-call(bf16[12,96,1152]{2,1,0:T(8,128)(2,1)} %get-tuple-element.28.after_ref.refs_0_, bf16[12,96,1152]{2,1,0:T(8,128)(2,1)} %get-tuple-element.32.refs_1_, bf16[12,96,1152]{2,1,0:T(8,128)(2,1)} %get-tuple-element.33.refs_2_, ...), custom_call_target="tpu_custom_call", output_to_operand_aliasing={{}: (9, {})} | custom-call | tf_op jit(solution)/shard_map/out/pallas_call | solution.py:300
  261.8 10.5 %out.9.refs_9_ = f32[96,96,1152]{2,1,0:T(8,128)} custom-call(bf16[12,96,1152]{2,1,0:T(8,128)(2,1)} %get-tuple-element.28.after_ref.refs_0_, bf16[12,96,1152]{2,1,0:T(8,128)(2,1)} %get-tuple-element.32.refs_1_, bf16[12,96,1152]{2,1,0:T(8,128)(2,1)} %get-tuple-element.33.refs_2_, ...), custom_call_target="tpu_custom_call", output_to_operand_aliasing={{}: (9, {})} | custom-call | tf_op jit(solution)/shard_map/out/pallas_call | solution.py:300
  272.4 5.4 %out.10.refs_9_ = f32[96,96,1152]{2,1,0:T(8,128)} custom-call(bf16[12,96,1152]{2,1,0:T(8,128)(2,1)} %get-tuple-element.28.after_ref.refs_0_, bf16[12,96,1152]{2,1,0:T(8,128)(2,1)} %get-tuple-element.32.refs_1_, bf16[12,96,1152]{2,1,0:T(8,128)(2,1)} %get-tuple-element.33.refs_2_, ...), custom_call_target="tpu_custom_call", output_to_operand_aliasing={{}: (9, {})} | custom-call | tf_op jit(solution)/shard_map/out/pallas_call | solution.py:300
  277.8 5.4 %out.11.refs_3_ = f32[96,96,1152]{2,1,0:T(8,128)} custom-call(bf16[12,96,1152]{2,1,0:T(8,128)(2,1)} %get-tuple-element.28.after_ref.refs_0_, bf16[12,96,1152]{2,1,0:T(8,128)(2,1)} %get-tuple-element.32.refs_1_, bf16[12,96,1152]{2,1,0:T(8,128)(2,1)} %get-tuple-element.33.refs_2_, ...), custom_call_target="tpu_custom_call", output_to_operand_aliasing={{}: (9, {})} | custom-call | tf_op jit(solution)/shard_map/out/pallas_call | solution.py:300
  283.3 4.1 %out.12.refs_3_ = f32[96,96,1152]{2,1,0:T(8,128)} custom-call(bf16[12,8,768]{2,1,0:T(8,128)(2,1)} %collective-permute-done.2.refs_0_, bf16[12,8,768]{2,1,0:T(8,128)(2,1)} %collective-permute-done.3.refs_1_, bf16[768,192]{1,0:T(8,128)(2,1)} %get-tuple-element.29.refs_2_, f32[96,96,1152]{2,1,0:T(8,128)} %out.11.refs_3_), custom_call_target="tpu_custom_call", output_to_operand_aliasing={{}: (3, {})} | custom-call | tf_op jit(solution)/shard_map/out/pallas_call | solution.py:300
  287.4 3.4 %out.13 = f32[96,96,1152]{2,1,0:T(8,128)} custom-call(bf16[12,8,384]{2,1,0:T(8,128)(2,1)} %collective-permute-done.refs_0_, bf16[12,8,384]{2,1,0:T(8,128)(2,1)} %collective-permute-done.1.refs_1_, bf16[768,192]{1,0:T(8,128)(2,1)} %get-tuple-element.29.refs_2_, f32[96,96,1152]{2,1,0:T(8,128)} %out.12.refs_3_), custom_call_target="tpu_custom_call", output_to_operand_aliasing={{}: (3, {})} | custom-call | tf_op jit(solution)/shard_map/out/pallas_call | solution.py:300
  (9 shorter events, 0.0 us)
Async XLA Ops:
  121.8 112.1 %collective-permute-start.10 = (bf16[12,48,1152]{2,1,0:T(8,128)(2,1)}, bf16[12,48,1152]{2,1,0:T(8,128)(2,1)}, u32[]{:S(2)}, u32[]{:S(2)}) collective-permute-start(bf16[12,48,1152]{2,1,0:T(8,128)(2,1)} %get-tuple-element.44), channel_id=1, source_target_pairs={{0,6},{1,7},{2,4},{3,5},{4,2},{5,3},{6,0},{7,1},{8,14},{9,15},{10,... | collective-permute-start | bytes 3981320 | tf_op jit(solution)/shard_map/ppermute | solution.py:266
  123.3 112.1 %collective-permute-start.11 = (bf16[12,48,1152]{2,1,0:T(8,128)(2,1)}, bf16[12,48,1152]{2,1,0:T(8,128)(2,1)}, u32[]{:S(2)}, u32[]{:S(2)}) collective-permute-start(bf16[12,48,1152]{2,1,0:T(8,128)(2,1)} %get-tuple-element.45), channel_id=1, source_target_pairs={{0,7},{1,6},{2,5},{3,4},{4,3},{5,2},{6,1},{7,0},{8,15},{9,14},{10,... | collective-permute-start | bytes 3981320 | tf_op jit(solution)/shard_map/ppermute | solution.py:266
  124.8 63.5 %collective-permute-start.4 = (bf16[12,8,1152]{2,1,0:T(8,128)(2,1)}, bf16[12,8,1152]{2,1,0:T(8,128)(2,1)}, u32[]{:S(2)}, u32[]{:S(2)}) collective-permute-start(bf16[12,8,1152]{2,1,0:T(8,128)(2,1)} %get-tuple-element.37), channel_id=1, source_target_pairs={{0,6},{1,7},{2,4},{3,5},{4,2},{5,3},{6,0},{7,1},{8,14},{9,15},{10,... | collective-permute-start | bytes 663560 | tf_op jit(solution)/shard_map/ppermute | solution.py:266
  126.2 105.0 %collective-permute-start.8 = (bf16[12,24,1152]{2,1,0:T(8,128)(2,1)}, bf16[12,24,1152]{2,1,0:T(8,128)(2,1)}, u32[]{:S(2)}, u32[]{:S(2)}) collective-permute-start(bf16[12,24,1152]{2,1,0:T(8,128)(2,1)} %get-tuple-element.42), channel_id=1, source_target_pairs={{0,6},{1,7},{2,4},{3,5},{4,2},{5,3},{6,0},{7,1},{8,14},{9,15},{10,... | collective-permute-start | bytes 1990664 | tf_op jit(solution)/shard_map/ppermute | solution.py:266
  127.7 105.0 %collective-permute-start.9 = (bf16[12,24,1152]{2,1,0:T(8,128)(2,1)}, bf16[12,24,1152]{2,1,0:T(8,128)(2,1)}, u32[]{:S(2)}, u32[]{:S(2)}) collective-permute-start(bf16[12,24,1152]{2,1,0:T(8,128)(2,1)} %get-tuple-element.43), channel_id=1, source_target_pairs={{0,7},{1,6},{2,5},{3,4},{4,3},{5,2},{6,1},{7,0},{8,15},{9,14},{10,... | collective-permute-start | bytes 1990664 | tf_op jit(solution)/shard_map/ppermute | solution.py:266
  188.2 32.9 %collective-permute-start.6 = (bf16[12,8,1152]{2,1,0:T(8,128)(2,1)}, bf16[12,8,1152]{2,1,0:T(8,128)(2,1)}, u32[]{:S(2)}, u32[]{:S(2)}) collective-permute-start(bf16[12,8,1152]{2,1,0:T(8,128)(2,1)} %get-tuple-element.40), channel_id=1, source_target_pairs={{0,6},{1,7},{2,4},{3,5},{4,2},{5,3},{6,0},{7,1},{8,14},{9,15},{10,... | collective-permute-start | bytes 663560 | tf_op jit(solution)/shard_map/ppermute | solution.py:266
  221.1 8.9 %collective-permute-start.7 = (bf16[12,8,1152]{2,1,0:T(8,128)(2,1)}, bf16[12,8,1152]{2,1,0:T(8,128)(2,1)}, u32[]{:S(2)}, u32[]{:S(2)}) collective-permute-start(bf16[12,8,1152]{2,1,0:T(8,128)(2,1)} %get-tuple-element.41), channel_id=1, source_target_pairs={{0,7},{1,6},{2,5},{3,4},{4,3},{5,2},{6,1},{7,0},{8,15},{9,14},{10,... | collective-permute-start | bytes 663560 | tf_op jit(solution)/shard_map/ppermute | solution.py:266
  230.1 47.7 %collective-permute-start.5 = (bf16[12,8,1152]{2,1,0:T(8,128)(2,1)}, bf16[12,8,1152]{2,1,0:T(8,128)(2,1)}, u32[]{:S(2)}, u32[]{:S(2)}) collective-permute-start(bf16[12,8,1152]{2,1,0:T(8,128)(2,1)} %get-tuple-element.38), channel_id=1, source_target_pairs={{0,7},{1,6},{2,5},{3,4},{4,3},{5,2},{6,1},{7,0},{8,15},{9,14},{10,... | collective-permute-start | bytes 663560 | tf_op jit(solution)/shard_map/ppermute | solution.py:266
  231.2 52.0 %collective-permute-start.2 = (bf16[12,8,768]{2,1,0:T(8,128)(2,1)}, bf16[12,8,768]{2,1,0:T(8,128)(2,1)}, u32[]{:S(2)}, u32[]{:S(2)}) collective-permute-start(bf16[12,8,768]{2,1,0:T(8,128)(2,1)} %get-tuple-element.30), channel_id=1, source_target_pairs={{0,6},{1,7},{2,4},{3,5},{4,2},{5,3},{6,0},{7,1},{8,14},{9,15},{10,... | collective-permute-start | bytes 442376 | tf_op jit(solution)/shard_map/ppermute | solution.py:266
  232.7 50.5 %collective-permute-start.3 = (bf16[12,8,768]{2,1,0:T(8,128)(2,1)}, bf16[12,8,768]{2,1,0:T(8,128)(2,1)}, u32[]{:S(2)}, u32[]{:S(2)}) collective-permute-start(bf16[12,8,768]{2,1,0:T(8,128)(2,1)} %get-tuple-element.31), channel_id=1, source_target_pairs={{0,7},{1,6},{2,5},{3,4},{4,3},{5,2},{6,1},{7,0},{8,15},{9,14},{10,... | collective-permute-start | bytes 442376 | tf_op jit(solution)/shard_map/ppermute | solution.py:266
  233.9 53.5 %collective-permute-start = (bf16[12,8,384]{2,1,0:T(8,128)(2,1)}, bf16[12,8,384]{2,1,0:T(8,128)(2,1)}, u32[]{:S(2)}, u32[]{:S(2)}) collective-permute-start(bf16[12,8,384]{2,1,0:T(8,128)(2,1)} %get-tuple-element.26), channel_id=1, source_target_pairs={{0,6},{1,7},{2,4},{3,5},{4,2},{5,3},{6,0},{7,1},{8,14},{9,15},{10,... | collective-permute-start | bytes 221192 | tf_op jit(solution)/shard_map/ppermute | solution.py:266
  235.4 52.0 %collective-permute-start.1 = (bf16[12,8,384]{2,1,0:T(8,128)(2,1)}, bf16[12,8,384]{2,1,0:T(8,128)(2,1)}, u32[]{:S(2)}, u32[]{:S(2)}) collective-permute-start(bf16[12,8,384]{2,1,0:T(8,128)(2,1)} %get-tuple-element.27), channel_id=1, source_target_pairs={{0,7},{1,6},{2,5},{3,4},{4,3},{5,2},{6,1},{7,0},{8,15},{9,14},{10,... | collective-permute-start | bytes 221192 | tf_op jit(solution)/shard_map/ppermute | solution.py:266

commit v4 on v2

--- a/solution.py
+++ b/solution.py
@@ -33,18 +33,20 @@
     return lax.dot_general(c, eye, (((0,), (0,)), ((), ())), preferred_element_type=F32).astype(BF16)
 
 
-def build_first(n, c_ref, l1_ref, r2_ref, ct_ref):
+def build_small(n, c_ref, r2_ref, ct_ref):
     c = c_ref[...]
-    ct = transposed(c, n)
-    ct_ref[...] = ct
-    tall = dot(pick((8 * n, n), lambda i, j: i // 8 == j), ct).astype(BF16)
-    wide = dot(tall, pick((n, 8 * n), lambda i, j: j % n == i))
-    keep = one_hot((8 * n, 8 * n), lambda i, j: i % 8 == j // n)
-    l1_ref[...] = jnp.where(keep, wide, 0.0).astype(BF16)
+    ct_ref[...] = transposed(c, n)
     tall = dot(pick((512, n), lambda i, j: i % 128 == j), c).astype(BF16)
     wide = dot(tall, pick((n, 4 * n), lambda i, j: j % n == i))
     keep = one_hot((512, 4 * n), lambda i, j: i // 128 == j // n)
     r2_ref[...] = jnp.where(keep, wide, 0.0).astype(BF16)
+
+
+def build_l1(n, first, size, ct_ref, l1_ref):
+    tall = dot(pick((8 * size, n), lambda i, j: i // 8 + first == j), ct_ref[...]).astype(BF16)
+    wide = dot(tall, pick((n, 8 * n), lambda i, j: j % n == i))
+    keep = one_hot((8 * size, 8 * n), lambda i, j: i % 8 == j // n)
+    l1_ref[pl.ds(pl.multiple_of(first * 8, 8 * size), 8 * size)] = jnp.where(keep, wide, 0.0).astype(BF16)
 
 
 def last_kernel(n, rows, me_ref, c_ref, after_ref, l4_ref):
@@ -90,8 +92,9 @@
 
     for g in range(n // 16):
         chunk(g).start()
-    fetch(1).start()
-    build_first(n, c_ref, l1_ref, r2_ref, ct_ref)
+    build_small(n, c_ref, r2_ref, ct_ref)
+    for k in DIRECT[:2]:
+        build_l1(n, flipped(me, k) * nj, nj, ct_ref, l1_ref)
     zero = jnp.zeros((8 * n, 128 - n), BF16)
 
     def remote(k, src, dst):
@@ -155,6 +158,8 @@
         send(before, i)
 
     some(DIRECT[:2], 0, 0, True)
+    fetch(1).start()
+    build_l1(n, 0, n, ct_ref, l1_ref)
     some((*DIRECT[2:], 0, *DIAGONAL), 0, 0, False)
 
     def row(i, carry):
@@ -195,16 +200,30 @@
     out_ref[...] = dot(l4_ref[...], rhs).reshape(out_ref.shape)
 
 
-def tail_kernel(n, n_in, a0, lane, lanes, parts, *refs):
-    l4_ref, out_hbm, (v_ref, sem) = refs[n_in], refs[-3], refs[-2:]
-    rhs = jnp.concatenate([r[...].reshape(-1, lanes) for r in refs[:n_in]], axis=0)
+def tail_kernel(n, rows, at, a0, lane, lanes, parts, *refs):
+    blocks, l4_hbm = refs[:len(at)], refs[len(at)]
+    out_hbm, rhs_ref, l4_ref, v_ref, in_sem, l4_sem, out_sem = refs[-7:]
     size = n // parts
+    loads = []
+    for x, (block, (a, first)) in enumerate(zip(blocks, at)):
+        loads.append(pltpu.make_async_copy(
+            block.at[:, pl.ds(a, 8), pl.ds(first, lanes)], rhs_ref.at[pl.ds(x * rows, rows)], in_sem.at[x]))
+    l4_loads = []
+    for x in range(parts):
+        i = pl.ds(8 * size * x, 8 * size)
+        l4_loads.append(pltpu.make_async_copy(l4_hbm.at[i], l4_ref.at[i], l4_sem.at[x]))
+    for copy in (*loads, *l4_loads):
+        copy.start()
+    for copy in loads:
+        copy.wait()
+    rhs = rhs_ref[...].reshape(8 * n, lanes)
     copies = []
     for x in range(parts):
         i = pl.ds(x * size, size)
+        l4_loads[x].wait()
         v_ref[i] = dot(l4_ref[pl.ds(8 * size * x, 8 * size)], rhs).reshape(size, 8, lanes)
         copies.append(pltpu.make_async_copy(
-            v_ref.at[i], out_hbm.at[i, pl.ds(a0, 8), pl.ds(lane, lanes)], sem.at[x]))
+            v_ref.at[i], out_hbm.at[i, pl.ds(a0, 8), pl.ds(lane, lanes)], out_sem.at[x]))
         copies[-1].start()
     for copy in copies:
         copy.wait()
@@ -260,10 +279,11 @@
 
         out = None
         for t_i, (a0, size, lane, lanes) in enumerate(TILES):
-            ins, specs = [], []
+            ins, specs, ats = [], [], []
             for k in range(n_dev):
                 block, at = (moved[k, t_i], (0, 0)) if (k, t_i) in moved else (got[k], (a0, lane))
                 ins.append(block)
+                ats.append(at)
                 specs.append(pl.BlockSpec((pl.Element(rows), pl.Element(8), pl.Element(lanes)), lambda i, at=at: (0, pl.multiple_of(at[0] + 8 * i, 8), at[1])))
             n_in = len(ins)
             ins.append(l4)
@@ -271,9 +291,11 @@
             if out is not None:
                 ins.append(out)
                 specs.append(hbm)
-            alone = size == 8
+            alone, parts = size == 8, 3
+            if alone:
+                specs = [hbm] * len(specs)
             out = pl.pallas_call(
-                functools.partial(tail_kernel, n, n_in, a0, lane, lanes, 3) if alone
+                functools.partial(tail_kernel, n, rows, ats, a0, lane, lanes, parts) if alone
                 else functools.partial(out_kernel, n_in, lanes),
                 grid=(size // 8,),
                 in_specs=specs,
@@ -282,7 +304,10 @@
                     lambda i, at=(a0, lane): (0, pl.multiple_of(at[0] + 8 * i, 8), at[1])),
                 out_shape=jax.ShapeDtypeStruct((n, n, wide), F32),
                 input_output_aliases={} if t_i == 0 else {len(ins) - 1: 0},
-                scratch_shapes=[pltpu.VMEM((n, 8, lanes), F32), pltpu.SemaphoreType.DMA((3,))] * alone,
+                scratch_shapes=[
+                    pltpu.VMEM((n, 8, lanes), BF16), pltpu.VMEM(square, BF16), pltpu.VMEM((n, 8, lanes), F32),
+                    pltpu.SemaphoreType.DMA((n_dev,)), pltpu.SemaphoreType.DMA((parts,)),
+                    pltpu.SemaphoreType.DMA((parts,))] * alone,
                 compiler_params=pltpu.CompilerParams(vmem_limit_bytes=67043328),
                 name='out',
             )(*ins)

time: 283 us -> 285 us (level)
  transfers between devices with their start and end apart: 12 -> 12, of which waited for: 3 -> 3; matrix products, arithmetic and copies ran while one was open for 0% -> 0% of each run, Pallas kernels for 15% -> 16%
where the time goes in v4:
time: 285 us
  Pallas kernels  170 us (60%)
  waiting for transfers between devices  99.5 us (35%)
  starting transfers between devices  15.2 us (5%)
    pallas_call x1, Pallas kernels, transform(): pl.pallas_call(functools.partial(exchange_kernel, n, n_dev, rows), in_spe...  122 us
    ppermute x12, waiting for transfers between devices, transform(): lax.ppermute(tiles[x * len(TILES) + t], 'dev', [(i, i ^ k) for i in range...  99.5 us
    pallas_call x6, Pallas kernels, transform(): pl.pallas_call(functools.partial(tail_kernel, n, rows, ats, a0, lane, lan...  45.6 us
    ppermute x12, starting transfers between devices, transform(): lax.ppermute(tiles[x * len(TILES) + t], 'dev', [(i, i ^ k) for i in range...  15.2 us
  transfers between devices with their start and end apart: 12, of which 3 were waited for; matrix products, arithmetic and copies ran while one was open for 0% of the time, Pallas kernels for 16%

profile of v4, /device:TPU:0, one launch (start us, length us, event | category | flops | bytes accessed | tf_op | source)
XLA Modules:
  0.0 284.9 jit_solution(16075905639272769197)
XLA Ops:
  0.0 121.8 %exchange.1 = (bf16[12,96,1152]{2,1,0:T(8,128)(2,1)}, bf16[12,96,1152]{2,1,0:T(8,128)(2,1)}, bf16[12,96,1152]{2,1,0:T(8,128)(2,1)}, bf16[12,96,1152]{2,1,0:T(8,1...) custom-call(bf16[12,96,96,96]{3,2,1,0:T(8,128)(2,1)} %a_hbm.1, ...), custom_call_target="tpu_custom_call" | custom-call | tf_op jit(solution)/shard_map/exchange/pallas_call | solution.py:251
  121.8 1.5 collective-permute-start.10
  123.3 1.5 collective-permute-start.11
  124.8 1.4 collective-permute-start.4
  126.2 1.5 collective-permute-start.8
  127.7 0.6 collective-permute-start.9
  128.3 59.9 %collective-permute-done.4.refs_6_ = bf16[12,8,1152]{2,1,0:T(8,128)(2,1)} collective-permute-done((bf16[12,8,1152]{2,1,0:T(8,128)(2,1)}, bf16[12,8,1152]{2,1,0:T(8,128)(2,1)}, u32[]{:S(2)}, u32[]{:S(2)}) %collective-permute-start.4) | collective-permute-done | bytes 221216 | tf_op jit(solution)/shard_map/ppermute | solution.py:270
  188.2 1.4 collective-permute-start.6
  189.7 31.5 %collective-permute-done.6.refs_6_ = bf16[12,8,1152]{2,1,0:T(8,128)(2,1)} collective-permute-done((bf16[12,8,1152]{2,1,0:T(8,128)(2,1)}, bf16[12,8,1152]{2,1,0:T(8,128)(2,1)}, u32[]{:S(2)}, u32[]{:S(2)}) %collective-permute-start.6) | collective-permute-done | bytes 221216 | tf_op jit(solution)/shard_map/ppermute | solution.py:270
  221.1 0.9 collective-permute-start.7
  222.0 8.1 %collective-permute-done.7.refs_7_ = bf16[12,8,1152]{2,1,0:T(8,128)(2,1)} collective-permute-done((bf16[12,8,1152]{2,1,0:T(8,128)(2,1)}, bf16[12,8,1152]{2,1,0:T(8,128)(2,1)}, u32[]{:S(2)}, u32[]{:S(2)}) %collective-permute-start.7) | collective-permute-done | bytes 221216 | tf_op jit(solution)/shard_map/ppermute | solution.py:270
  230.1 1.2 collective-permute-start.5
  231.2 0.0 collective-permute-done.8.refs_6_
  231.2 1.5 collective-permute-start.2
  232.7 1.2 collective-permute-start.3
  233.9 1.5 collective-permute-start
  235.4 1.2 collective-permute-start.1
  236.5 2.5 last.1.refs_8_
  239.1 17.2 %out.6.refs_9_ = f32[96,96,1152]{2,1,0:T(8,128)} custom-call(bf16[12,96,1152]{2,1,0:T(8,128)(2,1)} %get-tuple-element.23.after_ref.refs_0_, bf16[12,96,1152]{2,1,0:T(8,128)(2,1)} %get-tuple-element.24.refs_1_, bf16[12,96,1152]{2,1,0:T(8,128)(2,1)} %get-tuple-element.25.refs_2_, bf16[12,96,1152]{2,1,0:T(8,128)(2,1)} %get-tuple-element.26.refs_3_, ...), custom_call_target="tpu_custom_call" | custom-call | tf_op jit(solution)/shard_map/out/pallas_call | solution.py:297
  256.3 10.5 %out.7.refs_9_ = f32[96,96,1152]{2,1,0:T(8,128)} custom-call(bf16[12,96,1152]{2,1,0:T(8,128)(2,1)} %get-tuple-element.23.after_ref.refs_0_, bf16[12,96,1152]{2,1,0:T(8,128)(2,1)} %get-tuple-element.24.refs_1_, bf16[12,96,1152]{2,1,0:T(8,128)(2,1)} %get-tuple-element.25.refs_2_, ...), custom_call_target="tpu_custom_call", output_to_operand_aliasing={{}: (9, {})} | custom-call | tf_op jit(solution)/shard_map/out/pallas_call | solution.py:297
  266.8 5.1 %out.8.refs_9_ = f32[96,96,1152]{2,1,0:T(8,128)} custom-call(bf16[12,96,1152]{2,1,0:T(8,128)(2,1)} %get-tuple-element.23.after_ref.refs_0_, bf16[12,96,1152]{2,1,0:T(8,128)(2,1)} %get-tuple-element.24.refs_1_, bf16[12,96,1152]{2,1,0:T(8,128)(2,1)} %get-tuple-element.25.refs_2_, ...), custom_call_target="tpu_custom_call", output_to_operand_aliasing={{}: (9, {})} | custom-call | tf_op jit(solution)/shard_map/out/pallas_call | solution.py:297
  272.0 5.1 %out.9.refs_9_ = f32[96,96,1152]{2,1,0:T(8,128)} custom-call(bf16[12,96,1152]{2,1,0:T(8,128)(2,1)} %get-tuple-element.23.after_ref.refs_0_, bf16[12,96,1152]{2,1,0:T(8,128)(2,1)} %get-tuple-element.24.refs_1_, bf16[12,96,1152]{2,1,0:T(8,128)(2,1)} %get-tuple-element.25.refs_2_, ...), custom_call_target="tpu_custom_call", output_to_operand_aliasing={{}: (9, {})} | custom-call | tf_op jit(solution)/shard_map/out/pallas_call | solution.py:297
  277.1 4.1 %out.10.refs_9_ = f32[96,96,1152]{2,1,0:T(8,128)} custom-call(bf16[12,96,1152]{2,1,0:T(8,128)(2,1)} %get-tuple-element.23.after_ref.refs_0_, bf16[12,96,1152]{2,1,0:T(8,128)(2,1)} %get-tuple-element.24.refs_1_, bf16[12,96,1152]{2,1,0:T(8,128)(2,1)} %get-tuple-element.25.refs_2_, ...), custom_call_target="tpu_custom_call", output_to_operand_aliasing={{}: (9, {})} | custom-call | tf_op jit(solution)/shard_map/out/pallas_call | solution.py:297
  281.2 3.5 %out.11 = f32[96,96,1152]{2,1,0:T(8,128)} custom-call(bf16[12,96,1152]{2,1,0:T(8,128)(2,1)} %get-tuple-element.23.after_ref.refs_0_, bf16[12,96,1152]{2,1,0:T(8,128)(2,1)} %get-tuple-element.24.refs_1_, bf16[12,96,1152]{2,1,0:T(8,128)(2,1)} %get-tuple-element.25.refs_2_, ...), custom_call_target="tpu_custom_call", output_to_operand_aliasing={{}: (9, {})} | custom-call | tf_op jit(solution)/shard_map/out/pallas_call | solution.py:297
  (8 shorter events, 0.0 us)
Async XLA Ops:
  121.8 112.1 %collective-permute-start.10 = (bf16[12,48,1152]{2,1,0:T(8,128)(2,1)}, bf16[12,48,1152]{2,1,0:T(8,128)(2,1)}, u32[]{:S(2)}, u32[]{:S(2)}) collective-permute-start(bf16[12,48,1152]{2,1,0:T(8,128)(2,1)} %get-tuple-element.39), channel_id=1, source_target_pairs={{0,6},{1,7},{2,4},{3,5},{4,2},{5,3},{6,0},{7,1},{8,14},{9,15},{10,... | collective-permute-start | bytes 3981320 | tf_op jit(solution)/shard_map/ppermute | solution.py:270
  123.3 112.1 %collective-permute-start.11 = (bf16[12,48,1152]{2,1,0:T(8,128)(2,1)}, bf16[12,48,1152]{2,1,0:T(8,128)(2,1)}, u32[]{:S(2)}, u32[]{:S(2)}) collective-permute-start(bf16[12,48,1152]{2,1,0:T(8,128)(2,1)} %get-tuple-element.40), channel_id=1, source_target_pairs={{0,7},{1,6},{2,5},{3,4},{4,3},{5,2},{6,1},{7,0},{8,15},{9,14},{10,... | collective-permute-start | bytes 3981320 | tf_op jit(solution)/shard_map/ppermute | solution.py:270
  124.8 63.5 %collective-permute-start.4 = (bf16[12,8,1152]{2,1,0:T(8,128)(2,1)}, bf16[12,8,1152]{2,1,0:T(8,128)(2,1)}, u32[]{:S(2)}, u32[]{:S(2)}) collective-permute-start(bf16[12,8,1152]{2,1,0:T(8,128)(2,1)} %get-tuple-element.33), channel_id=1, source_target_pairs={{0,6},{1,7},{2,4},{3,5},{4,2},{5,3},{6,0},{7,1},{8,14},{9,15},{10,... | collective-permute-start | bytes 663560 | tf_op jit(solution)/shard_map/ppermute | solution.py:270
  126.2 105.0 %collective-permute-start.8 = (bf16[12,24,1152]{2,1,0:T(8,128)(2,1)}, bf16[12,24,1152]{2,1,0:T(8,128)(2,1)}, u32[]{:S(2)}, u32[]{:S(2)}) collective-permute-start(bf16[12,24,1152]{2,1,0:T(8,128)(2,1)} %get-tuple-element.37), channel_id=1, source_target_pairs={{0,6},{1,7},{2,4},{3,5},{4,2},{5,3},{6,0},{7,1},{8,14},{9,15},{10,... | collective-permute-start | bytes 1990664 | tf_op jit(solution)/shard_map/ppermute | solution.py:270
  127.7 105.0 %collective-permute-start.9 = (bf16[12,24,1152]{2,1,0:T(8,128)(2,1)}, bf16[12,24,1152]{2,1,0:T(8,128)(2,1)}, u32[]{:S(2)}, u32[]{:S(2)}) collective-permute-start(bf16[12,24,1152]{2,1,0:T(8,128)(2,1)} %get-tuple-element.38), channel_id=1, source_target_pairs={{0,7},{1,6},{2,5},{3,4},{4,3},{5,2},{6,1},{7,0},{8,15},{9,14},{10,... | collective-permute-start | bytes 1990664 | tf_op jit(solution)/shard_map/ppermute | solution.py:270
  188.2 32.9 %collective-permute-start.6 = (bf16[12,8,1152]{2,1,0:T(8,128)(2,1)}, bf16[12,8,1152]{2,1,0:T(8,128)(2,1)}, u32[]{:S(2)}, u32[]{:S(2)}) collective-permute-start(bf16[12,8,1152]{2,1,0:T(8,128)(2,1)} %get-tuple-element.35), channel_id=1, source_target_pairs={{0,6},{1,7},{2,4},{3,5},{4,2},{5,3},{6,0},{7,1},{8,14},{9,15},{10,... | collective-permute-start | bytes 663560 | tf_op jit(solution)/shard_map/ppermute | solution.py:270
  221.1 8.9 %collective-permute-start.7 = (bf16[12,8,1152]{2,1,0:T(8,128)(2,1)}, bf16[12,8,1152]{2,1,0:T(8,128)(2,1)}, u32[]{:S(2)}, u32[]{:S(2)}) collective-permute-start(bf16[12,8,1152]{2,1,0:T(8,128)(2,1)} %get-tuple-element.36), channel_id=1, source_target_pairs={{0,7},{1,6},{2,5},{3,4},{4,3},{5,2},{6,1},{7,0},{8,15},{9,14},{10,... | collective-permute-start | bytes 663560 | tf_op jit(solution)/shard_map/ppermute | solution.py:270
  230.1 41.9 %collective-permute-start.5 = (bf16[12,8,1152]{2,1,0:T(8,128)(2,1)}, bf16[12,8,1152]{2,1,0:T(8,128)(2,1)}, u32[]{:S(2)}, u32[]{:S(2)}) collective-permute-start(bf16[12,8,1152]{2,1,0:T(8,128)(2,1)} %get-tuple-element.34), channel_id=1, source_target_pairs={{0,7},{1,6},{2,5},{3,4},{4,3},{5,2},{6,1},{7,0},{8,15},{9,14},{10,... | collective-permute-start | bytes 663560 | tf_op jit(solution)/shard_map/ppermute | solution.py:270
  231.2 45.9 %collective-permute-start.2 = (bf16[12,8,640]{2,1,0:T(8,128)(2,1)}, bf16[12,8,640]{2,1,0:T(8,128)(2,1)}, u32[]{:S(2)}, u32[]{:S(2)}) collective-permute-start(bf16[12,8,640]{2,1,0:T(8,128)(2,1)} %get-tuple-element.31), channel_id=1, source_target_pairs={{0,6},{1,7},{2,4},{3,5},{4,2},{5,3},{6,0},{7,1},{8,14},{9,15},{10,... | collective-permute-start | bytes 368648 | tf_op jit(solution)/shard_map/ppermute | solution.py:270
  232.7 44.4 %collective-permute-start.3 = (bf16[12,8,640]{2,1,0:T(8,128)(2,1)}, bf16[12,8,640]{2,1,0:T(8,128)(2,1)}, u32[]{:S(2)}, u32[]{:S(2)}) collective-permute-start(bf16[12,8,640]{2,1,0:T(8,128)(2,1)} %get-tuple-element.32), channel_id=1, source_target_pairs={{0,7},{1,6},{2,5},{3,4},{4,3},{5,2},{6,1},{7,0},{8,15},{9,14},{10,... | collective-permute-start | bytes 368648 | tf_op jit(solution)/shard_map/ppermute | solution.py:270
  233.9 47.3 %collective-permute-start = (bf16[12,8,512]{2,1,0:T(8,128)(2,1)}, bf16[12,8,512]{2,1,0:T(8,128)(2,1)}, u32[]{:S(2)}, u32[]{:S(2)}) collective-permute-start(bf16[12,8,512]{2,1,0:T(8,128)(2,1)} %get-tuple-element.29), channel_id=1, source_target_pairs={{0,6},{1,7},{2,4},{3,5},{4,2},{5,3},{6,0},{7,1},{8,14},{9,15},{10,... | collective-permute-start | bytes 294920 | tf_op jit(solution)/shard_map/ppermute | solution.py:270
  235.4 45.8 %collective-permute-start.1 = (bf16[12,8,512]{2,1,0:T(8,128)(2,1)}, bf16[12,8,512]{2,1,0:T(8,128)(2,1)}, u32[]{:S(2)}, u32[]{:S(2)}) collective-permute-start(bf16[12,8,512]{2,1,0:T(8,128)(2,1)} %get-tuple-element.30), channel_id=1, source_target_pairs={{0,7},{1,6},{2,5},{3,4},{4,3},{5,2},{6,1},{7,0},{8,15},{9,14},{10,... | collective-permute-start | bytes 294920 | tf_op jit(solution)/shard_map/ppermute | solution.py:270

commit v5 on v2

--- a/solution.py
+++ b/solution.py
@@ -69,28 +69,31 @@
     return out
 
 
-def exchange_kernel(n, n_dev, rows, a_hbm, c_ref, *refs):
+def exchange_kernel(n, n_dev, rows, a_hbm, c_hbm, *refs):
     n_got, n_tile = n_dev - len(DIAGONAL), len(TILES)
     got, tiles = refs[:n_got], refs[n_got:n_got + len(DIAGONAL) * n_tile]
-    (a_buf, t1_ref, g_ref, l1_ref, r2_ref, ct_ref, a_sem, chunk_sem, own_sem, tile_sem, send_sem,
+    (a_buf, c_ref, t1_ref, g_ref, l1_ref, r2_ref, ct_ref, c_sem, a_sem, chunk_sem, own_sem, tile_sem, send_sem,
      recv_sem) = refs[n_got + len(tiles):]
     nj = n // n_dev
     me = lax.axis_index('dev')
+
+    def chunk(g):
+        q = pl.ds(g * 16, 16)
+        return pltpu.make_async_copy(a_hbm.at[0, q], a_buf.at[0, q], chunk_sem.at[g])
+
+    def fetch(i):
+        slot = lax.rem(i, 2)
+        return pltpu.make_async_copy(a_hbm.at[i], a_buf.at[slot], a_sem.at[slot])
+
+    c_copy = pltpu.make_async_copy(c_hbm, c_ref, c_sem)
+    c_copy.start()
+    for g in range(n // 16):
+        chunk(g).start()
+    fetch(1).start()
     barrier = pltpu.get_barrier_semaphore()
     for k in DIRECT:
         pl.semaphore_signal(barrier, inc=1, device_id={'dev': flipped(me, k)}, device_id_type=pl.DeviceIdType.MESH)
-
-    def chunk(g):
-        q = pl.ds(g * 16, 16)
-        return pltpu.make_async_copy(a_hbm.at[0, q], a_buf.at[0, q], chunk_sem.at[g])
-
-    def fetch(i):
-        slot = lax.rem(i, 2)
-        return pltpu.make_async_copy(a_hbm.at[i], a_buf.at[slot], a_sem.at[slot])
-
-    for g in range(n // 16):
-        chunk(g).start()
-    fetch(1).start()
+    c_copy.wait()
     build_first(n, c_ref, l1_ref, r2_ref, ct_ref)
     zero = jnp.zeros((8 * n, 128 - n), BF16)
 
@@ -133,26 +136,25 @@
         g_ref[k, i] = dot(ct_ref[...], h).astype(BF16)
 
     def some(ks, i, slot, wait):
-        def first(g, carry):
+        def first(pair, carry):
             if wait:
-                chunk(g).wait()
+                chunk(2 * pair).wait()
+                chunk(2 * pair + 1).wait()
             lhs = jnp.concatenate(
                 [l1_ref[pl.ds(pl.multiple_of(flipped(me, k) * 8 * nj, 8 * nj), 8 * nj)] for k in ks], axis=0)
-            q, t = step_one(slot, g, lhs)
-            for x, k in enumerate(ks):
-                t1_ref[pl.ds(flipped(me, k) * nj, nj), q, :] = t[x * nj:(x + 1) * nj]
+            for g in range(2):
+                q, t = step_one(slot, 2 * pair + g, lhs)
+                for x, k in enumerate(ks):
+                    t1_ref[pl.ds(flipped(me, k) * nj, nj), q, :] = t[x * nj:(x + 1) * nj]
             return carry
 
-        lax.fori_loop(0, n // 16, first, 0)
-        before = None
+        lax.fori_loop(0, n // 32, first, 0)
         for k in ks:
             step_two_three(k, i)
-            if before is not None:
-                send(before, i)
-            elif wait:
-                pl.semaphore_wait(barrier, len(DIRECT))
-            before = k
-        send(before, i)
+        if wait:
+            pl.semaphore_wait(barrier, len(DIRECT))
+        for k in ks:
+            send(k, i)
 
     some(DIRECT[:2], 0, 0, True)
     some((*DIRECT[2:], 0, *DIAGONAL), 0, 0, False)
@@ -231,14 +233,14 @@
         shapes += [(rows, size, lanes) for _ in DIAGONAL for _, size, _, lanes in TILES]
         outs = pl.pallas_call(
             functools.partial(exchange_kernel, n, n_dev, rows),
-            in_specs=[hbm, vmem],
+            in_specs=[hbm, hbm],
             out_specs=[hbm] * len(shapes),
             out_shape=[jax.ShapeDtypeStruct(s, BF16) for s in shapes],
             scratch_shapes=[
-                pltpu.VMEM((2, n, n, n), BF16), pltpu.VMEM((n, n, 128), BF16),
+                pltpu.VMEM((2, n, n, n), BF16), pltpu.VMEM((n, n), BF16), pltpu.VMEM((n, n, 128), BF16),
                 pltpu.VMEM((n_dev, rows, n, wide), BF16), pltpu.VMEM(square, BF16),
                 pltpu.VMEM(second, BF16), pltpu.VMEM((n, n), BF16),
-                pltpu.SemaphoreType.DMA((2,)), pltpu.SemaphoreType.DMA((n // 16,)), pltpu.SemaphoreType.DMA,
+                pltpu.SemaphoreType.DMA, pltpu.SemaphoreType.DMA((2,)), pltpu.SemaphoreType.DMA((n // 16,)), pltpu.SemaphoreType.DMA,
                 pltpu.SemaphoreType.DMA((len(shapes) - n_got,)),
                 pltpu.SemaphoreType.DMA((n_dev,)), pltpu.SemaphoreType.DMA((n_dev,))],
             compiler_params=pltpu.CompilerParams(collective_id=0, has_side_effects=True),
@@ -273,7 +275,7 @@
                 specs.append(hbm)
             alone = size == 8
             out = pl.pallas_call(
-                functools.partial(tail_kernel, n, n_in, a0, lane, lanes, 3) if alone
+                functools.partial(tail_kernel, n, n_in, a0, lane, lanes, 4) if alone
                 else functools.partial(out_kernel, n_in, lanes),
                 grid=(size // 8,),
                 in_specs=specs,
@@ -282,7 +284,7 @@
                     lambda i, at=(a0, lane): (0, pl.multiple_of(at[0] + 8 * i, 8), at[1])),
                 out_shape=jax.ShapeDtypeStruct((n, n, wide), F32),
                 input_output_aliases={} if t_i == 0 else {len(ins) - 1: 0},
-                scratch_shapes=[pltpu.VMEM((n, 8, lanes), F32), pltpu.SemaphoreType.DMA((3,))] * alone,
+                scratch_shapes=[pltpu.VMEM((n, 8, lanes), F32), pltpu.SemaphoreType.DMA((4,))] * alone,
                 compiler_params=pltpu.CompilerParams(vmem_limit_bytes=67043328),
                 name='out',
             )(*ins)

time: 283 us -> 283 us (level)
  no operation moved by 1% of the time
where the time goes in v5:
time: 283 us; the launch traced here: 282 us
  Pallas kernels  168 us (59%)
  waiting for transfers between devices  99.2 us (35%)
  starting transfers between devices  14.8 us (5%)
    pallas_call x1, Pallas kernels, transform(): pl.pallas_call(functools.partial(exchange_kernel, n, n_dev, rows), in_spe...  122 us
    ppermute x12, waiting for transfers between devices, transform(): lax.ppermute(tiles[x * len(TILES) + t], 'dev', [(i, i ^ k) for i in range...  99.2 us
    pallas_call x6, Pallas kernels, transform(): pl.pallas_call(functools.partial(tail_kernel, n, n_in, a0, lane, lanes, 4...  43.8 us
    ppermute x12, starting transfers between devices, transform(): lax.ppermute(tiles[x * len(TILES) + t], 'dev', [(i, i ^ k) for i in range...  14.8 us
  transfers between devices with their start and end apart: 12, of which 3 were waited for; matrix products, arithmetic and copies ran while one was open for 0% of the time, Pallas kernels for 15%

profile of v5, /device:TPU:0, one launch (start us, length us, event | category | flops | bytes accessed | tf_op | source)
XLA Modules:
  0.0 282.4 jit_solution(6027093309391244328)
XLA Ops:
  0.0 121.8 %exchange.1 = (bf16[12,96,1152]{2,1,0:T(8,128)(2,1)}, bf16[12,96,1152]{2,1,0:T(8,128)(2,1)}, bf16[12,96,1152]{2,1,0:T(8,128)(2,1)}, bf16[12,96,1152]{2,1,0:T(8,1...) custom-call(bf16[12,96,96,96]{3,2,1,0:T(8,128)(2,1)} %a_hbm.1, ...), custom_call_target="tpu_custom_call" | custom-call | tf_op jit(solution)/shard_map/exchange/pallas_call | solution.py:234
  121.8 1.5 collective-permute-start.10
  123.3 1.2 collective-permute-start.11
  124.5 1.5 collective-permute-start.4
  126.0 1.5 collective-permute-start.8
  127.4 0.9 collective-permute-start.9
  128.3 59.9 %collective-permute-done.4.refs_6_ = bf16[12,8,1152]{2,1,0:T(8,128)(2,1)} collective-permute-done((bf16[12,8,1152]{2,1,0:T(8,128)(2,1)}, bf16[12,8,1152]{2,1,0:T(8,128)(2,1)}, u32[]{:S(2)}, u32[]{:S(2)}) %collective-permute-start.4) | collective-permute-done | bytes 221216 | tf_op jit(solution)/shard_map/ppermute | solution.py:253
  188.2 1.5 collective-permute-start.6
  189.7 31.2 %collective-permute-done.6.refs_6_ = bf16[12,8,1152]{2,1,0:T(8,128)(2,1)} collective-permute-done((bf16[12,8,1152]{2,1,0:T(8,128)(2,1)}, bf16[12,8,1152]{2,1,0:T(8,128)(2,1)}, u32[]{:S(2)}, u32[]{:S(2)}) %collective-permute-start.6) | collective-permute-done | bytes 221216 | tf_op jit(solution)/shard_map/ppermute | solution.py:253
  220.9 0.6 collective-permute-start.7
  221.5 8.1 %collective-permute-done.7.refs_7_ = bf16[12,8,1152]{2,1,0:T(8,128)(2,1)} collective-permute-done((bf16[12,8,1152]{2,1,0:T(8,128)(2,1)}, bf16[12,8,1152]{2,1,0:T(8,128)(2,1)}, u32[]{:S(2)}, u32[]{:S(2)}) %collective-permute-start.7) | collective-permute-done | bytes 221216 | tf_op jit(solution)/shard_map/ppermute | solution.py:253
  229.6 0.9 collective-permute-start.5
  230.5 1.5 collective-permute-start.2
  232.0 1.4 collective-permute-start.3
  233.4 0.0 collective-permute-done.10.refs_6_
  233.4 1.5 collective-permute-start
  234.9 0.9 collective-permute-start.1
  235.8 2.5 last.1.refs_8_
  238.3 17.2 %out.6.refs_9_ = f32[96,96,1152]{2,1,0:T(8,128)} custom-call(bf16[12,96,1152]{2,1,0:T(8,128)(2,1)} %get-tuple-element.23.after_ref.refs_0_, bf16[12,96,1152]{2,1,0:T(8,128)(2,1)} %get-tuple-element.24.refs_1_, bf16[12,96,1152]{2,1,0:T(8,128)(2,1)} %get-tuple-element.25.refs_2_, bf16[12,96,1152]{2,1,0:T(8,128)(2,1)} %get-tuple-element.26.refs_3_, ...), custom_call_target="tpu_custom_call" | custom-call | tf_op jit(solution)/shard_map/out/pallas_call | solution.py:277
  255.5 10.5 %out.7.refs_9_ = f32[96,96,1152]{2,1,0:T(8,128)} custom-call(bf16[12,96,1152]{2,1,0:T(8,128)(2,1)} %get-tuple-element.23.after_ref.refs_0_, bf16[12,96,1152]{2,1,0:T(8,128)(2,1)} %get-tuple-element.24.refs_1_, bf16[12,96,1152]{2,1,0:T(8,128)(2,1)} %get-tuple-element.25.refs_2_, ...), custom_call_target="tpu_custom_call", output_to_operand_aliasing={{}: (9, {})} | custom-call | tf_op jit(solution)/shard_map/out/pallas_call | solution.py:277
  266.1 4.6 %out.8.refs_9_ = f32[96,96,1152]{2,1,0:T(8,128)} custom-call(bf16[12,96,1152]{2,1,0:T(8,128)(2,1)} %get-tuple-element.23.after_ref.refs_0_, bf16[12,96,1152]{2,1,0:T(8,128)(2,1)} %get-tuple-element.24.refs_1_, bf16[12,96,1152]{2,1,0:T(8,128)(2,1)} %get-tuple-element.25.refs_2_, ...), custom_call_target="tpu_custom_call", output_to_operand_aliasing={{}: (9, {})} | custom-call | tf_op jit(solution)/shard_map/out/pallas_call | solution.py:277
  270.7 4.6 %out.9.refs_9_ = f32[96,96,1152]{2,1,0:T(8,128)} custom-call(bf16[12,96,1152]{2,1,0:T(8,128)(2,1)} %get-tuple-element.23.after_ref.refs_0_, bf16[12,96,1152]{2,1,0:T(8,128)(2,1)} %get-tuple-element.24.refs_1_, bf16[12,96,1152]{2,1,0:T(8,128)(2,1)} %get-tuple-element.25.refs_2_, ...), custom_call_target="tpu_custom_call", output_to_operand_aliasing={{}: (9, {})} | custom-call | tf_op jit(solution)/shard_map/out/pallas_call | solution.py:277
  275.3 3.6 %out.10.refs_9_ = f32[96,96,1152]{2,1,0:T(8,128)} custom-call(bf16[12,96,1152]{2,1,0:T(8,128)(2,1)} %get-tuple-element.23.after_ref.refs_0_, bf16[12,96,1152]{2,1,0:T(8,128)(2,1)} %get-tuple-element.24.refs_1_, bf16[12,96,1152]{2,1,0:T(8,128)(2,1)} %get-tuple-element.25.refs_2_, ...), custom_call_target="tpu_custom_call", output_to_operand_aliasing={{}: (9, {})} | custom-call | tf_op jit(solution)/shard_map/out/pallas_call | solution.py:277
  279.0 3.2 %out.11 = f32[96,96,1152]{2,1,0:T(8,128)} custom-call(bf16[12,96,1152]{2,1,0:T(8,128)(2,1)} %get-tuple-element.23.after_ref.refs_0_, bf16[12,96,1152]{2,1,0:T(8,128)(2,1)} %get-tuple-element.24.refs_1_, bf16[12,96,1152]{2,1,0:T(8,128)(2,1)} %get-tuple-element.25.refs_2_, ...), custom_call_target="tpu_custom_call", output_to_operand_aliasing={{}: (9, {})} | custom-call | tf_op jit(solution)/shard_map/out/pallas_call | solution.py:277
  (8 shorter events, 0.0 us)
Async XLA Ops:
  121.8 111.6 %collective-permute-start.10 = (bf16[12,48,1152]{2,1,0:T(8,128)(2,1)}, bf16[12,48,1152]{2,1,0:T(8,128)(2,1)}, u32[]{:S(2)}, u32[]{:S(2)}) collective-permute-start(bf16[12,48,1152]{2,1,0:T(8,128)(2,1)} %get-tuple-element.39), channel_id=1, source_target_pairs={{0,6},{1,7},{2,4},{3,5},{4,2},{5,3},{6,0},{7,1},{8,14},{9,15},{10,... | collective-permute-start | bytes 3981320 | tf_op jit(solution)/shard_map/ppermute | solution.py:253
  123.3 111.6 %collective-permute-start.11 = (bf16[12,48,1152]{2,1,0:T(8,128)(2,1)}, bf16[12,48,1152]{2,1,0:T(8,128)(2,1)}, u32[]{:S(2)}, u32[]{:S(2)}) collective-permute-start(bf16[12,48,1152]{2,1,0:T(8,128)(2,1)} %get-tuple-element.40), channel_id=1, source_target_pairs={{0,7},{1,6},{2,5},{3,4},{4,3},{5,2},{6,1},{7,0},{8,15},{9,14},{10,... | collective-permute-start | bytes 3981320 | tf_op jit(solution)/shard_map/ppermute | solution.py:253
  124.5 63.7 %collective-permute-start.4 = (bf16[12,8,1152]{2,1,0:T(8,128)(2,1)}, bf16[12,8,1152]{2,1,0:T(8,128)(2,1)}, u32[]{:S(2)}, u32[]{:S(2)}) collective-permute-start(bf16[12,8,1152]{2,1,0:T(8,128)(2,1)} %get-tuple-element.33), channel_id=1, source_target_pairs={{0,6},{1,7},{2,4},{3,5},{4,2},{5,3},{6,0},{7,1},{8,14},{9,15},{10,... | collective-permute-start | bytes 663560 | tf_op jit(solution)/shard_map/ppermute | solution.py:253
  126.0 104.5 %collective-permute-start.8 = (bf16[12,24,1152]{2,1,0:T(8,128)(2,1)}, bf16[12,24,1152]{2,1,0:T(8,128)(2,1)}, u32[]{:S(2)}, u32[]{:S(2)}) collective-permute-start(bf16[12,24,1152]{2,1,0:T(8,128)(2,1)} %get-tuple-element.37), channel_id=1, source_target_pairs={{0,6},{1,7},{2,4},{3,5},{4,2},{5,3},{6,0},{7,1},{8,14},{9,15},{10,... | collective-permute-start | bytes 1990664 | tf_op jit(solution)/shard_map/ppermute | solution.py:253
  127.4 104.5 %collective-permute-start.9 = (bf16[12,24,1152]{2,1,0:T(8,128)(2,1)}, bf16[12,24,1152]{2,1,0:T(8,128)(2,1)}, u32[]{:S(2)}, u32[]{:S(2)}) collective-permute-start(bf16[12,24,1152]{2,1,0:T(8,128)(2,1)} %get-tuple-element.38), channel_id=1, source_target_pairs={{0,7},{1,6},{2,5},{3,4},{4,3},{5,2},{6,1},{7,0},{8,15},{9,14},{10,... | collective-permute-start | bytes 1990664 | tf_op jit(solution)/shard_map/ppermute | solution.py:253
  188.2 32.6 %collective-permute-start.6 = (bf16[12,8,1152]{2,1,0:T(8,128)(2,1)}, bf16[12,8,1152]{2,1,0:T(8,128)(2,1)}, u32[]{:S(2)}, u32[]{:S(2)}) collective-permute-start(bf16[12,8,1152]{2,1,0:T(8,128)(2,1)} %get-tuple-element.35), channel_id=1, source_target_pairs={{0,6},{1,7},{2,4},{3,5},{4,2},{5,3},{6,0},{7,1},{8,14},{9,15},{10,... | collective-permute-start | bytes 663560 | tf_op jit(solution)/shard_map/ppermute | solution.py:253
  220.9 8.7 %collective-permute-start.7 = (bf16[12,8,1152]{2,1,0:T(8,128)(2,1)}, bf16[12,8,1152]{2,1,0:T(8,128)(2,1)}, u32[]{:S(2)}, u32[]{:S(2)}) collective-permute-start(bf16[12,8,1152]{2,1,0:T(8,128)(2,1)} %get-tuple-element.36), channel_id=1, source_target_pairs={{0,7},{1,6},{2,5},{3,4},{4,3},{5,2},{6,1},{7,0},{8,15},{9,14},{10,... | collective-permute-start | bytes 663560 | tf_op jit(solution)/shard_map/ppermute | solution.py:253
  229.6 41.1 %collective-permute-start.5 = (bf16[12,8,1152]{2,1,0:T(8,128)(2,1)}, bf16[12,8,1152]{2,1,0:T(8,128)(2,1)}, u32[]{:S(2)}, u32[]{:S(2)}) collective-permute-start(bf16[12,8,1152]{2,1,0:T(8,128)(2,1)} %get-tuple-element.34), channel_id=1, source_target_pairs={{0,7},{1,6},{2,5},{3,4},{4,3},{5,2},{6,1},{7,0},{8,15},{9,14},{10,... | collective-permute-start | bytes 663560 | tf_op jit(solution)/shard_map/ppermute | solution.py:253
  230.5 44.8 %collective-permute-start.2 = (bf16[12,8,640]{2,1,0:T(8,128)(2,1)}, bf16[12,8,640]{2,1,0:T(8,128)(2,1)}, u32[]{:S(2)}, u32[]{:S(2)}) collective-permute-start(bf16[12,8,640]{2,1,0:T(8,128)(2,1)} %get-tuple-element.31), channel_id=1, source_target_pairs={{0,6},{1,7},{2,4},{3,5},{4,2},{5,3},{6,0},{7,1},{8,14},{9,15},{10,... | collective-permute-start | bytes 368648 | tf_op jit(solution)/shard_map/ppermute | solution.py:253
  232.0 43.4 %collective-permute-start.3 = (bf16[12,8,640]{2,1,0:T(8,128)(2,1)}, bf16[12,8,640]{2,1,0:T(8,128)(2,1)}, u32[]{:S(2)}, u32[]{:S(2)}) collective-permute-start(bf16[12,8,640]{2,1,0:T(8,128)(2,1)} %get-tuple-element.32), channel_id=1, source_target_pairs={{0,7},{1,6},{2,5},{3,4},{4,3},{5,2},{6,1},{7,0},{8,15},{9,14},{10,... | collective-permute-start | bytes 368648 | tf_op jit(solution)/shard_map/ppermute | solution.py:253
  233.4 45.6 %collective-permute-start = (bf16[12,8,512]{2,1,0:T(8,128)(2,1)}, bf16[12,8,512]{2,1,0:T(8,128)(2,1)}, u32[]{:S(2)}, u32[]{:S(2)}) collective-permute-start(bf16[12,8,512]{2,1,0:T(8,128)(2,1)} %get-tuple-element.29), channel_id=1, source_target_pairs={{0,6},{1,7},{2,4},{3,5},{4,2},{5,3},{6,0},{7,1},{8,14},{9,15},{10,... | collective-permute-start | bytes 294920 | tf_op jit(solution)/shard_map/ppermute | solution.py:253
  234.9 44.1 %collective-permute-start.1 = (bf16[12,8,512]{2,1,0:T(8,128)(2,1)}, bf16[12,8,512]{2,1,0:T(8,128)(2,1)}, u32[]{:S(2)}, u32[]{:S(2)}) collective-permute-start(bf16[12,8,512]{2,1,0:T(8,128)(2,1)} %get-tuple-element.30), channel_id=1, source_target_pairs={{0,7},{1,6},{2,5},{3,4},{4,3},{5,2},{6,1},{7,0},{8,15},{9,14},{10,... | collective-permute-start | bytes 294920 | tf_op jit(solution)/shard_map/ppermute | solution.py:253

commit v6 on v5

--- a/solution.py
+++ b/solution.py
@@ -69,13 +69,16 @@
     return out
 
 
-def exchange_kernel(n, n_dev, rows, a_hbm, c_hbm, *refs):
+def exchange_kernel(n, n_dev, rows, a_hbm, c_ref, *refs):
     n_got, n_tile = n_dev - len(DIAGONAL), len(TILES)
     got, tiles = refs[:n_got], refs[n_got:n_got + len(DIAGONAL) * n_tile]
-    (a_buf, c_ref, t1_ref, g_ref, l1_ref, r2_ref, ct_ref, c_sem, a_sem, chunk_sem, own_sem, tile_sem, send_sem,
+    (a_buf, t1_ref, g_ref, l1_ref, r2_ref, ct_ref, a_sem, chunk_sem, own_sem, tile_sem, send_sem,
      recv_sem) = refs[n_got + len(tiles):]
     nj = n // n_dev
     me = lax.axis_index('dev')
+    barrier = pltpu.get_barrier_semaphore()
+    for k in DIRECT:
+        pl.semaphore_signal(barrier, inc=1, device_id={'dev': flipped(me, k)}, device_id_type=pl.DeviceIdType.MESH)
 
     def chunk(g):
         q = pl.ds(g * 16, 16)
@@ -85,15 +88,9 @@
         slot = lax.rem(i, 2)
         return pltpu.make_async_copy(a_hbm.at[i], a_buf.at[slot], a_sem.at[slot])
 
-    c_copy = pltpu.make_async_copy(c_hbm, c_ref, c_sem)
-    c_copy.start()
     for g in range(n // 16):
         chunk(g).start()
     fetch(1).start()
-    barrier = pltpu.get_barrier_semaphore()
-    for k in DIRECT:
-        pl.semaphore_signal(barrier, inc=1, device_id={'dev': flipped(me, k)}, device_id_type=pl.DeviceIdType.MESH)
-    c_copy.wait()
     build_first(n, c_ref, l1_ref, r2_ref, ct_ref)
     zero = jnp.zeros((8 * n, 128 - n), BF16)
 
@@ -127,8 +124,8 @@
         t = jnp.concatenate([t[:, :128].reshape(nj, 8, 128), t[:, 128:].reshape(nj, 8, 128)], axis=1)
         return pl.ds(q0, 16), t.astype(BF16)
 
-    def step_two_three(k, i):
-        d = flipped(me, k)
+    def step_two_three(k, i, d=None):
+        d = flipped(me, k) if d is None else d
         t = t1_ref[pl.ds(d * nj, nj)].reshape(nj // 4, 4, n, 128)
         lhs = jnp.concatenate([t[:, jj].reshape(nj // 4 * n, 128) for jj in range(4)], axis=1)
         h = dot(lhs, r2_ref[...]).astype(BF16)
@@ -149,12 +146,23 @@
             return carry
 
         lax.fori_loop(0, n // 32, first, 0)
-        for k in ks:
-            step_two_three(k, i)
-        if wait:
-            pl.semaphore_wait(barrier, len(DIRECT))
-        for k in ks:
-            send(k, i)
+        if not wait:
+            for k in ks:
+                step_two_three(k, i)
+            for k in ks:
+                send(k, i)
+            return
+        core = me % 2
+        (k0, d0), (k1, d1) = ((k, flipped(me, k)) for k in ks)
+        for turn in range(2):
+            swap = core if turn == 0 else 1 - core
+            step_two_three(k0 + swap * (k1 - k0), i, d0 + swap * (d1 - d0))
+            if turn == 0:
+                pl.semaphore_wait(barrier, len(DIRECT))
+            for x, k in enumerate(ks):
+                @pl.when(swap == x)
+                def _(k=k):
+                    send(k, i)
 
     some(DIRECT[:2], 0, 0, True)
     some((*DIRECT[2:], 0, *DIAGONAL), 0, 0, False)
@@ -233,14 +241,14 @@
         shapes += [(rows, size, lanes) for _ in DIAGONAL for _, size, _, lanes in TILES]
         outs = pl.pallas_call(
             functools.partial(exchange_kernel, n, n_dev, rows),
-            in_specs=[hbm, hbm],
+            in_specs=[hbm, vmem],
             out_specs=[hbm] * len(shapes),
             out_shape=[jax.ShapeDtypeStruct(s, BF16) for s in shapes],
             scratch_shapes=[
-                pltpu.VMEM((2, n, n, n), BF16), pltpu.VMEM((n, n), BF16), pltpu.VMEM((n, n, 128), BF16),
+                pltpu.VMEM((2, n, n, n), BF16), pltpu.VMEM((n, n, 128), BF16),
                 pltpu.VMEM((n_dev, rows, n, wide), BF16), pltpu.VMEM(square, BF16),
                 pltpu.VMEM(second, BF16), pltpu.VMEM((n, n), BF16),
-                pltpu.SemaphoreType.DMA, pltpu.SemaphoreType.DMA((2,)), pltpu.SemaphoreType.DMA((n // 16,)), pltpu.SemaphoreType.DMA,
+                pltpu.SemaphoreType.DMA((2,)), pltpu.SemaphoreType.DMA((n // 16,)), pltpu.SemaphoreType.DMA,
                 pltpu.SemaphoreType.DMA((len(shapes) - n_got,)),
                 pltpu.SemaphoreType.DMA((n_dev,)), pltpu.SemaphoreType.DMA((n_dev,))],
             compiler_params=pltpu.CompilerParams(collective_id=0, has_side_effects=True),

time: 283 us -> 282 us (level)
  no operation moved by 1% of the time
where the time goes in v6:
time: 282 us; the launch traced here: 281 us
  Pallas kernels  168 us (60%)
  waiting for transfers between devices  98.9 us (35%)
  starting transfers between devices  14.5 us (5%)
    pallas_call x1, Pallas kernels, transform(): pl.pallas_call(functools.partial(exchange_kernel, n, n_dev, rows), in_spe...  122 us
    ppermute x12, waiting for transfers between devices, transform(): lax.ppermute(tiles[x * len(TILES) + t], 'dev', [(i, i ^ k) for i in range...  98.9 us
    pallas_call x6, Pallas kernels, transform(): pl.pallas_call(functools.partial(tail_kernel, n, n_in, a0, lane, lanes, 4...  43.8 us
    ppermute x12, starting transfers between devices, transform(): lax.ppermute(tiles[x * len(TILES) + t], 'dev', [(i, i ^ k) for i in range...  14.5 us
  transfers between devices with their start and end apart: 12, of which 3 were waited for; matrix products, arithmetic and copies ran while one was open for 0% of the time, Pallas kernels for 15%

profile of v6, /device:TPU:0, one launch (start us, length us, event | category | flops | bytes accessed | tf_op | source)
XLA Modules:
  0.0 281.4 jit_solution(2352653462426309409)
XLA Ops:
  0.0 121.5 %exchange.1 = (bf16[12,96,1152]{2,1,0:T(8,128)(2,1)}, bf16[12,96,1152]{2,1,0:T(8,128)(2,1)}, bf16[12,96,1152]{2,1,0:T(8,128)(2,1)}, bf16[12,96,1152]{2,1,0:T(8,1...) custom-call(bf16[12,96,96,96]{3,2,1,0:T(8,128)(2,1)} %a_hbm.1, ...), custom_call_target="tpu_custom_call" | custom-call | tf_op jit(solution)/shard_map/exchange/pallas_call | solution.py:242
  121.5 1.5 collective-permute-start.10
  123.0 1.0 collective-permute-start.11
  124.0 1.5 collective-permute-start.4
  125.5 1.4 collective-permute-start.8
  126.9 1.1 collective-permute-start.9
  128.1 59.9 %collective-permute-done.4.refs_6_ = bf16[12,8,1152]{2,1,0:T(8,128)(2,1)} collective-permute-done((bf16[12,8,1152]{2,1,0:T(8,128)(2,1)}, bf16[12,8,1152]{2,1,0:T(8,128)(2,1)}, u32[]{:S(2)}, u32[]{:S(2)}) %collective-permute-start.4) | collective-permute-done | bytes 221216 | tf_op jit(solution)/shard_map/ppermute | solution.py:261
  187.9 1.5 collective-permute-start.6
  189.4 30.9 %collective-permute-done.6.refs_6_ = bf16[12,8,1152]{2,1,0:T(8,128)(2,1)} collective-permute-done((bf16[12,8,1152]{2,1,0:T(8,128)(2,1)}, bf16[12,8,1152]{2,1,0:T(8,128)(2,1)}, u32[]{:S(2)}, u32[]{:S(2)}) %collective-permute-start.6) | collective-permute-done | bytes 221216 | tf_op jit(solution)/shard_map/ppermute | solution.py:261
  220.4 0.4 collective-permute-start.7
  220.8 8.0 %collective-permute-done.7.refs_7_ = bf16[12,8,1152]{2,1,0:T(8,128)(2,1)} collective-permute-done((bf16[12,8,1152]{2,1,0:T(8,128)(2,1)}, bf16[12,8,1152]{2,1,0:T(8,128)(2,1)}, u32[]{:S(2)}, u32[]{:S(2)}) %collective-permute-start.7) | collective-permute-done | bytes 221216 | tf_op jit(solution)/shard_map/ppermute | solution.py:261
  228.8 0.7 collective-permute-start.5
  229.6 1.4 collective-permute-start.2
  231.0 0.0 collective-permute-done.9.refs_7_
  231.0 1.7 collective-permute-start.3
  232.7 1.4 collective-permute-start
  234.1 0.7 collective-permute-start.1
  234.9 2.5 last.1.refs_8_
  237.4 17.2 %out.6.refs_9_ = f32[96,96,1152]{2,1,0:T(8,128)} custom-call(bf16[12,96,1152]{2,1,0:T(8,128)(2,1)} %get-tuple-element.23.after_ref.refs_0_, bf16[12,96,1152]{2,1,0:T(8,128)(2,1)} %get-tuple-element.24.refs_1_, bf16[12,96,1152]{2,1,0:T(8,128)(2,1)} %get-tuple-element.25.refs_2_, bf16[12,96,1152]{2,1,0:T(8,128)(2,1)} %get-tuple-element.26.refs_3_, ...), custom_call_target="tpu_custom_call" | custom-call | tf_op jit(solution)/shard_map/out/pallas_call | solution.py:285
  254.6 10.5 %out.7.refs_9_ = f32[96,96,1152]{2,1,0:T(8,128)} custom-call(bf16[12,96,1152]{2,1,0:T(8,128)(2,1)} %get-tuple-element.23.after_ref.refs_0_, bf16[12,96,1152]{2,1,0:T(8,128)(2,1)} %get-tuple-element.24.refs_1_, bf16[12,96,1152]{2,1,0:T(8,128)(2,1)} %get-tuple-element.25.refs_2_, ...), custom_call_target="tpu_custom_call", output_to_operand_aliasing={{}: (9, {})} | custom-call | tf_op jit(solution)/shard_map/out/pallas_call | solution.py:285
  265.1 4.6 %out.8.refs_9_ = f32[96,96,1152]{2,1,0:T(8,128)} custom-call(bf16[12,96,1152]{2,1,0:T(8,128)(2,1)} %get-tuple-element.23.after_ref.refs_0_, bf16[12,96,1152]{2,1,0:T(8,128)(2,1)} %get-tuple-element.24.refs_1_, bf16[12,96,1152]{2,1,0:T(8,128)(2,1)} %get-tuple-element.25.refs_2_, ...), custom_call_target="tpu_custom_call", output_to_operand_aliasing={{}: (9, {})} | custom-call | tf_op jit(solution)/shard_map/out/pallas_call | solution.py:285
  269.8 4.6 %out.9.refs_9_ = f32[96,96,1152]{2,1,0:T(8,128)} custom-call(bf16[12,96,1152]{2,1,0:T(8,128)(2,1)} %get-tuple-element.23.after_ref.refs_0_, bf16[12,96,1152]{2,1,0:T(8,128)(2,1)} %get-tuple-element.24.refs_1_, bf16[12,96,1152]{2,1,0:T(8,128)(2,1)} %get-tuple-element.25.refs_2_, ...), custom_call_target="tpu_custom_call", output_to_operand_aliasing={{}: (9, {})} | custom-call | tf_op jit(solution)/shard_map/out/pallas_call | solution.py:285
  274.4 3.6 %out.10.refs_9_ = f32[96,96,1152]{2,1,0:T(8,128)} custom-call(bf16[12,96,1152]{2,1,0:T(8,128)(2,1)} %get-tuple-element.23.after_ref.refs_0_, bf16[12,96,1152]{2,1,0:T(8,128)(2,1)} %get-tuple-element.24.refs_1_, bf16[12,96,1152]{2,1,0:T(8,128)(2,1)} %get-tuple-element.25.refs_2_, ...), custom_call_target="tpu_custom_call", output_to_operand_aliasing={{}: (9, {})} | custom-call | tf_op jit(solution)/shard_map/out/pallas_call | solution.py:285
  278.1 3.2 %out.11 = f32[96,96,1152]{2,1,0:T(8,128)} custom-call(bf16[12,96,1152]{2,1,0:T(8,128)(2,1)} %get-tuple-element.23.after_ref.refs_0_, bf16[12,96,1152]{2,1,0:T(8,128)(2,1)} %get-tuple-element.24.refs_1_, bf16[12,96,1152]{2,1,0:T(8,128)(2,1)} %get-tuple-element.25.refs_2_, ...), custom_call_target="tpu_custom_call", output_to_operand_aliasing={{}: (9, {})} | custom-call | tf_op jit(solution)/shard_map/out/pallas_call | solution.py:285
  (8 shorter events, 0.0 us)
Async XLA Ops:
  121.5 111.2 %collective-permute-start.10 = (bf16[12,48,1152]{2,1,0:T(8,128)(2,1)}, bf16[12,48,1152]{2,1,0:T(8,128)(2,1)}, u32[]{:S(2)}, u32[]{:S(2)}) collective-permute-start(bf16[12,48,1152]{2,1,0:T(8,128)(2,1)} %get-tuple-element.39), channel_id=1, source_target_pairs={{0,6},{1,7},{2,4},{3,5},{4,2},{5,3},{6,0},{7,1},{8,14},{9,15},{10,... | collective-permute-start | bytes 3981320 | tf_op jit(solution)/shard_map/ppermute | solution.py:261
  123.0 111.1 %collective-permute-start.11 = (bf16[12,48,1152]{2,1,0:T(8,128)(2,1)}, bf16[12,48,1152]{2,1,0:T(8,128)(2,1)}, u32[]{:S(2)}, u32[]{:S(2)}) collective-permute-start(bf16[12,48,1152]{2,1,0:T(8,128)(2,1)} %get-tuple-element.40), channel_id=1, source_target_pairs={{0,7},{1,6},{2,5},{3,4},{4,3},{5,2},{6,1},{7,0},{8,15},{9,14},{10,... | collective-permute-start | bytes 3981320 | tf_op jit(solution)/shard_map/ppermute | solution.py:261
  124.0 63.9 %collective-permute-start.4 = (bf16[12,8,1152]{2,1,0:T(8,128)(2,1)}, bf16[12,8,1152]{2,1,0:T(8,128)(2,1)}, u32[]{:S(2)}, u32[]{:S(2)}) collective-permute-start(bf16[12,8,1152]{2,1,0:T(8,128)(2,1)} %get-tuple-element.33), channel_id=1, source_target_pairs={{0,6},{1,7},{2,4},{3,5},{4,2},{5,3},{6,0},{7,1},{8,14},{9,15},{10,... | collective-permute-start | bytes 663560 | tf_op jit(solution)/shard_map/ppermute | solution.py:261
  125.5 104.1 %collective-permute-start.8 = (bf16[12,24,1152]{2,1,0:T(8,128)(2,1)}, bf16[12,24,1152]{2,1,0:T(8,128)(2,1)}, u32[]{:S(2)}, u32[]{:S(2)}) collective-permute-start(bf16[12,24,1152]{2,1,0:T(8,128)(2,1)} %get-tuple-element.37), channel_id=1, source_target_pairs={{0,6},{1,7},{2,4},{3,5},{4,2},{5,3},{6,0},{7,1},{8,14},{9,15},{10,... | collective-permute-start | bytes 1990664 | tf_op jit(solution)/shard_map/ppermute | solution.py:261
  126.9 104.1 %collective-permute-start.9 = (bf16[12,24,1152]{2,1,0:T(8,128)(2,1)}, bf16[12,24,1152]{2,1,0:T(8,128)(2,1)}, u32[]{:S(2)}, u32[]{:S(2)}) collective-permute-start(bf16[12,24,1152]{2,1,0:T(8,128)(2,1)} %get-tuple-element.38), channel_id=1, source_target_pairs={{0,7},{1,6},{2,5},{3,4},{4,3},{5,2},{6,1},{7,0},{8,15},{9,14},{10,... | collective-permute-start | bytes 1990664 | tf_op jit(solution)/shard_map/ppermute | solution.py:261
  187.9 32.4 %collective-permute-start.6 = (bf16[12,8,1152]{2,1,0:T(8,128)(2,1)}, bf16[12,8,1152]{2,1,0:T(8,128)(2,1)}, u32[]{:S(2)}, u32[]{:S(2)}) collective-permute-start(bf16[12,8,1152]{2,1,0:T(8,128)(2,1)} %get-tuple-element.35), channel_id=1, source_target_pairs={{0,6},{1,7},{2,4},{3,5},{4,2},{5,3},{6,0},{7,1},{8,14},{9,15},{10,... | collective-permute-start | bytes 663560 | tf_op jit(solution)/shard_map/ppermute | solution.py:261
  220.4 8.5 %collective-permute-start.7 = (bf16[12,8,1152]{2,1,0:T(8,128)(2,1)}, bf16[12,8,1152]{2,1,0:T(8,128)(2,1)}, u32[]{:S(2)}, u32[]{:S(2)}) collective-permute-start(bf16[12,8,1152]{2,1,0:T(8,128)(2,1)} %get-tuple-element.36), channel_id=1, source_target_pairs={{0,7},{1,6},{2,5},{3,4},{4,3},{5,2},{6,1},{7,0},{8,15},{9,14},{10,... | collective-permute-start | bytes 663560 | tf_op jit(solution)/shard_map/ppermute | solution.py:261
  228.8 40.9 %collective-permute-start.5 = (bf16[12,8,1152]{2,1,0:T(8,128)(2,1)}, bf16[12,8,1152]{2,1,0:T(8,128)(2,1)}, u32[]{:S(2)}, u32[]{:S(2)}) collective-permute-start(bf16[12,8,1152]{2,1,0:T(8,128)(2,1)} %get-tuple-element.34), channel_id=1, source_target_pairs={{0,7},{1,6},{2,5},{3,4},{4,3},{5,2},{6,1},{7,0},{8,15},{9,14},{10,... | collective-permute-start | bytes 663560 | tf_op jit(solution)/shard_map/ppermute | solution.py:261
  229.6 44.8 %collective-permute-start.2 = (bf16[12,8,640]{2,1,0:T(8,128)(2,1)}, bf16[12,8,640]{2,1,0:T(8,128)(2,1)}, u32[]{:S(2)}, u32[]{:S(2)}) collective-permute-start(bf16[12,8,640]{2,1,0:T(8,128)(2,1)} %get-tuple-element.31), channel_id=1, source_target_pairs={{0,6},{1,7},{2,4},{3,5},{4,2},{5,3},{6,0},{7,1},{8,14},{9,15},{10,... | collective-permute-start | bytes 368648 | tf_op jit(solution)/shard_map/ppermute | solution.py:261
  231.0 43.4 %collective-permute-start.3 = (bf16[12,8,640]{2,1,0:T(8,128)(2,1)}, bf16[12,8,640]{2,1,0:T(8,128)(2,1)}, u32[]{:S(2)}, u32[]{:S(2)}) collective-permute-start(bf16[12,8,640]{2,1,0:T(8,128)(2,1)} %get-tuple-element.32), channel_id=1, source_target_pairs={{0,7},{1,6},{2,5},{3,4},{4,3},{5,2},{6,1},{7,0},{8,15},{9,14},{10,... | collective-permute-start | bytes 368648 | tf_op jit(solution)/shard_map/ppermute | solution.py:261
  232.7 45.3 %collective-permute-start = (bf16[12,8,512]{2,1,0:T(8,128)(2,1)}, bf16[12,8,512]{2,1,0:T(8,128)(2,1)}, u32[]{:S(2)}, u32[]{:S(2)}) collective-permute-start(bf16[12,8,512]{2,1,0:T(8,128)(2,1)} %get-tuple-element.29), channel_id=1, source_target_pairs={{0,6},{1,7},{2,4},{3,5},{4,2},{5,3},{6,0},{7,1},{8,14},{9,15},{10,... | collective-permute-start | bytes 294920 | tf_op jit(solution)/shard_map/ppermute | solution.py:261
  234.1 43.9 %collective-permute-start.1 = (bf16[12,8,512]{2,1,0:T(8,128)(2,1)}, bf16[12,8,512]{2,1,0:T(8,128)(2,1)}, u32[]{:S(2)}, u32[]{:S(2)}) collective-permute-start(bf16[12,8,512]{2,1,0:T(8,128)(2,1)} %get-tuple-element.30), channel_id=1, source_target_pairs={{0,7},{1,6},{2,5},{3,4},{4,3},{5,2},{6,1},{7,0},{8,15},{9,14},{10,... | collective-permute-start | bytes 294920 | tf_op jit(solution)/shard_map/ppermute | solution.py:261

commit v7 on v6

--- a/solution.py
+++ b/solution.py
@@ -132,6 +132,13 @@
         h = jnp.concatenate([h[g * n:(g + 1) * n] for g in range(nj // 4)], axis=1)
         g_ref[k, i] = dot(ct_ref[...], h).astype(BF16)
 
+    def groups(i, *groups_):
+        for ks in groups_:
+            for k in ks:
+                step_two_three(k, i)
+            for k in ks:
+                send(k, i)
+
     def some(ks, i, slot, wait):
         def first(pair, carry):
             if wait:
@@ -147,10 +154,7 @@
 
         lax.fori_loop(0, n // 32, first, 0)
         if not wait:
-            for k in ks:
-                step_two_three(k, i)
-            for k in ks:
-                send(k, i)
+            groups(i, ks[:2], ks[2:])
             return
         core = me % 2
         (k0, d0), (k1, d1) = ((k, flipped(me, k)) for k in ks)
@@ -181,13 +185,7 @@
             return carry
 
         lax.fori_loop(0, n // 16, first, 0)
-        before = None
-        for k in (*DIRECT, 0, *DIAGONAL):
-            step_two_three(k, i)
-            if before is not None:
-                send(before, i)
-            before = k
-        send(before, i)
+        groups(i, DIRECT[:4], (*DIRECT[4:], 0, *DIAGONAL))
         return carry
 
     lax.fori_loop(1, rows, row, 0)

time: 282 us -> 282 us (level)
  no operation moved by 1% of the time
where the time goes in v7:
time: 282 us; the launch traced here: 281 us
  Pallas kernels  168 us (60%)
  waiting for transfers between devices  98.9 us (35%)
  starting transfers between devices  14.5 us (5%)
    pallas_call x1, Pallas kernels, transform(): pl.pallas_call(functools.partial(exchange_kernel, n, n_dev, rows), in_spe...  122 us
    ppermute x12, waiting for transfers between devices, transform(): lax.ppermute(tiles[x * len(TILES) + t], 'dev', [(i, i ^ k) for i in range...  98.9 us
    pallas_call x6, Pallas kernels, transform(): pl.pallas_call(functools.partial(tail_kernel, n, n_in, a0, lane, lanes, 4...  43.8 us
    ppermute x12, starting transfers between devices, transform(): lax.ppermute(tiles[x * len(TILES) + t], 'dev', [(i, i ^ k) for i in range...  14.5 us
  transfers between devices with their start and end apart: 12, of which 3 were waited for; matrix products, arithmetic and copies ran while one was open for 0% of the time, Pallas kernels for 15%

profile of v7, /device:TPU:0, one launch (start us, length us, event | category | flops | bytes accessed | tf_op | source)
XLA Modules:
  0.0 281.4 jit_solution(12562995511228895313)
XLA Ops:
  0.0 121.5 %exchange.1 = (bf16[12,96,1152]{2,1,0:T(8,128)(2,1)}, bf16[12,96,1152]{2,1,0:T(8,128)(2,1)}, bf16[12,96,1152]{2,1,0:T(8,128)(2,1)}, bf16[12,96,1152]{2,1,0:T(8,1...) custom-call(bf16[12,96,96,96]{3,2,1,0:T(8,128)(2,1)} %a_hbm.1, ...), custom_call_target="tpu_custom_call" | custom-call | tf_op jit(solution)/shard_map/exchange/pallas_call | solution.py:240
  121.5 1.5 collective-permute-start.10
  123.0 1.0 collective-permute-start.11
  124.0 1.5 collective-permute-start.4
  125.5 1.4 collective-permute-start.8
  126.9 1.1 collective-permute-start.9
  128.1 59.9 %collective-permute-done.4.refs_6_ = bf16[12,8,1152]{2,1,0:T(8,128)(2,1)} collective-permute-done((bf16[12,8,1152]{2,1,0:T(8,128)(2,1)}, bf16[12,8,1152]{2,1,0:T(8,128)(2,1)}, u32[]{:S(2)}, u32[]{:S(2)}) %collective-permute-start.4) | collective-permute-done | bytes 221216 | tf_op jit(solution)/shard_map/ppermute | solution.py:259
  187.9 1.5 collective-permute-start.6
  189.4 30.9 %collective-permute-done.6.refs_6_ = bf16[12,8,1152]{2,1,0:T(8,128)(2,1)} collective-permute-done((bf16[12,8,1152]{2,1,0:T(8,128)(2,1)}, bf16[12,8,1152]{2,1,0:T(8,128)(2,1)}, u32[]{:S(2)}, u32[]{:S(2)}) %collective-permute-start.6) | collective-permute-done | bytes 221216 | tf_op jit(solution)/shard_map/ppermute | solution.py:259
  220.4 0.4 collective-permute-start.7
  220.8 8.0 %collective-permute-done.7.refs_7_ = bf16[12,8,1152]{2,1,0:T(8,128)(2,1)} collective-permute-done((bf16[12,8,1152]{2,1,0:T(8,128)(2,1)}, bf16[12,8,1152]{2,1,0:T(8,128)(2,1)}, u32[]{:S(2)}, u32[]{:S(2)}) %collective-permute-start.7) | collective-permute-done | bytes 221216 | tf_op jit(solution)/shard_map/ppermute | solution.py:259
  228.8 0.7 collective-permute-start.5
  229.6 1.4 collective-permute-start.2
  231.0 0.0 collective-permute-done.9.refs_7_
  231.0 1.7 collective-permute-start.3
  232.7 1.4 collective-permute-start
  234.1 0.7 collective-permute-start.1
  234.9 2.5 last.1.refs_8_
  237.4 17.2 %out.6.refs_9_ = f32[96,96,1152]{2,1,0:T(8,128)} custom-call(bf16[12,96,1152]{2,1,0:T(8,128)(2,1)} %get-tuple-element.23.after_ref.refs_0_, bf16[12,96,1152]{2,1,0:T(8,128)(2,1)} %get-tuple-element.24.refs_1_, bf16[12,96,1152]{2,1,0:T(8,128)(2,1)} %get-tuple-element.25.refs_2_, bf16[12,96,1152]{2,1,0:T(8,128)(2,1)} %get-tuple-element.26.refs_3_, ...), custom_call_target="tpu_custom_call" | custom-call | tf_op jit(solution)/shard_map/out/pallas_call | solution.py:283
  254.6 10.5 %out.7.refs_9_ = f32[96,96,1152]{2,1,0:T(8,128)} custom-call(bf16[12,96,1152]{2,1,0:T(8,128)(2,1)} %get-tuple-element.23.after_ref.refs_0_, bf16[12,96,1152]{2,1,0:T(8,128)(2,1)} %get-tuple-element.24.refs_1_, bf16[12,96,1152]{2,1,0:T(8,128)(2,1)} %get-tuple-element.25.refs_2_, ...), custom_call_target="tpu_custom_call", output_to_operand_aliasing={{}: (9, {})} | custom-call | tf_op jit(solution)/shard_map/out/pallas_call | solution.py:283
  265.1 4.6 %out.8.refs_9_ = f32[96,96,1152]{2,1,0:T(8,128)} custom-call(bf16[12,96,1152]{2,1,0:T(8,128)(2,1)} %get-tuple-element.23.after_ref.refs_0_, bf16[12,96,1152]{2,1,0:T(8,128)(2,1)} %get-tuple-element.24.refs_1_, bf16[12,96,1152]{2,1,0:T(8,128)(2,1)} %get-tuple-element.25.refs_2_, ...), custom_call_target="tpu_custom_call", output_to_operand_aliasing={{}: (9, {})} | custom-call | tf_op jit(solution)/shard_map/out/pallas_call | solution.py:283
  269.8 4.6 %out.9.refs_9_ = f32[96,96,1152]{2,1,0:T(8,128)} custom-call(bf16[12,96,1152]{2,1,0:T(8,128)(2,1)} %get-tuple-element.23.after_ref.refs_0_, bf16[12,96,1152]{2,1,0:T(8,128)(2,1)} %get-tuple-element.24.refs_1_, bf16[12,96,1152]{2,1,0:T(8,128)(2,1)} %get-tuple-element.25.refs_2_, ...), custom_call_target="tpu_custom_call", output_to_operand_aliasing={{}: (9, {})} | custom-call | tf_op jit(solution)/shard_map/out/pallas_call | solution.py:283
  274.4 3.6 %out.10.refs_9_ = f32[96,96,1152]{2,1,0:T(8,128)} custom-call(bf16[12,96,1152]{2,1,0:T(8,128)(2,1)} %get-tuple-element.23.after_ref.refs_0_, bf16[12,96,1152]{2,1,0:T(8,128)(2,1)} %get-tuple-element.24.refs_1_, bf16[12,96,1152]{2,1,0:T(8,128)(2,1)} %get-tuple-element.25.refs_2_, ...), custom_call_target="tpu_custom_call", output_to_operand_aliasing={{}: (9, {})} | custom-call | tf_op jit(solution)/shard_map/out/pallas_call | solution.py:283
  278.1 3.2 %out.11 = f32[96,96,1152]{2,1,0:T(8,128)} custom-call(bf16[12,96,1152]{2,1,0:T(8,128)(2,1)} %get-tuple-element.23.after_ref.refs_0_, bf16[12,96,1152]{2,1,0:T(8,128)(2,1)} %get-tuple-element.24.refs_1_, bf16[12,96,1152]{2,1,0:T(8,128)(2,1)} %get-tuple-element.25.refs_2_, ...), custom_call_target="tpu_custom_call", output_to_operand_aliasing={{}: (9, {})} | custom-call | tf_op jit(solution)/shard_map/out/pallas_call | solution.py:283
  (8 shorter events, 0.0 us)
Async XLA Ops:
  121.5 111.2 %collective-permute-start.10 = (bf16[12,48,1152]{2,1,0:T(8,128)(2,1)}, bf16[12,48,1152]{2,1,0:T(8,128)(2,1)}, u32[]{:S(2)}, u32[]{:S(2)}) collective-permute-start(bf16[12,48,1152]{2,1,0:T(8,128)(2,1)} %get-tuple-element.39), channel_id=1, source_target_pairs={{0,6},{1,7},{2,4},{3,5},{4,2},{5,3},{6,0},{7,1},{8,14},{9,15},{10,... | collective-permute-start | bytes 3981320 | tf_op jit(solution)/shard_map/ppermute | solution.py:259
  123.0 111.1 %collective-permute-start.11 = (bf16[12,48,1152]{2,1,0:T(8,128)(2,1)}, bf16[12,48,1152]{2,1,0:T(8,128)(2,1)}, u32[]{:S(2)}, u32[]{:S(2)}) collective-permute-start(bf16[12,48,1152]{2,1,0:T(8,128)(2,1)} %get-tuple-element.40), channel_id=1, source_target_pairs={{0,7},{1,6},{2,5},{3,4},{4,3},{5,2},{6,1},{7,0},{8,15},{9,14},{10,... | collective-permute-start | bytes 3981320 | tf_op jit(solution)/shard_map/ppermute | solution.py:259
  124.0 63.9 %collective-permute-start.4 = (bf16[12,8,1152]{2,1,0:T(8,128)(2,1)}, bf16[12,8,1152]{2,1,0:T(8,128)(2,1)}, u32[]{:S(2)}, u32[]{:S(2)}) collective-permute-start(bf16[12,8,1152]{2,1,0:T(8,128)(2,1)} %get-tuple-element.33), channel_id=1, source_target_pairs={{0,6},{1,7},{2,4},{3,5},{4,2},{5,3},{6,0},{7,1},{8,14},{9,15},{10,... | collective-permute-start | bytes 663560 | tf_op jit(solution)/shard_map/ppermute | solution.py:259
  125.5 104.1 %collective-permute-start.8 = (bf16[12,24,1152]{2,1,0:T(8,128)(2,1)}, bf16[12,24,1152]{2,1,0:T(8,128)(2,1)}, u32[]{:S(2)}, u32[]{:S(2)}) collective-permute-start(bf16[12,24,1152]{2,1,0:T(8,128)(2,1)} %get-tuple-element.37), channel_id=1, source_target_pairs={{0,6},{1,7},{2,4},{3,5},{4,2},{5,3},{6,0},{7,1},{8,14},{9,15},{10,... | collective-permute-start | bytes 1990664 | tf_op jit(solution)/shard_map/ppermute | solution.py:259
  126.9 104.1 %collective-permute-start.9 = (bf16[12,24,1152]{2,1,0:T(8,128)(2,1)}, bf16[12,24,1152]{2,1,0:T(8,128)(2,1)}, u32[]{:S(2)}, u32[]{:S(2)}) collective-permute-start(bf16[12,24,1152]{2,1,0:T(8,128)(2,1)} %get-tuple-element.38), channel_id=1, source_target_pairs={{0,7},{1,6},{2,5},{3,4},{4,3},{5,2},{6,1},{7,0},{8,15},{9,14},{10,... | collective-permute-start | bytes 1990664 | tf_op jit(solution)/shard_map/ppermute | solution.py:259
  187.9 32.4 %collective-permute-start.6 = (bf16[12,8,1152]{2,1,0:T(8,128)(2,1)}, bf16[12,8,1152]{2,1,0:T(8,128)(2,1)}, u32[]{:S(2)}, u32[]{:S(2)}) collective-permute-start(bf16[12,8,1152]{2,1,0:T(8,128)(2,1)} %get-tuple-element.35), channel_id=1, source_target_pairs={{0,6},{1,7},{2,4},{3,5},{4,2},{5,3},{6,0},{7,1},{8,14},{9,15},{10,... | collective-permute-start | bytes 663560 | tf_op jit(solution)/shard_map/ppermute | solution.py:259
  220.4 8.5 %collective-permute-start.7 = (bf16[12,8,1152]{2,1,0:T(8,128)(2,1)}, bf16[12,8,1152]{2,1,0:T(8,128)(2,1)}, u32[]{:S(2)}, u32[]{:S(2)}) collective-permute-start(bf16[12,8,1152]{2,1,0:T(8,128)(2,1)} %get-tuple-element.36), channel_id=1, source_target_pairs={{0,7},{1,6},{2,5},{3,4},{4,3},{5,2},{6,1},{7,0},{8,15},{9,14},{10,... | collective-permute-start | bytes 663560 | tf_op jit(solution)/shard_map/ppermute | solution.py:259
  228.8 40.9 %collective-permute-start.5 = (bf16[12,8,1152]{2,1,0:T(8,128)(2,1)}, bf16[12,8,1152]{2,1,0:T(8,128)(2,1)}, u32[]{:S(2)}, u32[]{:S(2)}) collective-permute-start(bf16[12,8,1152]{2,1,0:T(8,128)(2,1)} %get-tuple-element.34), channel_id=1, source_target_pairs={{0,7},{1,6},{2,5},{3,4},{4,3},{5,2},{6,1},{7,0},{8,15},{9,14},{10,... | collective-permute-start | bytes 663560 | tf_op jit(solution)/shard_map/ppermute | solution.py:259
  229.6 44.8 %collective-permute-start.2 = (bf16[12,8,640]{2,1,0:T(8,128)(2,1)}, bf16[12,8,640]{2,1,0:T(8,128)(2,1)}, u32[]{:S(2)}, u32[]{:S(2)}) collective-permute-start(bf16[12,8,640]{2,1,0:T(8,128)(2,1)} %get-tuple-element.31), channel_id=1, source_target_pairs={{0,6},{1,7},{2,4},{3,5},{4,2},{5,3},{6,0},{7,1},{8,14},{9,15},{10,... | collective-permute-start | bytes 368648 | tf_op jit(solution)/shard_map/ppermute | solution.py:259
  231.0 43.4 %collective-permute-start.3 = (bf16[12,8,640]{2,1,0:T(8,128)(2,1)}, bf16[12,8,640]{2,1,0:T(8,128)(2,1)}, u32[]{:S(2)}, u32[]{:S(2)}) collective-permute-start(bf16[12,8,640]{2,1,0:T(8,128)(2,1)} %get-tuple-element.32), channel_id=1, source_target_pairs={{0,7},{1,6},{2,5},{3,4},{4,3},{5,2},{6,1},{7,0},{8,15},{9,14},{10,... | collective-permute-start | bytes 368648 | tf_op jit(solution)/shard_map/ppermute | solution.py:259
  232.7 45.3 %collective-permute-start = (bf16[12,8,512]{2,1,0:T(8,128)(2,1)}, bf16[12,8,512]{2,1,0:T(8,128)(2,1)}, u32[]{:S(2)}, u32[]{:S(2)}) collective-permute-start(bf16[12,8,512]{2,1,0:T(8,128)(2,1)} %get-tuple-element.29), channel_id=1, source_target_pairs={{0,6},{1,7},{2,4},{3,5},{4,2},{5,3},{6,0},{7,1},{8,14},{9,15},{10,... | collective-permute-start | bytes 294920 | tf_op jit(solution)/shard_map/ppermute | solution.py:259
  234.1 43.9 %collective-permute-start.1 = (bf16[12,8,512]{2,1,0:T(8,128)(2,1)}, bf16[12,8,512]{2,1,0:T(8,128)(2,1)}, u32[]{:S(2)}, u32[]{:S(2)}) collective-permute-start(bf16[12,8,512]{2,1,0:T(8,128)(2,1)} %get-tuple-element.30), channel_id=1, source_target_pairs={{0,7},{1,6},{2,5},{3,4},{4,3},{5,2},{6,1},{7,0},{8,15},{9,14},{10,... | collective-permute-start | bytes 294920 | tf_op jit(solution)/shard_map/ppermute | solution.py:259

commit v8 on v5

--- a/solution.py
+++ b/solution.py
@@ -69,13 +69,16 @@
     return out
 
 
-def exchange_kernel(n, n_dev, rows, a_hbm, c_hbm, *refs):
+def exchange_kernel(n, n_dev, rows, a_hbm, c_ref, *refs):
     n_got, n_tile = n_dev - len(DIAGONAL), len(TILES)
     got, tiles = refs[:n_got], refs[n_got:n_got + len(DIAGONAL) * n_tile]
-    (a_buf, c_ref, t1_ref, g_ref, l1_ref, r2_ref, ct_ref, c_sem, a_sem, chunk_sem, own_sem, tile_sem, send_sem,
+    (a_buf, t1_ref, g_ref, l1_ref, r2_ref, ct_ref, a_sem, chunk_sem, own_sem, tile_sem, send_sem,
      recv_sem) = refs[n_got + len(tiles):]
     nj = n // n_dev
     me = lax.axis_index('dev')
+    barrier = pltpu.get_barrier_semaphore()
+    for k in DIRECT:
+        pl.semaphore_signal(barrier, inc=1, device_id={'dev': flipped(me, k)}, device_id_type=pl.DeviceIdType.MESH)
 
     def chunk(g):
         q = pl.ds(g * 16, 16)
@@ -85,15 +88,9 @@
         slot = lax.rem(i, 2)
         return pltpu.make_async_copy(a_hbm.at[i], a_buf.at[slot], a_sem.at[slot])
 
-    c_copy = pltpu.make_async_copy(c_hbm, c_ref, c_sem)
-    c_copy.start()
     for g in range(n // 16):
         chunk(g).start()
     fetch(1).start()
-    barrier = pltpu.get_barrier_semaphore()
-    for k in DIRECT:
-        pl.semaphore_signal(barrier, inc=1, device_id={'dev': flipped(me, k)}, device_id_type=pl.DeviceIdType.MESH)
-    c_copy.wait()
     build_first(n, c_ref, l1_ref, r2_ref, ct_ref)
     zero = jnp.zeros((8 * n, 128 - n), BF16)
 
@@ -233,14 +230,14 @@
         shapes += [(rows, size, lanes) for _ in DIAGONAL for _, size, _, lanes in TILES]
         outs = pl.pallas_call(
             functools.partial(exchange_kernel, n, n_dev, rows),
-            in_specs=[hbm, hbm],
+            in_specs=[hbm, vmem],
             out_specs=[hbm] * len(shapes),
             out_shape=[jax.ShapeDtypeStruct(s, BF16) for s in shapes],
             scratch_shapes=[
-                pltpu.VMEM((2, n, n, n), BF16), pltpu.VMEM((n, n), BF16), pltpu.VMEM((n, n, 128), BF16),
+                pltpu.VMEM((2, n, n, n), BF16), pltpu.VMEM((n, n, 128), BF16),
                 pltpu.VMEM((n_dev, rows, n, wide), BF16), pltpu.VMEM(square, BF16),
                 pltpu.VMEM(second, BF16), pltpu.VMEM((n, n), BF16),
-                pltpu.SemaphoreType.DMA, pltpu.SemaphoreType.DMA((2,)), pltpu.SemaphoreType.DMA((n // 16,)), pltpu.SemaphoreType.DMA,
+                pltpu.SemaphoreType.DMA((2,)), pltpu.SemaphoreType.DMA((n // 16,)), pltpu.SemaphoreType.DMA,
                 pltpu.SemaphoreType.DMA((len(shapes) - n_got,)),
                 pltpu.SemaphoreType.DMA((n_dev,)), pltpu.SemaphoreType.DMA((n_dev,))],
             compiler_params=pltpu.CompilerParams(collective_id=0, has_side_effects=True),

time: 283 us -> 282 us (level)
  no operation moved by 1% of the time
where the time goes in v8:
time: 282 us
  Pallas kernels  167 us (59%)
  waiting for transfers between devices  99.2 us (35%)
  starting transfers between devices  14.9 us (5%)
    pallas_call x1, Pallas kernels, transform(): pl.pallas_call(functools.partial(exchange_kernel, n, n_dev, rows), in_spe...  121 us
    ppermute x12, waiting for transfers between devices, transform(): lax.ppermute(tiles[x * len(TILES) + t], 'dev', [(i, i ^ k) for i in range...  99.2 us
    pallas_call x6, Pallas kernels, transform(): pl.pallas_call(functools.partial(tail_kernel, n, n_in, a0, lane, lanes, 4...  43.8 us
    ppermute x12, starting transfers between devices, transform(): lax.ppermute(tiles[x * len(TILES) + t], 'dev', [(i, i ^ k) for i in range...  14.9 us
  transfers between devices with their start and end apart: 12, of which 3 were waited for; matrix products, arithmetic and copies ran while one was open for 0% of the time, Pallas kernels for 15%

profile of v8, /device:TPU:0, one launch (start us, length us, event | category | flops | bytes accessed | tf_op | source)
XLA Modules:
  0.0 281.8 jit_solution(13756484459473263471)
XLA Ops:
  0.0 121.1 %exchange.1 = (bf16[12,96,1152]{2,1,0:T(8,128)(2,1)}, bf16[12,96,1152]{2,1,0:T(8,128)(2,1)}, bf16[12,96,1152]{2,1,0:T(8,128)(2,1)}, bf16[12,96,1152]{2,1,0:T(8,1...) custom-call(bf16[12,96,96,96]{3,2,1,0:T(8,128)(2,1)} %a_hbm.1, ...), custom_call_target="tpu_custom_call" | custom-call | tf_op jit(solution)/shard_map/exchange/pallas_call | solution.py:231
  121.2 1.5 collective-permute-start.10
  122.7 1.2 collective-permute-start.11
  123.9 1.5 collective-permute-start.4
  125.4 1.5 collective-permute-start.8
  126.8 0.8 collective-permute-start.9
  127.7 59.9 %collective-permute-done.4.refs_6_ = bf16[12,8,1152]{2,1,0:T(8,128)(2,1)} collective-permute-done((bf16[12,8,1152]{2,1,0:T(8,128)(2,1)}, bf16[12,8,1152]{2,1,0:T(8,128)(2,1)}, u32[]{:S(2)}, u32[]{:S(2)}) %collective-permute-start.4) | collective-permute-done | bytes 221216 | tf_op jit(solution)/shard_map/ppermute | solution.py:250
  187.6 1.5 collective-permute-start.6
  189.0 31.2 %collective-permute-done.6.refs_6_ = bf16[12,8,1152]{2,1,0:T(8,128)(2,1)} collective-permute-done((bf16[12,8,1152]{2,1,0:T(8,128)(2,1)}, bf16[12,8,1152]{2,1,0:T(8,128)(2,1)}, u32[]{:S(2)}, u32[]{:S(2)}) %collective-permute-start.6) | collective-permute-done | bytes 221216 | tf_op jit(solution)/shard_map/ppermute | solution.py:250
  220.3 0.7 collective-permute-start.7
  220.9 8.1 %collective-permute-done.7.refs_7_ = bf16[12,8,1152]{2,1,0:T(8,128)(2,1)} collective-permute-done((bf16[12,8,1152]{2,1,0:T(8,128)(2,1)}, bf16[12,8,1152]{2,1,0:T(8,128)(2,1)}, u32[]{:S(2)}, u32[]{:S(2)}) %collective-permute-start.7) | collective-permute-done | bytes 221216 | tf_op jit(solution)/shard_map/ppermute | solution.py:250
  229.0 1.0 collective-permute-start.5
  229.9 1.5 collective-permute-start.2
  231.4 1.4 collective-permute-start.3
  232.8 0.0 collective-permute-done.10.refs_6_
  232.8 1.5 collective-permute-start
  234.3 1.0 collective-permute-start.1
  235.2 2.5 last.1.refs_8_
  237.8 17.2 %out.6.refs_9_ = f32[96,96,1152]{2,1,0:T(8,128)} custom-call(bf16[12,96,1152]{2,1,0:T(8,128)(2,1)} %get-tuple-element.23.after_ref.refs_0_, bf16[12,96,1152]{2,1,0:T(8,128)(2,1)} %get-tuple-element.24.refs_1_, bf16[12,96,1152]{2,1,0:T(8,128)(2,1)} %get-tuple-element.25.refs_2_, bf16[12,96,1152]{2,1,0:T(8,128)(2,1)} %get-tuple-element.26.refs_3_, ...), custom_call_target="tpu_custom_call" | custom-call | tf_op jit(solution)/shard_map/out/pallas_call | solution.py:274
  255.0 10.5 %out.7.refs_9_ = f32[96,96,1152]{2,1,0:T(8,128)} custom-call(bf16[12,96,1152]{2,1,0:T(8,128)(2,1)} %get-tuple-element.23.after_ref.refs_0_, bf16[12,96,1152]{2,1,0:T(8,128)(2,1)} %get-tuple-element.24.refs_1_, bf16[12,96,1152]{2,1,0:T(8,128)(2,1)} %get-tuple-element.25.refs_2_, ...), custom_call_target="tpu_custom_call", output_to_operand_aliasing={{}: (9, {})} | custom-call | tf_op jit(solution)/shard_map/out/pallas_call | solution.py:274
  265.5 4.6 %out.8.refs_9_ = f32[96,96,1152]{2,1,0:T(8,128)} custom-call(bf16[12,96,1152]{2,1,0:T(8,128)(2,1)} %get-tuple-element.23.after_ref.refs_0_, bf16[12,96,1152]{2,1,0:T(8,128)(2,1)} %get-tuple-element.24.refs_1_, bf16[12,96,1152]{2,1,0:T(8,128)(2,1)} %get-tuple-element.25.refs_2_, ...), custom_call_target="tpu_custom_call", output_to_operand_aliasing={{}: (9, {})} | custom-call | tf_op jit(solution)/shard_map/out/pallas_call | solution.py:274
  270.1 4.6 %out.9.refs_9_ = f32[96,96,1152]{2,1,0:T(8,128)} custom-call(bf16[12,96,1152]{2,1,0:T(8,128)(2,1)} %get-tuple-element.23.after_ref.refs_0_, bf16[12,96,1152]{2,1,0:T(8,128)(2,1)} %get-tuple-element.24.refs_1_, bf16[12,96,1152]{2,1,0:T(8,128)(2,1)} %get-tuple-element.25.refs_2_, ...), custom_call_target="tpu_custom_call", output_to_operand_aliasing={{}: (9, {})} | custom-call | tf_op jit(solution)/shard_map/out/pallas_call | solution.py:274
  274.8 3.6 %out.10.refs_9_ = f32[96,96,1152]{2,1,0:T(8,128)} custom-call(bf16[12,96,1152]{2,1,0:T(8,128)(2,1)} %get-tuple-element.23.after_ref.refs_0_, bf16[12,96,1152]{2,1,0:T(8,128)(2,1)} %get-tuple-element.24.refs_1_, bf16[12,96,1152]{2,1,0:T(8,128)(2,1)} %get-tuple-element.25.refs_2_, ...), custom_call_target="tpu_custom_call", output_to_operand_aliasing={{}: (9, {})} | custom-call | tf_op jit(solution)/shard_map/out/pallas_call | solution.py:274
  278.4 3.2 %out.11 = f32[96,96,1152]{2,1,0:T(8,128)} custom-call(bf16[12,96,1152]{2,1,0:T(8,128)(2,1)} %get-tuple-element.23.after_ref.refs_0_, bf16[12,96,1152]{2,1,0:T(8,128)(2,1)} %get-tuple-element.24.refs_1_, bf16[12,96,1152]{2,1,0:T(8,128)(2,1)} %get-tuple-element.25.refs_2_, ...), custom_call_target="tpu_custom_call", output_to_operand_aliasing={{}: (9, {})} | custom-call | tf_op jit(solution)/shard_map/out/pallas_call | solution.py:274
  (8 shorter events, 0.0 us)
Async XLA Ops:
  121.2 111.7 %collective-permute-start.10 = (bf16[12,48,1152]{2,1,0:T(8,128)(2,1)}, bf16[12,48,1152]{2,1,0:T(8,128)(2,1)}, u32[]{:S(2)}, u32[]{:S(2)}) collective-permute-start(bf16[12,48,1152]{2,1,0:T(8,128)(2,1)} %get-tuple-element.39), channel_id=1, source_target_pairs={{0,6},{1,7},{2,4},{3,5},{4,2},{5,3},{6,0},{7,1},{8,14},{9,15},{10,... | collective-permute-start | bytes 3981320 | tf_op jit(solution)/shard_map/ppermute | solution.py:250
  122.7 111.6 %collective-permute-start.11 = (bf16[12,48,1152]{2,1,0:T(8,128)(2,1)}, bf16[12,48,1152]{2,1,0:T(8,128)(2,1)}, u32[]{:S(2)}, u32[]{:S(2)}) collective-permute-start(bf16[12,48,1152]{2,1,0:T(8,128)(2,1)} %get-tuple-element.40), channel_id=1, source_target_pairs={{0,7},{1,6},{2,5},{3,4},{4,3},{5,2},{6,1},{7,0},{8,15},{9,14},{10,... | collective-permute-start | bytes 3981320 | tf_op jit(solution)/shard_map/ppermute | solution.py:250
  123.9 63.7 %collective-permute-start.4 = (bf16[12,8,1152]{2,1,0:T(8,128)(2,1)}, bf16[12,8,1152]{2,1,0:T(8,128)(2,1)}, u32[]{:S(2)}, u32[]{:S(2)}) collective-permute-start(bf16[12,8,1152]{2,1,0:T(8,128)(2,1)} %get-tuple-element.33), channel_id=1, source_target_pairs={{0,6},{1,7},{2,4},{3,5},{4,2},{5,3},{6,0},{7,1},{8,14},{9,15},{10,... | collective-permute-start | bytes 663560 | tf_op jit(solution)/shard_map/ppermute | solution.py:250
  125.4 104.6 %collective-permute-start.8 = (bf16[12,24,1152]{2,1,0:T(8,128)(2,1)}, bf16[12,24,1152]{2,1,0:T(8,128)(2,1)}, u32[]{:S(2)}, u32[]{:S(2)}) collective-permute-start(bf16[12,24,1152]{2,1,0:T(8,128)(2,1)} %get-tuple-element.37), channel_id=1, source_target_pairs={{0,6},{1,7},{2,4},{3,5},{4,2},{5,3},{6,0},{7,1},{8,14},{9,15},{10,... | collective-permute-start | bytes 1990664 | tf_op jit(solution)/shard_map/ppermute | solution.py:250
  126.8 104.6 %collective-permute-start.9 = (bf16[12,24,1152]{2,1,0:T(8,128)(2,1)}, bf16[12,24,1152]{2,1,0:T(8,128)(2,1)}, u32[]{:S(2)}, u32[]{:S(2)}) collective-permute-start(bf16[12,24,1152]{2,1,0:T(8,128)(2,1)} %get-tuple-element.38), channel_id=1, source_target_pairs={{0,7},{1,6},{2,5},{3,4},{4,3},{5,2},{6,1},{7,0},{8,15},{9,14},{10,... | collective-permute-start | bytes 1990664 | tf_op jit(solution)/shard_map/ppermute | solution.py:250
  187.6 32.7 %collective-permute-start.6 = (bf16[12,8,1152]{2,1,0:T(8,128)(2,1)}, bf16[12,8,1152]{2,1,0:T(8,128)(2,1)}, u32[]{:S(2)}, u32[]{:S(2)}) collective-permute-start(bf16[12,8,1152]{2,1,0:T(8,128)(2,1)} %get-tuple-element.35), channel_id=1, source_target_pairs={{0,6},{1,7},{2,4},{3,5},{4,2},{5,3},{6,0},{7,1},{8,14},{9,15},{10,... | collective-permute-start | bytes 663560 | tf_op jit(solution)/shard_map/ppermute | solution.py:250
  220.3 8.7 %collective-permute-start.7 = (bf16[12,8,1152]{2,1,0:T(8,128)(2,1)}, bf16[12,8,1152]{2,1,0:T(8,128)(2,1)}, u32[]{:S(2)}, u32[]{:S(2)}) collective-permute-start(bf16[12,8,1152]{2,1,0:T(8,128)(2,1)} %get-tuple-element.36), channel_id=1, source_target_pairs={{0,7},{1,6},{2,5},{3,4},{4,3},{5,2},{6,1},{7,0},{8,15},{9,14},{10,... | collective-permute-start | bytes 663560 | tf_op jit(solution)/shard_map/ppermute | solution.py:250
  229.0 41.2 %collective-permute-start.5 = (bf16[12,8,1152]{2,1,0:T(8,128)(2,1)}, bf16[12,8,1152]{2,1,0:T(8,128)(2,1)}, u32[]{:S(2)}, u32[]{:S(2)}) collective-permute-start(bf16[12,8,1152]{2,1,0:T(8,128)(2,1)} %get-tuple-element.34), channel_id=1, source_target_pairs={{0,7},{1,6},{2,5},{3,4},{4,3},{5,2},{6,1},{7,0},{8,15},{9,14},{10,... | collective-permute-start | bytes 663560 | tf_op jit(solution)/shard_map/ppermute | solution.py:250
  229.9 44.8 %collective-permute-start.2 = (bf16[12,8,640]{2,1,0:T(8,128)(2,1)}, bf16[12,8,640]{2,1,0:T(8,128)(2,1)}, u32[]{:S(2)}, u32[]{:S(2)}) collective-permute-start(bf16[12,8,640]{2,1,0:T(8,128)(2,1)} %get-tuple-element.31), channel_id=1, source_target_pairs={{0,6},{1,7},{2,4},{3,5},{4,2},{5,3},{6,0},{7,1},{8,14},{9,15},{10,... | collective-permute-start | bytes 368648 | tf_op jit(solution)/shard_map/ppermute | solution.py:250
  231.4 43.4 %collective-permute-start.3 = (bf16[12,8,640]{2,1,0:T(8,128)(2,1)}, bf16[12,8,640]{2,1,0:T(8,128)(2,1)}, u32[]{:S(2)}, u32[]{:S(2)}) collective-permute-start(bf16[12,8,640]{2,1,0:T(8,128)(2,1)} %get-tuple-element.32), channel_id=1, source_target_pairs={{0,7},{1,6},{2,5},{3,4},{4,3},{5,2},{6,1},{7,0},{8,15},{9,14},{10,... | collective-permute-start | bytes 368648 | tf_op jit(solution)/shard_map/ppermute | solution.py:250
  232.8 45.6 %collective-permute-start = (bf16[12,8,512]{2,1,0:T(8,128)(2,1)}, bf16[12,8,512]{2,1,0:T(8,128)(2,1)}, u32[]{:S(2)}, u32[]{:S(2)}) collective-permute-start(bf16[12,8,512]{2,1,0:T(8,128)(2,1)} %get-tuple-element.29), channel_id=1, source_target_pairs={{0,6},{1,7},{2,4},{3,5},{4,2},{5,3},{6,0},{7,1},{8,14},{9,15},{10,... | collective-permute-start | bytes 294920 | tf_op jit(solution)/shard_map/ppermute | solution.py:250
  234.3 44.2 %collective-permute-start.1 = (bf16[12,8,512]{2,1,0:T(8,128)(2,1)}, bf16[12,8,512]{2,1,0:T(8,128)(2,1)}, u32[]{:S(2)}, u32[]{:S(2)}) collective-permute-start(bf16[12,8,512]{2,1,0:T(8,128)(2,1)} %get-tuple-element.30), channel_id=1, source_target_pairs={{0,7},{1,6},{2,5},{3,4},{4,3},{5,2},{6,1},{7,0},{8,15},{9,14},{10,... | collective-permute-start | bytes 294920 | tf_op jit(solution)/shard_map/ppermute | solution.py:250

commit v9 on v8

--- a/solution.py
+++ b/solution.py
@@ -10,7 +10,7 @@
 
 TILES = ((0, 48, 0, 1152), (48, 24, 0, 1152), (72, 8, 0, 1152), (80, 8, 0, 1152), (88, 8, 0, 640), (88, 8, 640, 512))
 DIAGONAL = (6, 7)
-DIRECT = (2, 4, 3, 5, 1)
+DIRECT = (4, 2, 5, 3, 1)
 F32, BF16 = jnp.float32, jnp.bfloat16
 
 
@@ -33,14 +33,18 @@
     return lax.dot_general(c, eye, (((0,), (0,)), ((), ())), preferred_element_type=F32).astype(BF16)
 
 
-def build_first(n, c_ref, l1_ref, r2_ref, ct_ref):
+def l1_rows(n, j_of, size, ct):
+    tall = dot(pick((8 * size, n), lambda i, j: j_of(i // 8) == j), ct).astype(BF16)
+    wide = dot(tall, pick((n, 8 * n), lambda i, j: j % n == i))
+    keep = one_hot((8 * size, 8 * n), lambda i, j: i % 8 == j // n)
+    return jnp.where(keep, wide, 0.0).astype(BF16)
+
+
+def build_first(n, j_of, size, c_ref, l1_ref, r2_ref, ct_ref):
     c = c_ref[...]
     ct = transposed(c, n)
     ct_ref[...] = ct
-    tall = dot(pick((8 * n, n), lambda i, j: i // 8 == j), ct).astype(BF16)
-    wide = dot(tall, pick((n, 8 * n), lambda i, j: j % n == i))
-    keep = one_hot((8 * n, 8 * n), lambda i, j: i % 8 == j // n)
-    l1_ref[...] = jnp.where(keep, wide, 0.0).astype(BF16)
+    l1_ref[pl.ds(0, 8 * size)] = l1_rows(n, j_of, size, ct)
     tall = dot(pick((512, n), lambda i, j: i % 128 == j), c).astype(BF16)
     wide = dot(tall, pick((n, 4 * n), lambda i, j: j % n == i))
     keep = one_hot((512, 4 * n), lambda i, j: i // 128 == j // n)
@@ -91,7 +95,8 @@
     for g in range(n // 16):
         chunk(g).start()
     fetch(1).start()
-    build_first(n, c_ref, l1_ref, r2_ref, ct_ref)
+    d0, d1 = (flipped(me, k) for k in DIRECT[:2])
+    build_first(n, lambda x: jnp.where(x < nj, x + d0 * nj, x - nj + d1 * nj), 2 * nj, c_ref, l1_ref, r2_ref, ct_ref)
     zero = jnp.zeros((8 * n, 128 - n), BF16)
 
     def remote(k, src, dst):
@@ -137,8 +142,10 @@
             if wait:
                 chunk(2 * pair).wait()
                 chunk(2 * pair + 1).wait()
-            lhs = jnp.concatenate(
-                [l1_ref[pl.ds(pl.multiple_of(flipped(me, k) * 8 * nj, 8 * nj), 8 * nj)] for k in ks], axis=0)
+                lhs = l1_ref[pl.ds(0, len(ks) * 8 * nj)]
+            else:
+                lhs = jnp.concatenate(
+                    [l1_ref[pl.ds(pl.multiple_of(flipped(me, k) * 8 * nj, 8 * nj), 8 * nj)] for k in ks], axis=0)
             for g in range(2):
                 q, t = step_one(slot, 2 * pair + g, lhs)
                 for x, k in enumerate(ks):
@@ -146,14 +153,16 @@
             return carry
 
         lax.fori_loop(0, n // 32, first, 0)
-        for k in ks:
-            step_two_three(k, i)
-        if wait:
-            pl.semaphore_wait(barrier, len(DIRECT))
-        for k in ks:
-            send(k, i)
+        for part in (ks,) if wait else (ks[:2], ks[2:]):
+            for k in part:
+                step_two_three(k, i)
+            if wait:
+                pl.semaphore_wait(barrier, len(DIRECT))
+            for k in part:
+                send(k, i)
 
     some(DIRECT[:2], 0, 0, True)
+    l1_ref[...] = l1_rows(n, lambda x: x, n, ct_ref[...])
     some((*DIRECT[2:], 0, *DIAGONAL), 0, 0, False)
 
     def row(i, carry):

time: 282 us -> 282 us (level)
  no operation moved by 1% of the time
where the time goes in v9:
time: 282 us; the launch traced here: 281 us
  Pallas kernels  168 us (60%)
  waiting for transfers between devices  99 us (35%)
  starting transfers between devices  14.6 us (5%)
    pallas_call x1, Pallas kernels, transform(): pl.pallas_call(functools.partial(exchange_kernel, n, n_dev, rows), in_spe...  121 us
    ppermute x12, waiting for transfers between devices, transform(): lax.ppermute(tiles[x * len(TILES) + t], 'dev', [(i, i ^ k) for i in range...  99 us
    pallas_call x6, Pallas kernels, transform(): pl.pallas_call(functools.partial(tail_kernel, n, n_in, a0, lane, lanes, 4...  43.8 us
    ppermute x12, starting transfers between devices, transform(): lax.ppermute(tiles[x * len(TILES) + t], 'dev', [(i, i ^ k) for i in range...  14.6 us
  transfers between devices with their start and end apart: 12, of which 3 were waited for; matrix products, arithmetic and copies ran while one was open for 0% of the time, Pallas kernels for 15%

profile of v9, /device:TPU:0, one launch (start us, length us, event | category | flops | bytes accessed | tf_op | source)
XLA Modules:
  0.0 281.5 jit_solution(2803176736069762816)
XLA Ops:
  0.0 121.3 %exchange.1 = (bf16[12,96,1152]{2,1,0:T(8,128)(2,1)}, bf16[12,96,1152]{2,1,0:T(8,128)(2,1)}, bf16[12,96,1152]{2,1,0:T(8,128)(2,1)}, bf16[12,96,1152]{2,1,0:T(8,1...) custom-call(bf16[12,96,96,96]{3,2,1,0:T(8,128)(2,1)} %a_hbm.1, ...), custom_call_target="tpu_custom_call" | custom-call | tf_op jit(solution)/shard_map/exchange/pallas_call | solution.py:240
  121.3 1.5 collective-permute-start.10
  122.8 1.1 collective-permute-start.11
  123.9 1.5 collective-permute-start.4
  125.4 1.5 collective-permute-start.8
  126.8 1.0 collective-permute-start.9
  127.8 59.9 %collective-permute-done.4.refs_6_ = bf16[12,8,1152]{2,1,0:T(8,128)(2,1)} collective-permute-done((bf16[12,8,1152]{2,1,0:T(8,128)(2,1)}, bf16[12,8,1152]{2,1,0:T(8,128)(2,1)}, u32[]{:S(2)}, u32[]{:S(2)}) %collective-permute-start.4) | collective-permute-done | bytes 221216 | tf_op jit(solution)/shard_map/ppermute | solution.py:259
  187.7 1.5 collective-permute-start.6
  189.2 31.0 %collective-permute-done.6.refs_6_ = bf16[12,8,1152]{2,1,0:T(8,128)(2,1)} collective-permute-done((bf16[12,8,1152]{2,1,0:T(8,128)(2,1)}, bf16[12,8,1152]{2,1,0:T(8,128)(2,1)}, u32[]{:S(2)}, u32[]{:S(2)}) %collective-permute-start.6) | collective-permute-done | bytes 221216 | tf_op jit(solution)/shard_map/ppermute | solution.py:259
  220.3 0.5 collective-permute-start.7
  220.8 8.1 %collective-permute-done.7.refs_7_ = bf16[12,8,1152]{2,1,0:T(8,128)(2,1)} collective-permute-done((bf16[12,8,1152]{2,1,0:T(8,128)(2,1)}, bf16[12,8,1152]{2,1,0:T(8,128)(2,1)}, u32[]{:S(2)}, u32[]{:S(2)}) %collective-permute-start.7) | collective-permute-done | bytes 221216 | tf_op jit(solution)/shard_map/ppermute | solution.py:259
  228.8 0.8 collective-permute-start.5
  229.6 0.0 collective-permute-done.8.refs_6_
  229.6 1.5 collective-permute-start.2
  231.1 1.5 collective-permute-start.3
  232.7 1.5 collective-permute-start
  234.1 0.8 collective-permute-start.1
  234.9 2.5 last.1.refs_8_
  237.5 17.2 %out.6.refs_9_ = f32[96,96,1152]{2,1,0:T(8,128)} custom-call(bf16[12,96,1152]{2,1,0:T(8,128)(2,1)} %get-tuple-element.23.after_ref.refs_0_, bf16[12,96,1152]{2,1,0:T(8,128)(2,1)} %get-tuple-element.24.refs_1_, bf16[12,96,1152]{2,1,0:T(8,128)(2,1)} %get-tuple-element.25.refs_2_, bf16[12,96,1152]{2,1,0:T(8,128)(2,1)} %get-tuple-element.26.refs_3_, ...), custom_call_target="tpu_custom_call" | custom-call | tf_op jit(solution)/shard_map/out/pallas_call | solution.py:283
  254.7 10.5 %out.7.refs_9_ = f32[96,96,1152]{2,1,0:T(8,128)} custom-call(bf16[12,96,1152]{2,1,0:T(8,128)(2,1)} %get-tuple-element.23.after_ref.refs_0_, bf16[12,96,1152]{2,1,0:T(8,128)(2,1)} %get-tuple-element.24.refs_1_, bf16[12,96,1152]{2,1,0:T(8,128)(2,1)} %get-tuple-element.25.refs_2_, ...), custom_call_target="tpu_custom_call", output_to_operand_aliasing={{}: (9, {})} | custom-call | tf_op jit(solution)/shard_map/out/pallas_call | solution.py:283
  265.2 4.6 %out.8.refs_9_ = f32[96,96,1152]{2,1,0:T(8,128)} custom-call(bf16[12,96,1152]{2,1,0:T(8,128)(2,1)} %get-tuple-element.23.after_ref.refs_0_, bf16[12,96,1152]{2,1,0:T(8,128)(2,1)} %get-tuple-element.24.refs_1_, bf16[12,96,1152]{2,1,0:T(8,128)(2,1)} %get-tuple-element.25.refs_2_, ...), custom_call_target="tpu_custom_call", output_to_operand_aliasing={{}: (9, {})} | custom-call | tf_op jit(solution)/shard_map/out/pallas_call | solution.py:283
  269.8 4.6 %out.9.refs_9_ = f32[96,96,1152]{2,1,0:T(8,128)} custom-call(bf16[12,96,1152]{2,1,0:T(8,128)(2,1)} %get-tuple-element.23.after_ref.refs_0_, bf16[12,96,1152]{2,1,0:T(8,128)(2,1)} %get-tuple-element.24.refs_1_, bf16[12,96,1152]{2,1,0:T(8,128)(2,1)} %get-tuple-element.25.refs_2_, ...), custom_call_target="tpu_custom_call", output_to_operand_aliasing={{}: (9, {})} | custom-call | tf_op jit(solution)/shard_map/out/pallas_call | solution.py:283
  274.5 3.6 %out.10.refs_9_ = f32[96,96,1152]{2,1,0:T(8,128)} custom-call(bf16[12,96,1152]{2,1,0:T(8,128)(2,1)} %get-tuple-element.23.after_ref.refs_0_, bf16[12,96,1152]{2,1,0:T(8,128)(2,1)} %get-tuple-element.24.refs_1_, bf16[12,96,1152]{2,1,0:T(8,128)(2,1)} %get-tuple-element.25.refs_2_, ...), custom_call_target="tpu_custom_call", output_to_operand_aliasing={{}: (9, {})} | custom-call | tf_op jit(solution)/shard_map/out/pallas_call | solution.py:283
  278.1 3.2 %out.11 = f32[96,96,1152]{2,1,0:T(8,128)} custom-call(bf16[12,96,1152]{2,1,0:T(8,128)(2,1)} %get-tuple-element.23.after_ref.refs_0_, bf16[12,96,1152]{2,1,0:T(8,128)(2,1)} %get-tuple-element.24.refs_1_, bf16[12,96,1152]{2,1,0:T(8,128)(2,1)} %get-tuple-element.25.refs_2_, ...), custom_call_target="tpu_custom_call", output_to_operand_aliasing={{}: (9, {})} | custom-call | tf_op jit(solution)/shard_map/out/pallas_call | solution.py:283
  (8 shorter events, 0.0 us)
Async XLA Ops:
  121.3 111.3 %collective-permute-start.10 = (bf16[12,48,1152]{2,1,0:T(8,128)(2,1)}, bf16[12,48,1152]{2,1,0:T(8,128)(2,1)}, u32[]{:S(2)}, u32[]{:S(2)}) collective-permute-start(bf16[12,48,1152]{2,1,0:T(8,128)(2,1)} %get-tuple-element.39), channel_id=1, source_target_pairs={{0,6},{1,7},{2,4},{3,5},{4,2},{5,3},{6,0},{7,1},{8,14},{9,15},{10,... | collective-permute-start | bytes 3981320 | tf_op jit(solution)/shard_map/ppermute | solution.py:259
  122.8 111.3 %collective-permute-start.11 = (bf16[12,48,1152]{2,1,0:T(8,128)(2,1)}, bf16[12,48,1152]{2,1,0:T(8,128)(2,1)}, u32[]{:S(2)}, u32[]{:S(2)}) collective-permute-start(bf16[12,48,1152]{2,1,0:T(8,128)(2,1)} %get-tuple-element.40), channel_id=1, source_target_pairs={{0,7},{1,6},{2,5},{3,4},{4,3},{5,2},{6,1},{7,0},{8,15},{9,14},{10,... | collective-permute-start | bytes 3981320 | tf_op jit(solution)/shard_map/ppermute | solution.py:259
  123.9 63.8 %collective-permute-start.4 = (bf16[12,8,1152]{2,1,0:T(8,128)(2,1)}, bf16[12,8,1152]{2,1,0:T(8,128)(2,1)}, u32[]{:S(2)}, u32[]{:S(2)}) collective-permute-start(bf16[12,8,1152]{2,1,0:T(8,128)(2,1)} %get-tuple-element.33), channel_id=1, source_target_pairs={{0,6},{1,7},{2,4},{3,5},{4,2},{5,3},{6,0},{7,1},{8,14},{9,15},{10,... | collective-permute-start | bytes 663560 | tf_op jit(solution)/shard_map/ppermute | solution.py:259
  125.4 104.2 %collective-permute-start.8 = (bf16[12,24,1152]{2,1,0:T(8,128)(2,1)}, bf16[12,24,1152]{2,1,0:T(8,128)(2,1)}, u32[]{:S(2)}, u32[]{:S(2)}) collective-permute-start(bf16[12,24,1152]{2,1,0:T(8,128)(2,1)} %get-tuple-element.37), channel_id=1, source_target_pairs={{0,6},{1,7},{2,4},{3,5},{4,2},{5,3},{6,0},{7,1},{8,14},{9,15},{10,... | collective-permute-start | bytes 1990664 | tf_op jit(solution)/shard_map/ppermute | solution.py:259
  126.8 104.3 %collective-permute-start.9 = (bf16[12,24,1152]{2,1,0:T(8,128)(2,1)}, bf16[12,24,1152]{2,1,0:T(8,128)(2,1)}, u32[]{:S(2)}, u32[]{:S(2)}) collective-permute-start(bf16[12,24,1152]{2,1,0:T(8,128)(2,1)} %get-tuple-element.38), channel_id=1, source_target_pairs={{0,7},{1,6},{2,5},{3,4},{4,3},{5,2},{6,1},{7,0},{8,15},{9,14},{10,... | collective-permute-start | bytes 1990664 | tf_op jit(solution)/shard_map/ppermute | solution.py:259
  187.7 32.5 %collective-permute-start.6 = (bf16[12,8,1152]{2,1,0:T(8,128)(2,1)}, bf16[12,8,1152]{2,1,0:T(8,128)(2,1)}, u32[]{:S(2)}, u32[]{:S(2)}) collective-permute-start(bf16[12,8,1152]{2,1,0:T(8,128)(2,1)} %get-tuple-element.35), channel_id=1, source_target_pairs={{0,6},{1,7},{2,4},{3,5},{4,2},{5,3},{6,0},{7,1},{8,14},{9,15},{10,... | collective-permute-start | bytes 663560 | tf_op jit(solution)/shard_map/ppermute | solution.py:259
  220.3 8.6 %collective-permute-start.7 = (bf16[12,8,1152]{2,1,0:T(8,128)(2,1)}, bf16[12,8,1152]{2,1,0:T(8,128)(2,1)}, u32[]{:S(2)}, u32[]{:S(2)}) collective-permute-start(bf16[12,8,1152]{2,1,0:T(8,128)(2,1)} %get-tuple-element.36), channel_id=1, source_target_pairs={{0,7},{1,6},{2,5},{3,4},{4,3},{5,2},{6,1},{7,0},{8,15},{9,14},{10,... | collective-permute-start | bytes 663560 | tf_op jit(solution)/shard_map/ppermute | solution.py:259
  228.8 41.0 %collective-permute-start.5 = (bf16[12,8,1152]{2,1,0:T(8,128)(2,1)}, bf16[12,8,1152]{2,1,0:T(8,128)(2,1)}, u32[]{:S(2)}, u32[]{:S(2)}) collective-permute-start(bf16[12,8,1152]{2,1,0:T(8,128)(2,1)} %get-tuple-element.34), channel_id=1, source_target_pairs={{0,7},{1,6},{2,5},{3,4},{4,3},{5,2},{6,1},{7,0},{8,15},{9,14},{10,... | collective-permute-start | bytes 663560 | tf_op jit(solution)/shard_map/ppermute | solution.py:259
  229.6 44.8 %collective-permute-start.2 = (bf16[12,8,640]{2,1,0:T(8,128)(2,1)}, bf16[12,8,640]{2,1,0:T(8,128)(2,1)}, u32[]{:S(2)}, u32[]{:S(2)}) collective-permute-start(bf16[12,8,640]{2,1,0:T(8,128)(2,1)} %get-tuple-element.31), channel_id=1, source_target_pairs={{0,6},{1,7},{2,4},{3,5},{4,2},{5,3},{6,0},{7,1},{8,14},{9,15},{10,... | collective-permute-start | bytes 368648 | tf_op jit(solution)/shard_map/ppermute | solution.py:259
  231.1 43.3 %collective-permute-start.3 = (bf16[12,8,640]{2,1,0:T(8,128)(2,1)}, bf16[12,8,640]{2,1,0:T(8,128)(2,1)}, u32[]{:S(2)}, u32[]{:S(2)}) collective-permute-start(bf16[12,8,640]{2,1,0:T(8,128)(2,1)} %get-tuple-element.32), channel_id=1, source_target_pairs={{0,7},{1,6},{2,5},{3,4},{4,3},{5,2},{6,1},{7,0},{8,15},{9,14},{10,... | collective-permute-start | bytes 368648 | tf_op jit(solution)/shard_map/ppermute | solution.py:259
  232.7 45.4 %collective-permute-start = (bf16[12,8,512]{2,1,0:T(8,128)(2,1)}, bf16[12,8,512]{2,1,0:T(8,128)(2,1)}, u32[]{:S(2)}, u32[]{:S(2)}) collective-permute-start(bf16[12,8,512]{2,1,0:T(8,128)(2,1)} %get-tuple-element.29), channel_id=1, source_target_pairs={{0,6},{1,7},{2,4},{3,5},{4,2},{5,3},{6,0},{7,1},{8,14},{9,15},{10,... | collective-permute-start | bytes 294920 | tf_op jit(solution)/shard_map/ppermute | solution.py:259
  234.1 44.0 %collective-permute-start.1 = (bf16[12,8,512]{2,1,0:T(8,128)(2,1)}, bf16[12,8,512]{2,1,0:T(8,128)(2,1)}, u32[]{:S(2)}, u32[]{:S(2)}) collective-permute-start(bf16[12,8,512]{2,1,0:T(8,128)(2,1)} %get-tuple-element.30), channel_id=1, source_target_pairs={{0,7},{1,6},{2,5},{3,4},{4,3},{5,2},{6,1},{7,0},{8,15},{9,14},{10,... | collective-permute-start | bytes 294920 | tf_op jit(solution)/shard_map/ppermute | solution.py:259

commit v10 on v9

--- a/solution.py
+++ b/solution.py
@@ -10,7 +10,7 @@
 
 TILES = ((0, 48, 0, 1152), (48, 24, 0, 1152), (72, 8, 0, 1152), (80, 8, 0, 1152), (88, 8, 0, 640), (88, 8, 640, 512))
 DIAGONAL = (6, 7)
-DIRECT = (4, 2, 5, 3, 1)
+DIRECT = (2, 4, 3, 5, 1)
 F32, BF16 = jnp.float32, jnp.bfloat16
 
 
@@ -281,7 +281,7 @@
                 specs.append(hbm)
             alone = size == 8
             out = pl.pallas_call(
-                functools.partial(tail_kernel, n, n_in, a0, lane, lanes, 4) if alone
+                functools.partial(tail_kernel, n, n_in, a0, lane, lanes, 6) if alone
                 else functools.partial(out_kernel, n_in, lanes),
                 grid=(size // 8,),
                 in_specs=specs,
@@ -290,7 +290,7 @@
                     lambda i, at=(a0, lane): (0, pl.multiple_of(at[0] + 8 * i, 8), at[1])),
                 out_shape=jax.ShapeDtypeStruct((n, n, wide), F32),
                 input_output_aliases={} if t_i == 0 else {len(ins) - 1: 0},
-                scratch_shapes=[pltpu.VMEM((n, 8, lanes), F32), pltpu.SemaphoreType.DMA((4,))] * alone,
+                scratch_shapes=[pltpu.VMEM((n, 8, lanes), F32), pltpu.SemaphoreType.DMA((6,))] * alone,
                 compiler_params=pltpu.CompilerParams(vmem_limit_bytes=67043328),
                 name='out',
             )(*ins)

time: 282 us -> 282 us (level)
  no operation moved by 1% of the time
where the time goes in v10:
time: 282 us; the launch traced here: 281 us
  Pallas kernels  167 us (59%)
  waiting for transfers between devices  99.1 us (35%)
  starting transfers between devices  14.6 us (5%)
    pallas_call x1, Pallas kernels, transform(): pl.pallas_call(functools.partial(exchange_kernel, n, n_dev, rows), in_spe...  121 us
    ppermute x12, waiting for transfers between devices, transform(): lax.ppermute(tiles[x * len(TILES) + t], 'dev', [(i, i ^ k) for i in range...  99.1 us
    pallas_call x6, Pallas kernels, transform(): pl.pallas_call(functools.partial(tail_kernel, n, n_in, a0, lane, lanes, 6...  43.6 us
    ppermute x12, starting transfers between devices, transform(): lax.ppermute(tiles[x * len(TILES) + t], 'dev', [(i, i ^ k) for i in range...  14.6 us
  transfers between devices with their start and end apart: 12, of which 3 were waited for; matrix products, arithmetic and copies ran while one was open for 0% of the time, Pallas kernels for 15%

profile of v10, /device:TPU:0, one launch (start us, length us, event | category | flops | bytes accessed | tf_op | source)
XLA Modules:
  0.0 281.3 jit_solution(5413222933333502875)
XLA Ops:
  0.0 121.3 %exchange.1 = (bf16[12,96,1152]{2,1,0:T(8,128)(2,1)}, bf16[12,96,1152]{2,1,0:T(8,128)(2,1)}, bf16[12,96,1152]{2,1,0:T(8,128)(2,1)}, bf16[12,96,1152]{2,1,0:T(8,1...) custom-call(bf16[12,96,96,96]{3,2,1,0:T(8,128)(2,1)} %a_hbm.1, ...), custom_call_target="tpu_custom_call" | custom-call | tf_op jit(solution)/shard_map/exchange/pallas_call | solution.py:240
  121.3 1.5 collective-permute-start.10
  122.8 1.1 collective-permute-start.11
  123.9 1.5 collective-permute-start.4
  125.4 1.5 collective-permute-start.8
  126.8 1.0 collective-permute-start.9
  127.8 59.9 %collective-permute-done.4.refs_6_ = bf16[12,8,1152]{2,1,0:T(8,128)(2,1)} collective-permute-done((bf16[12,8,1152]{2,1,0:T(8,128)(2,1)}, bf16[12,8,1152]{2,1,0:T(8,128)(2,1)}, u32[]{:S(2)}, u32[]{:S(2)}) %collective-permute-start.4) | collective-permute-done | bytes 221216 | tf_op jit(solution)/shard_map/ppermute | solution.py:259
  187.8 1.4 collective-permute-start.6
  189.2 31.1 %collective-permute-done.6.refs_6_ = bf16[12,8,1152]{2,1,0:T(8,128)(2,1)} collective-permute-done((bf16[12,8,1152]{2,1,0:T(8,128)(2,1)}, bf16[12,8,1152]{2,1,0:T(8,128)(2,1)}, u32[]{:S(2)}, u32[]{:S(2)}) %collective-permute-start.6) | collective-permute-done | bytes 221216 | tf_op jit(solution)/shard_map/ppermute | solution.py:259
  220.3 0.5 collective-permute-start.7
  220.8 8.0 %collective-permute-done.7.refs_7_ = bf16[12,8,1152]{2,1,0:T(8,128)(2,1)} collective-permute-done((bf16[12,8,1152]{2,1,0:T(8,128)(2,1)}, bf16[12,8,1152]{2,1,0:T(8,128)(2,1)}, u32[]{:S(2)}, u32[]{:S(2)}) %collective-permute-start.7) | collective-permute-done | bytes 221216 | tf_op jit(solution)/shard_map/ppermute | solution.py:259
  228.8 0.8 collective-permute-start.5
  229.7 0.0 collective-permute-done.8.refs_6_
  229.7 1.4 collective-permute-start.2
  231.1 1.6 collective-permute-start.3
  232.7 1.4 collective-permute-start
  234.1 0.8 collective-permute-start.1
  235.0 2.5 last.1.refs_8_
  237.5 17.2 %out.6.refs_9_ = f32[96,96,1152]{2,1,0:T(8,128)} custom-call(bf16[12,96,1152]{2,1,0:T(8,128)(2,1)} %get-tuple-element.23.after_ref.refs_0_, bf16[12,96,1152]{2,1,0:T(8,128)(2,1)} %get-tuple-element.24.refs_1_, bf16[12,96,1152]{2,1,0:T(8,128)(2,1)} %get-tuple-element.25.refs_2_, bf16[12,96,1152]{2,1,0:T(8,128)(2,1)} %get-tuple-element.26.refs_3_, ...), custom_call_target="tpu_custom_call" | custom-call | tf_op jit(solution)/shard_map/out/pallas_call | solution.py:283
  254.7 10.5 %out.7.refs_9_ = f32[96,96,1152]{2,1,0:T(8,128)} custom-call(bf16[12,96,1152]{2,1,0:T(8,128)(2,1)} %get-tuple-element.23.after_ref.refs_0_, bf16[12,96,1152]{2,1,0:T(8,128)(2,1)} %get-tuple-element.24.refs_1_, bf16[12,96,1152]{2,1,0:T(8,128)(2,1)} %get-tuple-element.25.refs_2_, ...), custom_call_target="tpu_custom_call", output_to_operand_aliasing={{}: (9, {})} | custom-call | tf_op jit(solution)/shard_map/out/pallas_call | solution.py:283
  265.2 4.5 %out.8.refs_9_ = f32[96,96,1152]{2,1,0:T(8,128)} custom-call(bf16[12,96,1152]{2,1,0:T(8,128)(2,1)} %get-tuple-element.23.after_ref.refs_0_, bf16[12,96,1152]{2,1,0:T(8,128)(2,1)} %get-tuple-element.24.refs_1_, bf16[12,96,1152]{2,1,0:T(8,128)(2,1)} %get-tuple-element.25.refs_2_, ...), custom_call_target="tpu_custom_call", output_to_operand_aliasing={{}: (9, {})} | custom-call | tf_op jit(solution)/shard_map/out/pallas_call | solution.py:283
  269.8 4.5 %out.9.refs_9_ = f32[96,96,1152]{2,1,0:T(8,128)} custom-call(bf16[12,96,1152]{2,1,0:T(8,128)(2,1)} %get-tuple-element.23.after_ref.refs_0_, bf16[12,96,1152]{2,1,0:T(8,128)(2,1)} %get-tuple-element.24.refs_1_, bf16[12,96,1152]{2,1,0:T(8,128)(2,1)} %get-tuple-element.25.refs_2_, ...), custom_call_target="tpu_custom_call", output_to_operand_aliasing={{}: (9, {})} | custom-call | tf_op jit(solution)/shard_map/out/pallas_call | solution.py:283
  274.3 3.6 %out.10.refs_9_ = f32[96,96,1152]{2,1,0:T(8,128)} custom-call(bf16[12,96,1152]{2,1,0:T(8,128)(2,1)} %get-tuple-element.23.after_ref.refs_0_, bf16[12,96,1152]{2,1,0:T(8,128)(2,1)} %get-tuple-element.24.refs_1_, bf16[12,96,1152]{2,1,0:T(8,128)(2,1)} %get-tuple-element.25.refs_2_, ...), custom_call_target="tpu_custom_call", output_to_operand_aliasing={{}: (9, {})} | custom-call | tf_op jit(solution)/shard_map/out/pallas_call | solution.py:283
  278.0 3.2 %out.11 = f32[96,96,1152]{2,1,0:T(8,128)} custom-call(bf16[12,96,1152]{2,1,0:T(8,128)(2,1)} %get-tuple-element.23.after_ref.refs_0_, bf16[12,96,1152]{2,1,0:T(8,128)(2,1)} %get-tuple-element.24.refs_1_, bf16[12,96,1152]{2,1,0:T(8,128)(2,1)} %get-tuple-element.25.refs_2_, ...), custom_call_target="tpu_custom_call", output_to_operand_aliasing={{}: (9, {})} | custom-call | tf_op jit(solution)/shard_map/out/pallas_call | solution.py:283
  (8 shorter events, 0.0 us)
Async XLA Ops:
  121.3 111.3 %collective-permute-start.10 = (bf16[12,48,1152]{2,1,0:T(8,128)(2,1)}, bf16[12,48,1152]{2,1,0:T(8,128)(2,1)}, u32[]{:S(2)}, u32[]{:S(2)}) collective-permute-start(bf16[12,48,1152]{2,1,0:T(8,128)(2,1)} %get-tuple-element.39), channel_id=1, source_target_pairs={{0,6},{1,7},{2,4},{3,5},{4,2},{5,3},{6,0},{7,1},{8,14},{9,15},{10,... | collective-permute-start | bytes 3981320 | tf_op jit(solution)/shard_map/ppermute | solution.py:259
  122.8 111.3 %collective-permute-start.11 = (bf16[12,48,1152]{2,1,0:T(8,128)(2,1)}, bf16[12,48,1152]{2,1,0:T(8,128)(2,1)}, u32[]{:S(2)}, u32[]{:S(2)}) collective-permute-start(bf16[12,48,1152]{2,1,0:T(8,128)(2,1)} %get-tuple-element.40), channel_id=1, source_target_pairs={{0,7},{1,6},{2,5},{3,4},{4,3},{5,2},{6,1},{7,0},{8,15},{9,14},{10,... | collective-permute-start | bytes 3981320 | tf_op jit(solution)/shard_map/ppermute | solution.py:259
  123.9 63.9 %collective-permute-start.4 = (bf16[12,8,1152]{2,1,0:T(8,128)(2,1)}, bf16[12,8,1152]{2,1,0:T(8,128)(2,1)}, u32[]{:S(2)}, u32[]{:S(2)}) collective-permute-start(bf16[12,8,1152]{2,1,0:T(8,128)(2,1)} %get-tuple-element.33), channel_id=1, source_target_pairs={{0,6},{1,7},{2,4},{3,5},{4,2},{5,3},{6,0},{7,1},{8,14},{9,15},{10,... | collective-permute-start | bytes 663560 | tf_op jit(solution)/shard_map/ppermute | solution.py:259
  125.4 104.3 %collective-permute-start.8 = (bf16[12,24,1152]{2,1,0:T(8,128)(2,1)}, bf16[12,24,1152]{2,1,0:T(8,128)(2,1)}, u32[]{:S(2)}, u32[]{:S(2)}) collective-permute-start(bf16[12,24,1152]{2,1,0:T(8,128)(2,1)} %get-tuple-element.37), channel_id=1, source_target_pairs={{0,6},{1,7},{2,4},{3,5},{4,2},{5,3},{6,0},{7,1},{8,14},{9,15},{10,... | collective-permute-start | bytes 1990664 | tf_op jit(solution)/shard_map/ppermute | solution.py:259
  126.8 104.2 %collective-permute-start.9 = (bf16[12,24,1152]{2,1,0:T(8,128)(2,1)}, bf16[12,24,1152]{2,1,0:T(8,128)(2,1)}, u32[]{:S(2)}, u32[]{:S(2)}) collective-permute-start(bf16[12,24,1152]{2,1,0:T(8,128)(2,1)} %get-tuple-element.38), channel_id=1, source_target_pairs={{0,7},{1,6},{2,5},{3,4},{4,3},{5,2},{6,1},{7,0},{8,15},{9,14},{10,... | collective-permute-start | bytes 1990664 | tf_op jit(solution)/shard_map/ppermute | solution.py:259
  187.8 32.5 %collective-permute-start.6 = (bf16[12,8,1152]{2,1,0:T(8,128)(2,1)}, bf16[12,8,1152]{2,1,0:T(8,128)(2,1)}, u32[]{:S(2)}, u32[]{:S(2)}) collective-permute-start(bf16[12,8,1152]{2,1,0:T(8,128)(2,1)} %get-tuple-element.35), channel_id=1, source_target_pairs={{0,6},{1,7},{2,4},{3,5},{4,2},{5,3},{6,0},{7,1},{8,14},{9,15},{10,... | collective-permute-start | bytes 663560 | tf_op jit(solution)/shard_map/ppermute | solution.py:259
  220.3 8.6 %collective-permute-start.7 = (bf16[12,8,1152]{2,1,0:T(8,128)(2,1)}, bf16[12,8,1152]{2,1,0:T(8,128)(2,1)}, u32[]{:S(2)}, u32[]{:S(2)}) collective-permute-start(bf16[12,8,1152]{2,1,0:T(8,128)(2,1)} %get-tuple-element.36), channel_id=1, source_target_pairs={{0,7},{1,6},{2,5},{3,4},{4,3},{5,2},{6,1},{7,0},{8,15},{9,14},{10,... | collective-permute-start | bytes 663560 | tf_op jit(solution)/shard_map/ppermute | solution.py:259
  228.8 40.9 %collective-permute-start.5 = (bf16[12,8,1152]{2,1,0:T(8,128)(2,1)}, bf16[12,8,1152]{2,1,0:T(8,128)(2,1)}, u32[]{:S(2)}, u32[]{:S(2)}) collective-permute-start(bf16[12,8,1152]{2,1,0:T(8,128)(2,1)} %get-tuple-element.34), channel_id=1, source_target_pairs={{0,7},{1,6},{2,5},{3,4},{4,3},{5,2},{6,1},{7,0},{8,15},{9,14},{10,... | collective-permute-start | bytes 663560 | tf_op jit(solution)/shard_map/ppermute | solution.py:259
  229.7 44.7 %collective-permute-start.2 = (bf16[12,8,640]{2,1,0:T(8,128)(2,1)}, bf16[12,8,640]{2,1,0:T(8,128)(2,1)}, u32[]{:S(2)}, u32[]{:S(2)}) collective-permute-start(bf16[12,8,640]{2,1,0:T(8,128)(2,1)} %get-tuple-element.31), channel_id=1, source_target_pairs={{0,6},{1,7},{2,4},{3,5},{4,2},{5,3},{6,0},{7,1},{8,14},{9,15},{10,... | collective-permute-start | bytes 368648 | tf_op jit(solution)/shard_map/ppermute | solution.py:259
  231.1 43.3 %collective-permute-start.3 = (bf16[12,8,640]{2,1,0:T(8,128)(2,1)}, bf16[12,8,640]{2,1,0:T(8,128)(2,1)}, u32[]{:S(2)}, u32[]{:S(2)}) collective-permute-start(bf16[12,8,640]{2,1,0:T(8,128)(2,1)} %get-tuple-element.32), channel_id=1, source_target_pairs={{0,7},{1,6},{2,5},{3,4},{4,3},{5,2},{6,1},{7,0},{8,15},{9,14},{10,... | collective-permute-start | bytes 368648 | tf_op jit(solution)/shard_map/ppermute | solution.py:259
  232.7 45.3 %collective-permute-start = (bf16[12,8,512]{2,1,0:T(8,128)(2,1)}, bf16[12,8,512]{2,1,0:T(8,128)(2,1)}, u32[]{:S(2)}, u32[]{:S(2)}) collective-permute-start(bf16[12,8,512]{2,1,0:T(8,128)(2,1)} %get-tuple-element.29), channel_id=1, source_target_pairs={{0,6},{1,7},{2,4},{3,5},{4,2},{5,3},{6,0},{7,1},{8,14},{9,15},{10,... | collective-permute-start | bytes 294920 | tf_op jit(solution)/shard_map/ppermute | solution.py:259
  234.1 43.8 %collective-permute-start.1 = (bf16[12,8,512]{2,1,0:T(8,128)(2,1)}, bf16[12,8,512]{2,1,0:T(8,128)(2,1)}, u32[]{:S(2)}, u32[]{:S(2)}) collective-permute-start(bf16[12,8,512]{2,1,0:T(8,128)(2,1)} %get-tuple-element.30), channel_id=1, source_target_pairs={{0,7},{1,6},{2,5},{3,4},{4,3},{5,2},{6,1},{7,0},{8,15},{9,14},{10,... | collective-permute-start | bytes 294920 | tf_op jit(solution)/shard_map/ppermute | solution.py:259
